TPU v7x, 8 devices: a whole 2x2x1 slice. The times are simulated.
8 devices in a mesh: replica: 1 (over z), model: 8 (over y, x, core).
Axes of the slice: x: 2, y: 2, z: 1, core: 2. Of those that a mesh axis runs over, the one named last changes fastest.
Arguments:
- x: bfloat16 [128, 8192], P('replica')
- cache_len: int32 [128], P('replica')
- w_query: bfloat16 [2, 8192, 8192], P(None, None, 'model')
- w_key: bfloat16 [2, 8192, 128], replicated
- w_value: bfloat16 [2, 8192, 128], replicated
- w_out: bfloat16 [2, 8192, 8192], P(None, 'model')
- k_cache: bfloat16 [2, 128, 2048, 128], P(None, ('replica', 'model'))
- v_cache: bfloat16 [2, 128, 2048, 128], P(None, ('replica', 'model'))
Outputs:
- output 1: bfloat16 [128, 8192], P('replica')
- output 2: bfloat16 [2, 128, 2048, 128], P(None, ('replica', 'model'))
- output 3: bfloat16 [2, 128, 2048, 128], P(None, ('replica', 'model'))
All inputs are finite; a program needn't handle non-finite values.
Results may differ from a plain program's by a relative error of at most 0.00536.
Values are sent between devices in bfloat16 or wider.
A program may use at most 1 GiB of HBM per device.

v0:
```python
import jax
import jax.numpy as jnp
from jax import lax
from jax.sharding import PartitionSpec as P, NamedSharding


def write_token(cache, new_rows, cache_len):
    positions = lax.broadcasted_iota(jnp.int32, (1, cache.shape[1], 1), 1)
    return jnp.where(positions == cache_len[:, None, None], new_rows[:, None, :], cache)


def attend_rows(query, k_layer, v_layer, cache_len):
    seq_len = k_layer.shape[1]
    head_dim = k_layer.shape[2]
    scores = jnp.einsum("bhd,bsd->bhs", query, k_layer, preferred_element_type=jnp.float32) * (head_dim ** -0.5)
    positions = lax.broadcasted_iota(jnp.int32, (1, 1, seq_len), 2)
    scores = jnp.where(positions <= cache_len[:, None, None], scores, -jnp.inf)
    weights = jax.nn.softmax(scores, axis=-1).astype(jnp.bfloat16)
    context = jnp.einsum("bhs,bsd->bhd", weights, v_layer, preferred_element_type=jnp.float32)
    return context.astype(jnp.bfloat16)


def solution(mesh):
    groups = mesh.shape["model"]
    row_axes = ("replica", "model")
    cache_spec = P(None, row_axes, None, None)

    def device_step(x, cache_len, w_query, w_key, w_value, w_out, k_cache, v_cache):
        rows = x.shape[0]
        local_rows = rows // groups
        head_dim = k_cache.shape[-1]
        local_heads = w_query.shape[-1] // head_dim
        first_row = lax.axis_index("model") * local_rows
        my_len = lax.dynamic_slice_in_dim(cache_len, first_row, local_rows)
        hidden = x
        k_layers = []
        v_layers = []
        for layer in range(w_query.shape[0]):
            my_rows = lax.dynamic_slice_in_dim(hidden, first_row, local_rows)
            query = jnp.dot(hidden, w_query[layer], preferred_element_type=jnp.float32).astype(jnp.bfloat16)
            query = query.reshape(rows, local_heads, head_dim)
            k_new = jnp.dot(my_rows, w_key[layer], preferred_element_type=jnp.float32).astype(jnp.bfloat16)
            v_new = jnp.dot(my_rows, w_value[layer], preferred_element_type=jnp.float32).astype(jnp.bfloat16)
            k_layer = write_token(k_cache[layer], k_new, my_len)
            v_layer = write_token(v_cache[layer], v_new, my_len)
            query = lax.all_to_all(query, "model", 0, 1, tiled=True)
            context = attend_rows(query, k_layer, v_layer, my_len)
            context = lax.all_to_all(context, "model", 1, 0, tiled=True)
            part_sum = jnp.dot(context.reshape(rows, local_heads * head_dim), w_out[layer], preferred_element_type=jnp.float32)
            total = lax.psum(part_sum, "model")
            hidden = (hidden.astype(jnp.float32) + total).astype(jnp.bfloat16)
            k_layers.append(k_layer)
            v_layers.append(v_layer)
        return hidden, jnp.stack(k_layers), jnp.stack(v_layers)

    return jax.shard_map(
        device_step,
        mesh=mesh,
        in_specs=(P("replica", None), P("replica"), P(None, None, "model"), P(), P(), P(None, "model", None), cache_spec, cache_spec),
        out_specs=(P("replica", None), cache_spec, cache_spec),
        check_vma=False,
    )
```

profile of v0, /device:TPU:0, one launch (start us, length us, event | category | flops | bytes accessed | tf_op | source)
XLA Modules:
  0.0 302.6 jit_solution(10935121952445660147)
XLA Ops:
  7.2 8.7 %fusion.63 = bf16[16,8,8,128]{3,1,2,0:T(8,128)(2,1)S(1)} fusion(bf16[128,8192]{1,0:T(8,128)(2,1)} %param.8, bf16[2,8192,1024]{2,1,0:T(8,128)(2,1)} %param.10), kind=kOutput, calls=%fused_computation.75 | convolution fusion | flops 2147614720 | bytes 19136512 | tf_op jit(solution)/shard_map/dot_general | solution.py:40
  15.9 0.8 copy.23
  16.7 4.3 %all-to-all-start = ((bf16[128,8,128]{2,1,0:T(8,128)(2,1)}), bf16[128,8,128]{2,1,0:T(8,128)(2,1)S(1)}, u32[]{:S(2)}, u32[]{:S(2)}) async-start(bf16[128,8,128]{2,1,0:T(8,128)(2,1)} %bitcast.25), calls=%async_computation | async-start | bytes 524288 | tf_op jit(solution)/shard_map/all_to_all | solution.py:46
  21.1 2.1 fusion.66
  23.2 0.1 iota_compare_fusion.1
  23.3 2.1 fusion.69
  25.4 2.3 all-to-all-done
  27.7 12.5 %fusion.17 = f32[16,64,2048]{2,1,0:T(8,128)} fusion(pred[16,2048]{1,0:T(8,128)(4,1)S(1)} %get-tuple-element.10, bf16[2,16,2048,128]{3,2,1,0:T(8,128)(2,1)} %param.14, bf16[16,128]{1,0:T(8,128)(2,1)S(1)} %fusion.66, bf16[8,16,8,128]{3,2,1,0:T(8,128)(2,1)S(1)} %bitcast.96), kind=kOutput, calls=%fused_computation.23 | convolution fusion | flops 541065216 | bytes 17076224 | tf_op jit(solution)/shard_map/bhd,bsd->bhs/dot_general | solution.py:15
  40.2 12.0 %fusion.98 = (f32[16,64]{1,0:T(8,128)S(1)}, f32[16,64,2048]{2,1,0:T(8,128)}) fusion(f32[16,64,2048]{2,1,0:T(8,128)} %fusion.17, pred[16,2048]{1,0:T(8,128)(4,1)S(1)} %get-tuple-element.9), kind=kOutput, calls=%fused_computation.102 | output fusion | flops 12584959 | bytes 16814080 | tf_op jit(solution)/shard_map/sub | solution.py:18
  52.3 9.4 %fusion.52 = bf16[16,64,128]{2,1,0:T(8,128)(2,1)S(1)} fusion(pred[16,2048]{1,0:T(8,128)(4,1)S(1)} %get-tuple-element.10, bf16[2,16,2048,128]{3,2,1,0:T(8,128)(2,1)S(1)} %bitcast.91, bf16[16,128]{1,0:T(8,128)(2,1)S(1)} %fusion.69, f32[16,64,2048]{2,1,0:T(8,128)} %get-tuple-element.12, f32[16,64]{1,0:T(8,128)S(1)} %get-tuple-element.11), kind=kOutput, calls=%fused_computation.70 | convolution fusion | flops 545390592 | bytes 17084416 | tf_op jit(solution)/shard_map/bhs,bsd->bhd/dot_general | solution.py:19
  61.7 0.2 copy.18
  61.9 8.1 %all_to_all.66 = bf16[16,64,128]{2,0,1:T(8,128)(2,1)S(1)} all-to-all(bf16[16,64,128]{2,0,1:T(8,128)(2,1)S(1)} %copy.18), channel_id=1, replica_groups=mesh['replica'=1,'model'=8] {'model'}, dimensions={1} | all-to-all | bytes 524288 | tf_op jit(solution)/shard_map/all_to_all | solution.py:48
  70.0 10.1 %fusion.6 = f32[128,8192]{1,0:T(8,128)} fusion(bf16[2,1024,8192]{2,1,0:T(8,128)(2,1)} %param.13, bf16[16,8,8,128]{3,2,1,0:T(8,128)(2,1)S(1)} %bitcast.98), kind=kOutput, calls=%fused_computation.8 | convolution fusion | flops 2147483648 | bytes 21233664 | tf_op jit(solution)/shard_map/dot_general | solution.py:49
  80.2 68.5 %all-reduce.3.cloned.1.call-done = f32[128,8192]{1,0:T(8,128)} async-done(((f32[128,8192]{1,0:T(8,128)}), f32[128,8192]{1,0:T(8,128)}) %all-reduce.3.cloned.1.call-update) | async-done | bytes 4194320 | tf_op jit(solution)/shard_map/psum | solution.py:50
  148.7 3.4 %add_convert_fusion.1 = bf16[128,8192]{1,0:T(8,128)(2,1)S(1)} fusion(f32[128,8192]{1,0:T(8,128)} %all-reduce.3.cloned.1.call-done, bf16[128,8192]{1,0:T(8,128)(2,1)} %param.8), kind=kLoop, calls=%fused_computation.48 | loop fusion | flops 3145728 | bytes 8388608 | tf_op jit(solution)/shard_map/convert_element_type | solution.py:51
  152.1 0.6 copy-done
  152.8 0.4 fusion.75
  153.2 8.1 %fusion.60 = bf16[16,8,8,128]{3,1,2,0:T(8,128)(2,1)S(1)} fusion(bf16[128,8192]{1,0:T(8,128)(2,1)S(1)} %add_convert_fusion.1, bf16[2,8192,1024]{2,1,0:T(8,128)(2,1)} %param.10), kind=kOutput, calls=%fused_computation.74 | convolution fusion | flops 2147614720 | bytes 19136512 | tf_op jit(solution)/shard_map/dot_general | solution.py:40
  161.3 0.8 copy.25
  162.1 2.1 all-to-all-start.2
  164.3 2.0 fusion.72
  166.2 4.6 %all-to-all-done.2 = bf16[128,8,128]{2,1,0:T(8,128)(2,1)S(1)} async-done(((bf16[128,8,128]{2,1,0:T(8,128)(2,1)}), bf16[128,8,128]{2,1,0:T(8,128)(2,1)S(1)}, u32[]{:S(2)}, u32[]{:S(2)}) %all-to-all-start.2) | async-done | bytes 262176 | tf_op jit(solution)/shard_map/all_to_all | solution.py:46
  170.8 12.5 %fusion.15 = f32[16,64,2048]{2,1,0:T(8,128)} fusion(pred[16,2048]{1,0:T(8,128)(4,1)S(1)} %get-tuple-element.10, bf16[2,16,2048,128]{3,2,1,0:T(8,128)(2,1)} %param.14, bf16[16,128]{1,0:T(8,128)(2,1)S(1)} %fusion.72, bf16[8,16,8,128]{3,2,1,0:T(8,128)(2,1)S(1)} %bitcast.97), kind=kOutput, calls=%fused_computation.19 | convolution fusion | flops 541065216 | bytes 17076224 | tf_op jit(solution)/shard_map/bhd,bsd->bhs/dot_general | solution.py:15
  183.4 12.0 %fusion.99 = (f32[16,64]{1,0:T(8,128)S(1)}, f32[16,64,2048]{2,1,0:T(8,128)}) fusion(f32[16,64,2048]{2,1,0:T(8,128)} %fusion.15, pred[16,2048]{1,0:T(8,128)(4,1)S(1)} %get-tuple-element.9), kind=kOutput, calls=%fused_computation.103 | output fusion | flops 12584959 | bytes 16814080 | tf_op jit(solution)/shard_map/sub | solution.py:18
  195.5 9.4 %fusion.53 = bf16[16,64,128]{2,1,0:T(8,128)(2,1)S(1)} fusion(pred[16,2048]{1,0:T(8,128)(4,1)S(1)} %get-tuple-element.10, bf16[2,16,2048,128]{3,2,1,0:T(8,128)(2,1)S(1)} %bitcast.93, bf16[16,128]{1,0:T(8,128)(2,1)S(1)} %fusion.75, f32[16,64,2048]{2,1,0:T(8,128)} %get-tuple-element.14, f32[16,64]{1,0:T(8,128)S(1)} %get-tuple-element.13), kind=kOutput, calls=%fused_computation.71 | convolution fusion | flops 545390592 | bytes 17084416 | tf_op jit(solution)/shard_map/bhs,bsd->bhd/dot_general | solution.py:19
  204.8 0.2 copy.21
  205.0 8.1 %all_to_all.67 = bf16[16,64,128]{2,0,1:T(8,128)(2,1)S(1)} all-to-all(bf16[16,64,128]{2,0,1:T(8,128)(2,1)S(1)} %copy.21), channel_id=1, replica_groups=mesh['replica'=1,'model'=8] {'model'}, dimensions={1} | all-to-all | bytes 524288 | tf_op jit(solution)/shard_map/all_to_all | solution.py:48
  213.2 10.1 %fusion.2 = f32[128,8192]{1,0:T(8,128)} fusion(bf16[2,1024,8192]{2,1,0:T(8,128)(2,1)} %param.13, bf16[16,8,8,128]{3,2,1,0:T(8,128)(2,1)S(1)} %bitcast.99), kind=kOutput, calls=%fused_computation.4 | convolution fusion | flops 2147483648 | bytes 21233664 | tf_op jit(solution)/shard_map/dot_general | solution.py:49
  223.3 20.2 %broadcast_select_fusion.1 = (bf16[1,16,2048,128]{3,2,1,0:T(8,128)(2,1)S(1)}, bf16[1,16,2048,128]{3,2,1,0:T(8,128)(2,1)}, bf16[1,16,2048,128]{3,2,1,0:T(8,128)(2,1)}, bf16[1,16,2048,128]{3,2,1,0:T(8,128)(2,1)}) fusion(pred[16,2048]{1,0:T(8,128)(4,1)S(1)} %get-tuple-element.10, bf16[2,16,2048,128]{3,2,1,0:T(8,128)(2,1)} %param.15, ...), kind=kLoop, calls=%fused_computation.31 | loop fusion | flops 16777216 | bytes 67158016 | tf_op jit(solution)/shard_map/jit(_where)/select_n | solution.py:9
  243.5 20.1 %pad_maximum_fusion = (bf16[2,16,2048,128]{3,2,1,0:T(8,128)(2,1)}, bf16[2,16,2048,128]{3,2,1,0:T(8,128)(2,1)}) fusion(bf16[1,16,2048,128]{3,2,1,0:T(8,128)(2,1)} %get-tuple-element.7, bf16[1,16,2048,128]{3,2,1,0:T(8,128)(2,1)} %get-tuple-element.8, bf16[1,16,2048,128]{3,2,1,0:T(8,128)(2,1)} %get-tuple-element.4, ...), kind=kLoop, calls=%fused_computation.2 | loop fusion | flops 16777216 | bytes 67108864 | tf_op jit(solution)/shard_map/stack | solution.py:54
  263.6 28.2 %all-reduce.5.cloned.1.call-done = f32[128,8192]{1,0:T(8,128)} async-done(((f32[128,8192]{1,0:T(8,128)}), f32[128,8192]{1,0:T(8,128)}) %all-reduce.5.cloned.1.call-update) | async-done | bytes 4194320 | tf_op jit(solution)/shard_map/psum | solution.py:50
  291.8 3.9 %add_convert_fusion = bf16[128,8192]{1,0:T(8,128)(2,1)} fusion(f32[128,8192]{1,0:T(8,128)} %all-reduce.5.cloned.1.call-done, bf16[128,8192]{1,0:T(8,128)(2,1)S(1)} %add_convert_fusion.1), kind=kLoop, calls=%fused_computation.44 | loop fusion | flops 3145728 | bytes 8388608 | tf_op jit(solution)/shard_map/convert_element_type | solution.py:51
  (28 shorter events, 0.4 us)
Async XLA Ops:
  7.2 13.9 %copy-start.1 = (s32[128]{0:T(128)S(1)}, s32[128]{0:T(128)}, u32[]{:S(2)}) copy-start(s32[128]{0:T(128)} %param.9) | copy-start | bytes 1540
  16.7 11.0 %all-to-all-start = ((bf16[128,8,128]{2,1,0:T(8,128)(2,1)}), bf16[128,8,128]{2,1,0:T(8,128)(2,1)S(1)}, u32[]{:S(2)}, u32[]{:S(2)}) async-start(bf16[128,8,128]{2,1,0:T(8,128)(2,1)} %bitcast.25), calls=%async_computation | async-start | bytes 524288 | tf_op jit(solution)/shard_map/all_to_all | solution.py:46
  21.0 127.7 %all-reduce.3.cloned.1.call-start = ((), (), s32[]{:S(2)}) async-start(), calls=%async_computation.4 | async-start | bytes 8388608 | tf_op jit(solution)/shard_map/psum | solution.py:50
  27.7 24.6 %slice-start = ((s8[16777216]{0:T(1024)(128)(4,1)}), s8[4194304]{0:T(1024)(128)(4,1)S(1)}, s32[]{:S(2)}) async-start(s8[16777216]{0:T(1024)(128)(4,1)} %bitcast.90), calls=%async_computation.6 | async-start | bytes 8388608
  27.7 24.6 %slice-start.1 = ((s8[16777216]{0:T(1024)(128)(4,1)}), s8[4194304]{0:T(1024)(128)(4,1)S(1)}, s32[]{:S(2)}) async-start(s8[16777216]{0:T(1024)(128)(4,1)} %bitcast.90), calls=%async_computation.7 | async-start | bytes 8388608
  27.7 24.6 %slice-start.2 = ((s8[16777216]{0:T(1024)(128)(4,1)}), s8[4194304]{0:T(1024)(128)(4,1)S(1)}, s32[]{:S(2)}) async-start(s8[16777216]{0:T(1024)(128)(4,1)} %bitcast.90), calls=%async_computation.8 | async-start | bytes 8388608
  40.2 12.1 %slice-start.3 = ((s8[16777216]{0:T(1024)(128)(4,1)}), s8[4194304]{0:T(1024)(128)(4,1)S(1)}, s32[]{:S(2)}) async-start(s8[16777216]{0:T(1024)(128)(4,1)} %bitcast.90), calls=%async_computation.9 | async-start | bytes 8388608
  148.7 4.1 %copy-start = (bf16[2,8192,128]{2,1,0:T(8,128)(2,1)S(1)}, bf16[2,8192,128]{2,1,0:T(8,128)(2,1)}, u32[]{:S(2)}) copy-start(bf16[2,8192,128]{2,1,0:T(8,128)(2,1)} %param.12) | copy-start | bytes 12582916
  162.1 8.8 %all-to-all-start.2 = ((bf16[128,8,128]{2,1,0:T(8,128)(2,1)}), bf16[128,8,128]{2,1,0:T(8,128)(2,1)S(1)}, u32[]{:S(2)}, u32[]{:S(2)}) async-start(bf16[128,8,128]{2,1,0:T(8,128)(2,1)} %bitcast.30), calls=%async_computation.2 | async-start | bytes 524288 | tf_op jit(solution)/shard_map/all_to_all | solution.py:46
  164.2 127.6 %all-reduce.5.cloned.1.call-start = ((), (), s32[]{:S(2)}) async-start(), calls=%async_computation.5 | async-start | bytes 8388608 | tf_op jit(solution)/shard_map/psum | solution.py:50
  170.8 24.6 %slice-start.4 = ((s8[16777216]{0:T(1024)(128)(4,1)}), s8[4194304]{0:T(1024)(128)(4,1)S(1)}, s32[]{:S(2)}) async-start(s8[16777216]{0:T(1024)(128)(4,1)} %bitcast.92), calls=%async_computation.10 | async-start | bytes 8388608
  170.8 24.6 %slice-start.5 = ((s8[16777216]{0:T(1024)(128)(4,1)}), s8[4194304]{0:T(1024)(128)(4,1)S(1)}, s32[]{:S(2)}) async-start(s8[16777216]{0:T(1024)(128)(4,1)} %bitcast.92), calls=%async_computation.11 | async-start | bytes 8388608
  170.8 24.6 %slice-start.6 = ((s8[16777216]{0:T(1024)(128)(4,1)}), s8[4194304]{0:T(1024)(128)(4,1)S(1)}, s32[]{:S(2)}) async-start(s8[16777216]{0:T(1024)(128)(4,1)} %bitcast.92), calls=%async_computation.12 | async-start | bytes 8388608
  183.4 12.1 %slice-start.7 = ((s8[16777216]{0:T(1024)(128)(4,1)}), s8[4194304]{0:T(1024)(128)(4,1)S(1)}, s32[]{:S(2)}) async-start(s8[16777216]{0:T(1024)(128)(4,1)} %bitcast.92), calls=%async_computation.13 | async-start | bytes 8388608
Sparse Core Ops, SparseCore 0:
  80.3 68.3 all-reduce.2
  223.4 68.3 all-reduce.4
where the time goes:
time: 304 us; the launch traced here: 303 us
  waiting for transfers between devices  104 us (34%)
  matrix products  87.4 us (29%)
  other arithmetic  71.9 us (24%)
  blocking collectives  16.2 us (5%)
  between operations  14.2 us (5%)
  starting transfers between devices  6.53 us (2%)
    psum x2, waiting for transfers between devices, device_step(): total = lax.psum(part_sum, 'model')  96.7 us
    dot_general x2, matrix products, attend_rows(): jnp.einsum('bhd,bsd->bhs', query, k_layer, preferred_element_type=jnp.flo...  25.1 us
    sub x2, other arithmetic, attend_rows(): weights = jax.nn.softmax(scores, axis=-1).astype(jnp.bfloat16)  24.1 us
    select_n x1, other arithmetic, write_token(): jnp.where(positions == cache_len[:, None, None], new_rows[:, None, :], ca...  20.2 us
    dot_general x2, matrix products, device_step(): jnp.dot(context.reshape(rows, local_heads * head_dim), w_out[layer], pref...  20.2 us
    another operation x1, other arithmetic, device_step(): return (hidden, jnp.stack(k_layers), jnp.stack(v_layers))  20.1 us
    dot_general x2, matrix products, attend_rows(): jnp.einsum('bhs,bsd->bhd', weights, v_layer, preferred_element_type=jnp.f...  18.8 us
    dot_general x2, matrix products, device_step(): jnp.dot(hidden, w_query[layer], preferred_element_type=jnp.float32)  16.9 us
  transfers between devices with their start and end apart: 4, of which 4 were waited for; matrix products, arithmetic and copies ran while one was open for 15% of the time, Pallas kernels for 0%

commit v1 on v0

v1 whole, which is shorter than its diff:
```python
import functools

import jax
import jax.numpy as jnp
from jax import lax
from jax.experimental import pallas as pl
from jax.experimental.pallas import tpu as pltpu
from jax.sharding import PartitionSpec as P

MESH = pl.DeviceIdType.MESH
BF16 = jnp.bfloat16
F32 = jnp.float32
VMEM_LIMIT = 62 * 1024 * 1024

DEVICES = 8
ROWS = 128
MY_ROWS = 16
D_MODEL = 8192
HEAD_DIM = 128
MY_HEADS = 8
NUM_HEADS = 64
MY_COLS = 1024
SEQ = 2048
TILE = 256
TILES = MY_COLS // TILE

GROUPS = 2
PIECE = MY_COLS // GROUPS
HALF = ROWS // 2


def dot(a, b):
    return jnp.dot(a, b, preferred_element_type=F32)


def places():
    me = lax.axis_index("model")
    core = lax.rem(me, 2)
    x = lax.rem(lax.div(me, 2), 2)
    y = lax.div(me, 4)
    flip = 1 - 2 * core
    xn = me + 2 - 4 * x
    yn = me + 4 - 8 * y
    diag = xn + 4 - 8 * y
    return me, flip, xn, yn, diag


class Copies:
    def __init__(self, send_sems, recv_sems):
        self.send_sems, self.recv_sems, self.started = send_sems, recv_sems, []

    def start(self, src, dst, device):
        i = len(self.started)
        copy = pltpu.make_async_remote_copy(
            src_ref=src,
            dst_ref=dst,
            send_sem=self.send_sems.at[i],
            recv_sem=self.recv_sems.at[i],
            device_id={"model": device},
            device_id_type=MESH,
        )
        copy.start()
        self.started.append(copy)
        return copy

    def finish(self):
        for copy in self.started:
            copy.wait_send()


class Loads:
    def __init__(self, sems):
        self.sems, self.count = sems, 0

    def start(self, src, dst):
        copy = pltpu.make_async_copy(src, dst, self.sems.at[self.count])
        copy.start()
        self.count += 1
        return copy


def meet_all(me):
    barrier = pltpu.get_barrier_semaphore()
    for k in range(1, DEVICES):
        pl.semaphore_signal(barrier, inc=1, device_id={"model": lax.rem(me + k, DEVICES)}, device_id_type=MESH)
    pl.semaphore_wait(barrier, DEVICES - 1)


def send_query_tile(copies, me, j, q_send, q_out):
    started = []
    for k in range(1, DEVICES):
        to = lax.rem(me + k, DEVICES)
        started.append(copies.start(q_send.at[j, to], q_out.at[j, me], to))
    return started


def new_rows(h_rows, w):
    return dot(h_rows, w)


def query_kernel(x_hbm, wq_hbm, wk_hbm, wv_hbm, q_out, kn_out, vn_out,
                 x_buf, wq_buf, wk_buf, wv_buf, q_send, load_sems, send_sems, recv_sems):
    me, _, _, _, _ = places()
    loads = Loads(load_sems)
    x_load = loads.start(x_hbm, x_buf)
    wq_loads = [loads.start(wq_hbm.at[0, :, pl.ds(j * TILE, TILE)], wq_buf.at[j]) for j in range(TILES)]
    wk_load = loads.start(wk_hbm.at[0], wk_buf)
    wv_load = loads.start(wv_hbm.at[0], wv_buf)
    meet_all(me)
    copies = Copies(send_sems, recv_sems)
    x_load.wait()
    arrivals = []
    for j in range(TILES):
        wq_loads[j].wait()
        q_send[j] = dot(x_buf[...], wq_buf[j]).astype(BF16).reshape(DEVICES, MY_ROWS, TILE)
        arrivals += send_query_tile(copies, me, j, q_send, q_out)
        q_out[j, me] = q_send[j, me]
    x_rows = x_buf[pl.ds(pl.multiple_of(me * MY_ROWS, MY_ROWS), MY_ROWS), :]
    wk_load.wait()
    kn_out[...] = dot(x_rows, wk_buf[...]).astype(BF16)
    wv_load.wait()
    vn_out[...] = dot(x_rows, wv_buf[...]).astype(BF16)
    for copy in arrivals:
        copy.wait_recv()
    copies.finish()


def query_call(x, w_query, w_key, w_value):
    any_spec = pl.BlockSpec(memory_space=pl.ANY)
    vmem_spec = pl.BlockSpec(memory_space=pltpu.VMEM)
    sends = TILES * (DEVICES - 1)
    return pl.pallas_call(
        query_kernel,
        name="query",
        out_shape=(
            jax.ShapeDtypeStruct((TILES, DEVICES, MY_ROWS, TILE), BF16),
            jax.ShapeDtypeStruct((MY_ROWS, HEAD_DIM), BF16),
            jax.ShapeDtypeStruct((MY_ROWS, HEAD_DIM), BF16),
        ),
        in_specs=[any_spec] * 4,
        out_specs=(vmem_spec,) * 3,
        scratch_shapes=[
            pltpu.VMEM((ROWS, D_MODEL), BF16),
            pltpu.VMEM((TILES, D_MODEL, TILE), BF16),
            pltpu.VMEM((D_MODEL, HEAD_DIM), BF16),
            pltpu.VMEM((D_MODEL, HEAD_DIM), BF16),
            pltpu.VMEM((TILES, DEVICES, MY_ROWS, TILE), BF16),
            pltpu.SemaphoreType.DMA((TILES + 3,)),
            pltpu.SemaphoreType.DMA((sends,)),
            pltpu.SemaphoreType.DMA((sends,)),
        ],
        compiler_params=pltpu.CompilerParams(
            collective_id=0, has_side_effects=True, vmem_limit_bytes=VMEM_LIMIT
        ),
    )(x, w_query, w_key, w_value)


def attend_kernel(layer, has_prev, *refs):
    if has_prev:
        len_ref, q_ref, kn_ref, vn_ref, k_hbm, v_hbm, _, _ = refs[:8]
        rest = refs[8:]
    else:
        len_ref, q_ref, kn_ref, vn_ref, k_hbm, v_hbm = refs[:6]
        rest = refs[6:]
    ctx_ref, k_out, v_out, k_buf, v_buf, q_buf, kn_buf, vn_buf, in_sems, out_sems = rest
    me = lax.axis_index("model")

    def load(which, b):
        hbm, buf = ((k_hbm, k_buf), (v_hbm, v_buf))[which]
        return pltpu.make_async_copy(hbm.at[layer, b], buf.at[b], in_sems.at[which, b])

    def save(which, b):
        hbm, buf = ((k_out, k_buf), (v_out, v_buf))[which]
        return pltpu.make_async_copy(buf.at[b], hbm.at[layer, b], out_sems.at[which, b])

    @pl.loop(0, MY_ROWS)
    def _(b):
        load(0, b).start()
        load(1, b).start()

    kn_buf[...] = kn_ref[...].astype(F32)
    vn_buf[...] = vn_ref[...].astype(F32)
    for j in range(TILES):
        for src in range(DEVICES):
            block = q_ref[j, src].astype(F32)
            for h in range(TILE // HEAD_DIM):
                head = src * MY_HEADS + j * (TILE // HEAD_DIM) + h
                q_buf[:, head, :] = block[:, h * HEAD_DIM:(h + 1) * HEAD_DIM]

    scale = HEAD_DIM ** -0.5

    @pl.loop(0, MY_ROWS)
    def _(b):
        pos = len_ref[me * MY_ROWS + b]
        base = pl.multiple_of((pos // 16) * 16, 16)
        here = lax.broadcasted_iota(jnp.int32, (16, HEAD_DIM), 0) == pos - base

        def patch(buf, new):
            tile = buf[b, pl.ds(base, 16), :].astype(F32)
            row = jnp.broadcast_to(new[pl.ds(b, 1), :], (16, HEAD_DIM))
            buf[b, pl.ds(base, 16), :] = jnp.where(here, row, tile).astype(BF16)

        def attend(n):
            q = q_buf[b].astype(BF16)
            k = k_buf[b, 0:n, :]
            s = lax.dot_general(q, k, (((1,), (1,)), ((), ())), preferred_element_type=F32) * scale
            t = lax.broadcasted_iota(jnp.int32, (NUM_HEADS, n), 1)
            s = jnp.where(t <= pos, s, -jnp.inf)
            e = jnp.exp(s - jnp.max(s, axis=1, keepdims=True))
            p = (e * (1.0 / jnp.sum(e, axis=1, keepdims=True))).astype(BF16)
            c = dot(p, v_buf[b, 0:n, :])
            ctx_ref[:, b] = c.reshape(DEVICES, MY_HEADS, HEAD_DIM).astype(BF16)

        load(0, b).wait()
        patch(k_buf, kn_buf)
        load(1, b).wait()
        patch(v_buf, vn_buf)

        @pl.when(pos < 256)
        def _():
            attend(256)

        @pl.when(jnp.logical_and(pos >= 256, pos < 1024))
        def _():
            attend(1024)

        @pl.when(pos >= 1024)
        def _():
            attend(2048)

        save(0, b).start()
        save(1, b).start()

    @pl.loop(0, MY_ROWS)
    def _(b):
        save(0, b).wait()
        save(1, b).wait()


def attend_call(layer, cache_len, q, kn, vn, k_cache, v_cache, prev):
    any_spec = pl.BlockSpec(memory_space=pl.ANY)
    vmem_spec = pl.BlockSpec(memory_space=pltpu.VMEM)
    return pl.pallas_call(
        functools.partial(attend_kernel, layer, bool(prev)),
        name="attend",
        out_shape=(
            jax.ShapeDtypeStruct((DEVICES, MY_ROWS, MY_HEADS, HEAD_DIM), BF16),
            jax.ShapeDtypeStruct(k_cache.shape, BF16),
            jax.ShapeDtypeStruct(v_cache.shape, BF16),
        ),
        in_specs=[pl.BlockSpec(memory_space=pltpu.SMEM)] + [vmem_spec] * 3 + [any_spec] * (2 + len(prev)),
        out_specs=(vmem_spec, any_spec, any_spec),
        scratch_shapes=[
            pltpu.VMEM((MY_ROWS, SEQ, HEAD_DIM), BF16),
            pltpu.VMEM((MY_ROWS, SEQ, HEAD_DIM), BF16),
            pltpu.VMEM((MY_ROWS, NUM_HEADS, HEAD_DIM), F32),
            pltpu.VMEM((MY_ROWS, HEAD_DIM), F32),
            pltpu.VMEM((MY_ROWS, HEAD_DIM), F32),
            pltpu.SemaphoreType.DMA((2, MY_ROWS)),
            pltpu.SemaphoreType.DMA((2, MY_ROWS)),
        ],
        input_output_aliases={6: 1, 7: 2} if prev else {},
        compiler_params=pltpu.CompilerParams(vmem_limit_bytes=VMEM_LIMIT),
    )(cache_len, q, kn, vn, k_cache, v_cache, *prev)


SELF, XN, YN, DIAG = range(4)


def combine_kernel(layer, last, *refs):
    if last:
        (ctx_in, res_hbm, wo_hbm, out_hbm,
         ctx_buf, lhs, res_buf, wo_buf, send_d2d, recv_d2d, acc, rx_diag, ry_diag, rx_dir, ry_dir, rx_fwd, ry_fwd, h_buf,
         load_sems, send_sems, recv_sems) = refs
    else:
        (ctx_in, res_hbm, wo_hbm, wq_hbm, wk_hbm, wv_hbm, own_out, q_out, kn_out, vn_out,
         ctx_buf, lhs, res_buf, wo_buf, send_d2d, recv_d2d, acc, rx_diag, ry_diag, rx_dir, ry_dir, rx_fwd, ry_fwd, h_buf,
         wq_buf, wk_buf, wv_buf, q_acc, q_send,
         load_sems, send_sems, recv_sems) = refs
    me, flip, xn, yn, diag = places()
    partner = me + flip
    chip_mate = {SELF: me, XN: xn, YN: yn, DIAG: diag}
    owner = lambda r, c: chip_mate[r] + c * flip
    column = lambda r, c, g: pl.multiple_of(owner(r, c) * MY_COLS + g * PIECE, PIECE)
    loads = Loads(load_sems)
    copies = Copies(send_sems, recv_sems)
    order = (DIAG, XN, YN, SELF)
    steps = [(g, r) for g in range(GROUPS) for r in order]
    top, bottom = pl.ds(0, HALF), pl.ds(HALF, HALF)

    own_load = loads.start(ctx_in.at[me], ctx_buf.at[me])
    wo_loads = {}
    for g, r in steps:
        for c in (1, 0):
            wo_loads[g, r, c] = loads.start(wo_hbm.at[layer, :, pl.ds(column(r, c, g), PIECE)], wo_buf.at[g, r, c])
    if last:
        res_load = loads.start(res_hbm, res_buf)
    else:
        res_load = loads.start(res_hbm.at[:, pl.ds(pl.multiple_of(me * MY_COLS, MY_COLS), MY_COLS)], res_buf)
        wq_loads = {}
        for r in (SELF, XN, YN, DIAG):
            for c in (0, 1):
                for g in range(GROUPS):
                    wq_loads[r, c, g] = loads.start(
                        wq_hbm.at[layer + 1, pl.ds(column(r, c, g), PIECE), :], wq_buf.at[r, c, g])
        wk_load = loads.start(wk_hbm.at[layer + 1], wk_buf)
        wv_load = loads.start(wv_hbm.at[layer + 1], wv_buf)

    meet_all(me)

    arrivals = []
    for k in range(1, DEVICES):
        to = lax.rem(me + k, DEVICES)
        arrivals.append(copies.start(ctx_in.at[to], ctx_buf.at[me], to))
    own_load.wait()
    for copy in arrivals:
        copy.wait_recv()
    for src in range(DEVICES):
        rows = ctx_buf[src].astype(F32).reshape(MY_ROWS, MY_COLS).astype(BF16)
        lhs[src * MY_ROWS:(src + 1) * MY_ROWS, :] = rows

    d2d = {}
    first, direct, forward = {}, {}, {}

    def settle(g, r):
        d2d[g, r].wait_recv()
        acc[g, r] += recv_d2d[g, r]
        if r == DIAG:
            first[g, 0] = copies.start(acc.at[g, r, top], rx_diag.at[g], xn)
            first[g, 1] = copies.start(acc.at[g, r, bottom], ry_diag.at[g], yn)

    def send_direct(g):
        direct[g, 0] = copies.start(acc.at[g, XN, top], rx_dir.at[g], xn)
        direct[g, 1] = copies.start(acc.at[g, YN, bottom], ry_dir.at[g], yn)

    pending = None
    for g, r in steps:
        wo_loads[g, r, 1].wait()
        send_d2d[g, r] = dot(lhs[...], wo_buf[g, r, 1])
        d2d[g, r] = copies.start(send_d2d.at[g, r], recv_d2d.at[g, r], partner)
        wo_loads[g, r, 0].wait()
        acc[g, r] = dot(lhs[...], wo_buf[g, r, 0])
        if pending is not None:
            settle(*pending)
            if pending == (0, YN):
                send_direct(0)
        pending = (g, r)
    settle(*pending)
    if GROUPS == 1:
        pass

    for g in range(GROUPS):
        first[g, 0].wait_recv()
        acc[g, YN, top] += rx_diag[g]
        forward[g, 1] = copies.start(acc.at[g, YN, top], ry_fwd.at[g], yn)
        first[g, 1].wait_recv()
        acc[g, XN, bottom] += ry_diag[g]
        forward[g, 0] = copies.start(acc.at[g, XN, bottom], rx_fwd.at[g], xn)
        if g + 1 < GROUPS:
            send_direct(g + 1)

    res_load.wait()
    gather = {}

    def finish_piece(g):
        cols = slice(g * PIECE, (g + 1) * PIECE)
        direct[g, 0].wait_recv()
        forward[g, 1].wait_recv()
        total = acc[g, SELF, top] + rx_dir[g] + ry_fwd[g]
        h_buf[SELF, 0, g, top] = (res_buf[top, cols].astype(F32) + total).astype(BF16)
        direct[g, 1].wait_recv()
        forward[g, 0].wait_recv()
        total = acc[g, SELF, bottom] + ry_dir[g] + rx_fwd[g]
        h_buf[SELF, 0, g, bottom] = (res_buf[bottom, cols].astype(F32) + total).astype(BF16)
        mine = h_buf.at[SELF, 0, g]
        gather[XN, 0, g] = [copies.start(mine, h_buf.at[XN, 0, g], xn)]
        gather[YN, 0, g] = [copies.start(mine, h_buf.at[YN, 0, g], yn)]
        gather[SELF, 1, g] = [copies.start(mine, h_buf.at[SELF, 1, g], partner)]
        if not last:
            own_out[:, cols] = h_buf[SELF, 0, g]

    def arrive(r, c, g):
        for copy in gather[r, c, g]:
            copy.wait_recv()

    stores = []
    if last:
        def use(r, c, g):
            stores.append(loads.start(h_buf.at[r, c, g], out_hbm.at[:, pl.ds(column(r, c, g), PIECE)]))
    else:
        q_acc[...] = jnp.zeros_like(q_acc)

        def use(r, c, g):
            wq_loads[r, c, g].wait()
            q_acc[...] += dot(h_buf[r, c, g], wq_buf[r, c, g])

    for g in range(GROUPS):
        finish_piece(g)
    for g in range(GROUPS):
        use(SELF, 0, g)
    for g in range(GROUPS):
        arrive(SELF, 1, g)
        use(SELF, 1, g)
    for g in range(GROUPS):
        arrive(XN, 0, g)
        down = [copies.start(h_buf.at[XN, 0, g, top], h_buf.at[DIAG, 0, g, top], yn)]
        gather[XN, 1, g] = [copies.start(h_buf.at[XN, 0, g], h_buf.at[XN, 1, g], partner)]
        arrive(YN, 0, g)
        down += [copies.start(h_buf.at[YN, 0, g, bottom], h_buf.at[DIAG, 0, g, bottom], xn)]
        gather[DIAG, 0, g] = down
        gather[YN, 1, g] = [copies.start(h_buf.at[YN, 0, g], h_buf.at[YN, 1, g], partner)]
        use(XN, 0, g)
        use(YN, 0, g)
        arrive(XN, 1, g)
        use(XN, 1, g)
        arrive(YN, 1, g)
        use(YN, 1, g)
    for g in range(GROUPS):
        arrive(DIAG, 0, g)
        gather[DIAG, 1, g] = [copies.start(h_buf.at[DIAG, 0, g], h_buf.at[DIAG, 1, g], partner)]
        use(DIAG, 0, g)
    for g in range(GROUPS):
        arrive(DIAG, 1, g)
        use(DIAG, 1, g)

    if last:
        for store in stores:
            store.wait()
    else:
        arrivals = []
        for j in range(TILES):
            q_send[j] = q_acc[:, j * TILE:(j + 1) * TILE].astype(BF16).reshape(DEVICES, MY_ROWS, TILE)
            arrivals += send_query_tile(copies, me, j, q_send, q_out)
            q_out[j, me] = q_send[j, me]
        wk_load.wait()
        wv_load.wait()
        mine = pl.ds(pl.multiple_of(me * MY_ROWS, MY_ROWS), MY_ROWS)
        kn = jnp.zeros((MY_ROWS, HEAD_DIM), F32)
        vn = jnp.zeros((MY_ROWS, HEAD_DIM), F32)
        for r in (SELF, XN, YN, DIAG):
            for c in (0, 1):
                for g in range(GROUPS):
                    rows = h_buf[r, c, g, mine, :]
                    depth = pl.ds(column(r, c, g), PIECE)
                    kn += dot(rows, wk_buf[depth, :])
                    vn += dot(rows, wv_buf[depth, :])
        kn_out[...] = kn.astype(BF16)
        vn_out[...] = vn.astype(BF16)
        for copy in arrivals:
            copy.wait_recv()
    copies.finish()


def combine_call(layer, last, ctx, residual, w_out, more):
    any_spec = pl.BlockSpec(memory_space=pl.ANY)
    vmem_spec = pl.BlockSpec(memory_space=pltpu.VMEM)
    sends = (DEVICES - 1) + GROUPS * (4 + 6 + 9)
    loads = 1 + 8 * GROUPS + 1 + 8 * GROUPS
    scratch = [
        pltpu.VMEM((DEVICES, MY_ROWS, MY_HEADS, HEAD_DIM), BF16),
        pltpu.VMEM((ROWS, MY_COLS), BF16),
        pltpu.VMEM((ROWS, MY_COLS), BF16),
        pltpu.VMEM((GROUPS, 4, 2, MY_COLS, PIECE), BF16),
        pltpu.VMEM((GROUPS, 4, ROWS, PIECE), F32),
        pltpu.VMEM((GROUPS, 4, ROWS, PIECE), F32),
        pltpu.VMEM((GROUPS, 4, ROWS, PIECE), F32),
    ] + [pltpu.VMEM((GROUPS, HALF, PIECE), F32)] * 6 + [
        pltpu.VMEM((4, 2, GROUPS, ROWS, PIECE), BF16),
    ]
    if last:
        out_shape = jax.ShapeDtypeStruct((ROWS, D_MODEL), BF16)
        out_specs = any_spec
    else:
        out_shape = (
            jax.ShapeDtypeStruct((ROWS, MY_COLS), BF16),
            jax.ShapeDtypeStruct((TILES, DEVICES, MY_ROWS, TILE), BF16),
            jax.ShapeDtypeStruct((MY_ROWS, HEAD_DIM), BF16),
            jax.ShapeDtypeStruct((MY_ROWS, HEAD_DIM), BF16),
        )
        out_specs = (vmem_spec,) * 4
        sends += TILES * (DEVICES - 1)
        loads += 2
        scratch += [
            pltpu.VMEM((4, 2, GROUPS, PIECE, MY_COLS), BF16),
            pltpu.VMEM((D_MODEL, HEAD_DIM), BF16),
            pltpu.VMEM((D_MODEL, HEAD_DIM), BF16),
            pltpu.VMEM((ROWS, MY_COLS), F32),
            pltpu.VMEM((TILES, DEVICES, MY_ROWS, TILE), BF16),
        ]
    scratch += [
        pltpu.SemaphoreType.DMA((loads,)),
        pltpu.SemaphoreType.DMA((sends,)),
        pltpu.SemaphoreType.DMA((sends,)),
    ]
    return pl.pallas_call(
        functools.partial(combine_kernel, layer, last),
        name="combine_last" if last else "combine",
        out_shape=out_shape,
        in_specs=[vmem_spec] + [any_spec] * (2 + len(more)),
        out_specs=out_specs,
        scratch_shapes=scratch,
        compiler_params=pltpu.CompilerParams(
            collective_id=2 if last else 1, has_side_effects=True, vmem_limit_bytes=VMEM_LIMIT
        ),
    )(ctx, residual, w_out, *more)


def solution(mesh):
    cache_spec = P(None, ("replica", "model"), None, None)

    def device_step(x, cache_len, w_query, w_key, w_value, w_out, k_cache, v_cache):
        q, kn, vn = query_call(x, w_query, w_key, w_value)
        ctx, k_all, v_all = attend_call(0, cache_len, q, kn, vn, k_cache, v_cache, ())
        own, q, kn, vn = combine_call(0, False, ctx, x, w_out, (w_query, w_key, w_value))
        ctx, k_all, v_all = attend_call(1, cache_len, q, kn, vn, k_cache, v_cache, (k_all, v_all))
        out = combine_call(1, True, ctx, own, w_out, ())
        return out, k_all, v_all

    return jax.shard_map(
        device_step,
        mesh=mesh,
        in_specs=(P("replica", None), P("replica"), P(None, None, "model"), P(), P(), P(None, "model", None), cache_spec, cache_spec),
        out_specs=(P("replica", None), cache_spec, cache_spec),
        check_vma=False,
    )
```

time: 304 us -> 134 us (0.44)
  Pallas kernels: 0 us -> 129 us
  waiting for transfers between devices: 104 us -> 0 us
  matrix products: 87.4 us -> 0 us
  other arithmetic: 71.9 us -> 0 us
  blocking collectives: 16.2 us -> 0 us
  between operations: 14.2 us -> 0.67 us
  starting transfers between devices: 6.53 us -> 0 us
    pallas_call x0 -> x5, Pallas kernels: none -> 129 us  [the longest x2 85.8 us: combine_call(): pl.pallas_call(functools.partial(combine_kernel, layer, last), name='comb...]
    psum x2 -> x0, waiting for transfers between devices: 96.7 us -> none  [device_step(): total = lax.psum(part_sum, 'model')]
    dot_general x12 -> x0, matrix products: 87.4 us -> none  [the longest x2 25.1 us: attend_rows(): jnp.einsum('bhd,bsd->bhs', query, k_layer, preferred_element_type=jnp.flo...]
    sub x2 -> x0, other arithmetic: 24.1 us -> none  [attend_rows(): weights = jax.nn.softmax(scores, axis=-1).astype(jnp.bfloat16)]
    select_n x1 -> x0, other arithmetic: 20.2 us -> none  [write_token(): jnp.where(positions == cache_len[:, None, None], new_rows[:, None, :], ca...]
    another operation x1 -> x0, other arithmetic: 20.1 us -> none  [device_step(): return (hidden, jnp.stack(k_layers), jnp.stack(v_layers))]
    all_to_all x2 -> x0, blocking collectives: 16.2 us -> none  [device_step(): context = lax.all_to_all(context, 'model', 1, 0, tiled=True)]
    convert_element_type x2 -> x0, other arithmetic: 7.33 us -> none  [device_step(): hidden = (hidden.astype(jnp.float32) + total).astype(jnp.bfloat16)]
  transfers between devices with their start and end apart: 4 -> 0, of which waited for: 4 -> 0; matrix products, arithmetic and copies ran while one was open for 15% -> 0% of each run, Pallas kernels for 0% -> 0%
where the time goes in v1:
time: 134 us; the launch traced here: 133 us
  Pallas kernels  129 us (96%)
  local copies, waits for them, and re-layouts  3.1 us (2%)
    pallas_call x2, Pallas kernels, combine_call(): pl.pallas_call(functools.partial(combine_kernel, layer, last), name='comb...  85.8 us
    pallas_call x2, Pallas kernels, attend_call(): pl.pallas_call(functools.partial(attend_kernel, layer, bool(prev)), name=...  28.4 us
    pallas_call x1, Pallas kernels, query_call(): pl.pallas_call(query_kernel, name='query', out_shape=(jax.ShapeDtypeStruc...  15.1 us
    unnamed x1, local copies, waits for them, and re-layouts  3.1 us

profile of v1, /device:TPU:0, one launch (start us, length us, event | category | flops | bytes accessed | tf_op | source)
XLA Modules:
  0.0 133.0 jit_solution(17871107328979035675)
XLA Ops:
  0.6 15.1 %query.1 = (bf16[4,8,16,256]{3,2,1,0:T(8,128)(2,1)}, bf16[16,128]{1,0:T(8,128)(2,1)}, bf16[16,128]{1,0:T(8,128)(2,1)}) custom-call(bf16[128,8192]{1,0:T(8,128)(2,1)} %refs_1_.1, bf16[2,8192,1024]{2,1,0:T(8,128)(2,1)} %refs_3_.1, bf16[2,8192,128]{2,1,0:T(8,128)(2,1)} %refs_4_.4, bf16[2,8192,128]{2,1,0:T(8,128)(2,1)} %refs_5_.4), custom_call_target="tpu_custom_call" | custom-call | tf_op jit(solution)/shard_map/query/pallas_call | solution.py:132
  15.7 14.3 %attend.2 = (bf16[8,16,8,128]{3,2,1,0:T(8,128)(2,1)}, bf16[2,16,2048,128]{3,2,1,0:T(8,128)(2,1)}, bf16[2,16,2048,128]{3,2,1,0:T(8,128)(2,1)}) custom-call(s32[128]{0:T(128)} %refs_0_.3, bf16[4,8,16,256]{3,2,1,0:T(8,128)(2,1)} %get-tuple-element.16.refs_1_, bf16[16,128]{1,0:T(8,128)(2,1)} %get-tuple-element.17.refs_2_, ...), custom_call_target="tpu_custom_call" | custom-call | tf_op jit(solution)/shard_map/attend/pallas_call | solution.py:243
  30.0 45.8 %combine.1 = (bf16[128,1024]{1,0:T(8,128)(2,1)}, bf16[4,8,16,256]{3,2,1,0:T(8,128)(2,1)}, bf16[16,128]{1,0:T(8,128)(2,1)}, bf16[16,128]{1,0:T(8,128)(2,1)}) custom-call(bf16[8,16,8,128]{3,2,1,0:T(8,128)(2,1)} %get-tuple-element.19.refs_0_, bf16[128,8192]{1,0:T(8,128)(2,1)} %refs_1_.1, bf16[2,1024,8192]{2,1,0:T(8,128)(2,1)} %refs_2_.3, ...), custom_call_target="tpu_custom_call" | custom-call | tf_op jit(solution)/shard_map/combine/pallas_call | solution.py:495
  75.8 14.1 %attend.3 = (bf16[8,16,8,128]{3,2,1,0:T(8,128)(2,1)}, bf16[2,16,2048,128]{3,2,1,0:T(8,128)(2,1)}, bf16[2,16,2048,128]{3,2,1,0:T(8,128)(2,1)}) custom-call(s32[128]{0:T(128)} %refs_0_.3, bf16[4,8,16,256]{3,2,1,0:T(8,128)(2,1)} %get-tuple-element.20.refs_1_, bf16[16,128]{1,0:T(8,128)(2,1)} %get-tuple-element.21.refs_2_, ...), custom_call_target="tpu_custom_call", output_to_operand_aliasing={{1}: (6, {}), {2}: (7, {})} | custom-call | tf_op jit(solution)/shard_map/attend/pallas_call | solution.py:243
  89.9 40.0 %combine_last.1 = bf16[128,8192]{1,0:T(8,128)(2,1)} custom-call(bf16[8,16,8,128]{3,2,1,0:T(8,128)(2,1)} %get-tuple-element.25.refs_0_, bf16[128,1024]{1,0:T(8,128)(2,1)} %get-tuple-element.26.refs_1_, bf16[2,1024,8192]{2,1,0:T(8,128)(2,1)} %refs_2_.3), custom_call_target="tpu_custom_call" | custom-call | tf_op jit(solution)/shard_map/combine_last/pallas_call | solution.py:495
  129.9 3.1 %copy.16 = bf16[128,8192]{1,0:T(8,128)(2,1)} copy(bf16[128,8192]{1,0:T(8,128)(2,1)} %combine_last.1) | data formatting | bytes 4194304

commit v2 on v1

--- a/solution.py
+++ b/solution.py
@@ -10,7 +10,7 @@
 MESH = pl.DeviceIdType.MESH
 BF16 = jnp.bfloat16
 F32 = jnp.float32
-VMEM_LIMIT = 62 * 1024 * 1024
+MIB = 1024 * 1024
 
 DEVICES = 8
 ROWS = 128
@@ -24,9 +24,13 @@
 TILE = 256
 TILES = MY_COLS // TILE
 
+HALF_COLS = 512
 GROUPS = 2
 PIECE = MY_COLS // GROUPS
 HALF = ROWS // 2
+SLOTS = 8 * GROUPS
+TOGETHER = 2
+SPANS = (256, 1024, 2048)
 
 
 def dot(a, b):
@@ -98,7 +102,27 @@
     return dot(h_rows, w)
 
 
-def query_kernel(x_hbm, wq_hbm, wk_hbm, wv_hbm, q_out, kn_out, vn_out,
+def load_cache(loads, layer, k_hbm, v_hbm, kv_pre):
+    return [loads.start(hbm.at[layer], kv_pre.at[i]) for i, hbm in enumerate((k_hbm, v_hbm))]
+
+
+def in_vmem(*arrays):
+    return [pltpu.with_memory_space_constraint(a, pltpu.VMEM) for a in arrays]
+
+
+def in_hbm(*arrays):
+    return [pltpu.with_memory_space_constraint(a, pltpu.HBM) for a in arrays]
+
+
+QUERY_SHAPES = (
+    pltpu.VMEM((TILES, DEVICES, MY_ROWS, TILE), BF16),
+    pltpu.VMEM((MY_ROWS, HEAD_DIM), BF16),
+    pltpu.VMEM((MY_ROWS, HEAD_DIM), BF16),
+    pltpu.VMEM((2, MY_ROWS, SEQ, HEAD_DIM), BF16),
+)
+
+
+def query_kernel(x_hbm, wq_hbm, wk_hbm, wv_hbm, k_hbm, v_hbm, q_out, kn_out, vn_out, kv_pre,
                  x_buf, wq_buf, wk_buf, wv_buf, q_send, load_sems, send_sems, recv_sems):
     me, _, _, _, _ = places()
     loads = Loads(load_sems)
@@ -106,6 +130,7 @@
     wq_loads = [loads.start(wq_hbm.at[0, :, pl.ds(j * TILE, TILE)], wq_buf.at[j]) for j in range(TILES)]
     wk_load = loads.start(wk_hbm.at[0], wk_buf)
     wv_load = loads.start(wv_hbm.at[0], wv_buf)
+    cache_loads = load_cache(loads, 0, k_hbm, v_hbm, kv_pre)
     meet_all(me)
     copies = Copies(send_sems, recv_sems)
     x_load.wait()
@@ -123,60 +148,44 @@
     for copy in arrivals:
         copy.wait_recv()
     copies.finish()
-
-
-def query_call(x, w_query, w_key, w_value):
+    for load in cache_loads:
+        load.wait()
+
+
+def query_call(x, w_query, w_key, w_value, k_cache, v_cache):
     any_spec = pl.BlockSpec(memory_space=pl.ANY)
     vmem_spec = pl.BlockSpec(memory_space=pltpu.VMEM)
     sends = TILES * (DEVICES - 1)
     return pl.pallas_call(
         query_kernel,
         name="query",
-        out_shape=(
-            jax.ShapeDtypeStruct((TILES, DEVICES, MY_ROWS, TILE), BF16),
-            jax.ShapeDtypeStruct((MY_ROWS, HEAD_DIM), BF16),
-            jax.ShapeDtypeStruct((MY_ROWS, HEAD_DIM), BF16),
-        ),
-        in_specs=[any_spec] * 4,
-        out_specs=(vmem_spec,) * 3,
+        out_shape=QUERY_SHAPES,
+        in_specs=[any_spec] * 6,
+        out_specs=(vmem_spec,) * len(QUERY_SHAPES),
         scratch_shapes=[
             pltpu.VMEM((ROWS, D_MODEL), BF16),
             pltpu.VMEM((TILES, D_MODEL, TILE), BF16),
             pltpu.VMEM((D_MODEL, HEAD_DIM), BF16),
             pltpu.VMEM((D_MODEL, HEAD_DIM), BF16),
             pltpu.VMEM((TILES, DEVICES, MY_ROWS, TILE), BF16),
-            pltpu.SemaphoreType.DMA((TILES + 3,)),
+            pltpu.SemaphoreType.DMA((TILES + 5,)),
             pltpu.SemaphoreType.DMA((sends,)),
             pltpu.SemaphoreType.DMA((sends,)),
         ],
         compiler_params=pltpu.CompilerParams(
-            collective_id=0, has_side_effects=True, vmem_limit_bytes=VMEM_LIMIT
+            collective_id=0, has_side_effects=True, vmem_limit_bytes=26 * MIB
         ),
-    )(x, w_query, w_key, w_value)
-
-
-def attend_kernel(layer, has_prev, *refs):
-    if has_prev:
-        len_ref, q_ref, kn_ref, vn_ref, k_hbm, v_hbm, _, _ = refs[:8]
-        rest = refs[8:]
-    else:
-        len_ref, q_ref, kn_ref, vn_ref, k_hbm, v_hbm = refs[:6]
-        rest = refs[6:]
-    ctx_ref, k_out, v_out, k_buf, v_buf, q_buf, kn_buf, vn_buf, in_sems, out_sems = rest
+    )(*in_hbm(x, w_query, w_key, w_value, k_cache, v_cache))
+
+
+def attend_kernel(layer, has_prev, len_ref, q_ref, kn_ref, vn_ref, *refs):
+    k_out, v_out, ctx_ref, kv_buf, q_buf, kn_buf, vn_buf, out_sems = refs[-8:]
+    k_buf, v_buf = kv_buf.at[0], kv_buf.at[1]
     me = lax.axis_index("model")
-
-    def load(which, b):
-        hbm, buf = ((k_hbm, k_buf), (v_hbm, v_buf))[which]
-        return pltpu.make_async_copy(hbm.at[layer, b], buf.at[b], in_sems.at[which, b])
 
     def save(which, b):
         hbm, buf = ((k_out, k_buf), (v_out, v_buf))[which]
         return pltpu.make_async_copy(buf.at[b], hbm.at[layer, b], out_sems.at[which, b])
-
-    @pl.loop(0, MY_ROWS)
-    def _(b):
-        load(0, b).start()
-        load(1, b).start()
 
     kn_buf[...] = kn_ref[...].astype(F32)
     vn_buf[...] = vn_ref[...].astype(F32)
@@ -194,42 +203,40 @@
         pos = len_ref[me * MY_ROWS + b]
         base = pl.multiple_of((pos // 16) * 16, 16)
         here = lax.broadcasted_iota(jnp.int32, (16, HEAD_DIM), 0) == pos - base
-
-        def patch(buf, new):
+        for buf, new in ((k_buf, kn_buf), (v_buf, vn_buf)):
             tile = buf[b, pl.ds(base, 16), :].astype(F32)
             row = jnp.broadcast_to(new[pl.ds(b, 1), :], (16, HEAD_DIM))
             buf[b, pl.ds(base, 16), :] = jnp.where(here, row, tile).astype(BF16)
 
-        def attend(n):
-            q = q_buf[b].astype(BF16)
-            k = k_buf[b, 0:n, :]
-            s = lax.dot_general(q, k, (((1,), (1,)), ((), ())), preferred_element_type=F32) * scale
-            t = lax.broadcasted_iota(jnp.int32, (NUM_HEADS, n), 1)
-            s = jnp.where(t <= pos, s, -jnp.inf)
-            e = jnp.exp(s - jnp.max(s, axis=1, keepdims=True))
-            p = (e * (1.0 / jnp.sum(e, axis=1, keepdims=True))).astype(BF16)
-            c = dot(p, v_buf[b, 0:n, :])
-            ctx_ref[:, b] = c.reshape(DEVICES, MY_HEADS, HEAD_DIM).astype(BF16)
-
-        load(0, b).wait()
-        patch(k_buf, kn_buf)
-        load(1, b).wait()
-        patch(v_buf, vn_buf)
-
-        @pl.when(pos < 256)
-        def _():
-            attend(256)
-
-        @pl.when(jnp.logical_and(pos >= 256, pos < 1024))
-        def _():
-            attend(1024)
-
-        @pl.when(pos >= 1024)
-        def _():
-            attend(2048)
-
+    @pl.loop(0, MY_ROWS)
+    def _(b):
         save(0, b).start()
         save(1, b).start()
+
+    def attend(b, pos, n):
+        q = q_buf[b].astype(BF16)
+        k = k_buf[b, 0:n, :]
+        s = lax.dot_general(q, k, (((1,), (1,)), ((), ())), preferred_element_type=F32) * scale
+        t = lax.broadcasted_iota(jnp.int32, (NUM_HEADS, n), 1)
+        s = jnp.where(t <= pos, s, -jnp.inf)
+        e = jnp.exp(s - jnp.max(s, axis=1, keepdims=True))
+        p = (e * (1.0 / jnp.sum(e, axis=1, keepdims=True))).astype(BF16)
+        c = dot(p, v_buf[b, 0:n, :])
+        return c.reshape(DEVICES, MY_HEADS, HEAD_DIM).astype(BF16)
+
+    @pl.loop(0, MY_ROWS // TOGETHER)
+    def _(i):
+        rows = [i * TOGETHER + k for k in range(TOGETHER)]
+        pos = [len_ref[me * MY_ROWS + b] for b in rows]
+        longest = functools.reduce(jnp.maximum, pos)
+        low = 0
+        for n in SPANS:
+            @pl.when(jnp.logical_and(longest >= low, longest < n))
+            def _(n=n):
+                done = [attend(b, p, n) for b, p in zip(rows, pos)]
+                for b, c in zip(rows, done):
+                    ctx_ref[:, b] = c
+            low = n
 
     @pl.loop(0, MY_ROWS)
     def _(b):
@@ -237,31 +244,31 @@
         save(1, b).wait()
 
 
-def attend_call(layer, cache_len, q, kn, vn, k_cache, v_cache, prev):
+def attend_call(layer, cache_len, q, kn, vn, kv_pre, prev):
     any_spec = pl.BlockSpec(memory_space=pl.ANY)
     vmem_spec = pl.BlockSpec(memory_space=pltpu.VMEM)
-    return pl.pallas_call(
+    whole = jax.ShapeDtypeStruct((2,) + kv_pre.shape[1:], BF16)
+    k_all, v_all, ctx, _ = pl.pallas_call(
         functools.partial(attend_kernel, layer, bool(prev)),
         name="attend",
         out_shape=(
-            jax.ShapeDtypeStruct((DEVICES, MY_ROWS, MY_HEADS, HEAD_DIM), BF16),
-            jax.ShapeDtypeStruct(k_cache.shape, BF16),
-            jax.ShapeDtypeStruct(v_cache.shape, BF16),
+            whole,
+            whole,
+            pltpu.VMEM((DEVICES, MY_ROWS, MY_HEADS, HEAD_DIM), BF16),
+            pltpu.VMEM(kv_pre.shape, BF16),
         ),
-        in_specs=[pl.BlockSpec(memory_space=pltpu.SMEM)] + [vmem_spec] * 3 + [any_spec] * (2 + len(prev)),
-        out_specs=(vmem_spec, any_spec, any_spec),
+        in_specs=[pl.BlockSpec(memory_space=pltpu.SMEM)] + [vmem_spec] * 4 + [any_spec] * len(prev),
+        out_specs=(any_spec, any_spec, vmem_spec, vmem_spec),
         scratch_shapes=[
-            pltpu.VMEM((MY_ROWS, SEQ, HEAD_DIM), BF16),
-            pltpu.VMEM((MY_ROWS, SEQ, HEAD_DIM), BF16),
             pltpu.VMEM((MY_ROWS, NUM_HEADS, HEAD_DIM), F32),
             pltpu.VMEM((MY_ROWS, HEAD_DIM), F32),
             pltpu.VMEM((MY_ROWS, HEAD_DIM), F32),
             pltpu.SemaphoreType.DMA((2, MY_ROWS)),
-            pltpu.SemaphoreType.DMA((2, MY_ROWS)),
         ],
-        input_output_aliases={6: 1, 7: 2} if prev else {},
-        compiler_params=pltpu.CompilerParams(vmem_limit_bytes=VMEM_LIMIT),
-    )(cache_len, q, kn, vn, k_cache, v_cache, *prev)
+        input_output_aliases={4: 3} | ({5: 0, 6: 1} if prev else {}),
+        compiler_params=pltpu.CompilerParams(vmem_limit_bytes=16 * MIB),
+    )(cache_len, *in_vmem(q, kn, vn, kv_pre), *prev)
+    return ctx, k_all, v_all
 
 
 SELF, XN, YN, DIAG = range(4)
@@ -269,13 +276,13 @@
 
 def combine_kernel(layer, last, *refs):
     if last:
-        (ctx_in, res_hbm, wo_hbm, out_hbm,
-         ctx_buf, lhs, res_buf, wo_buf, send_d2d, recv_d2d, acc, rx_diag, ry_diag, rx_dir, ry_dir, rx_fwd, ry_fwd, h_buf,
+        (ctx_in, res_hbm, wo_hbm, out_ref,
+         ctx_buf, lhs, res_buf, w_buf, send_d2d, recv_d2d, acc, rx_diag, ry_diag, rx_dir, ry_dir, rx_fwd, ry_fwd, h_buf,
          load_sems, send_sems, recv_sems) = refs
     else:
-        (ctx_in, res_hbm, wo_hbm, wq_hbm, wk_hbm, wv_hbm, own_out, q_out, kn_out, vn_out,
-         ctx_buf, lhs, res_buf, wo_buf, send_d2d, recv_d2d, acc, rx_diag, ry_diag, rx_dir, ry_dir, rx_fwd, ry_fwd, h_buf,
-         wq_buf, wk_buf, wv_buf, q_acc, q_send,
+        (ctx_in, res_hbm, wo_hbm, wq_hbm, wk_hbm, wv_hbm, k_hbm, v_hbm, own_out, q_out, kn_out, vn_out, kv_pre,
+         ctx_buf, lhs, res_buf, w_buf, send_d2d, recv_d2d, acc, rx_diag, ry_diag, rx_dir, ry_dir, rx_fwd, ry_fwd, h_buf,
+         wk_buf, wv_buf, q_acc, q_send,
          load_sems, send_sems, recv_sems) = refs
     me, flip, xn, yn, diag = places()
     partner = me + flip
@@ -289,22 +296,31 @@
     top, bottom = pl.ds(0, HALF), pl.ds(HALF, HALF)
 
     own_load = loads.start(ctx_in.at[me], ctx_buf.at[me])
-    wo_loads = {}
+    wo_loads, wo_slot = {}, {}
     for g, r in steps:
         for c in (1, 0):
-            wo_loads[g, r, c] = loads.start(wo_hbm.at[layer, :, pl.ds(column(r, c, g), PIECE)], wo_buf.at[g, r, c])
+            slot = wo_slot[g, r, c] = len(wo_slot)
+            wo_loads[g, r, c] = loads.start(wo_hbm.at[layer, :, pl.ds(column(r, c, g), PIECE)], w_buf.at[slot])
     if last:
         res_load = loads.start(res_hbm, res_buf)
     else:
         res_load = loads.start(res_hbm.at[:, pl.ds(pl.multiple_of(me * MY_COLS, MY_COLS), MY_COLS)], res_buf)
-        wq_loads = {}
-        for r in (SELF, XN, YN, DIAG):
-            for c in (0, 1):
-                for g in range(GROUPS):
-                    wq_loads[r, c, g] = loads.start(
-                        wq_hbm.at[layer + 1, pl.ds(column(r, c, g), PIECE), :], wq_buf.at[r, c, g])
         wk_load = loads.start(wk_hbm.at[layer + 1], wk_buf)
         wv_load = loads.start(wv_hbm.at[layer + 1], wv_buf)
+    wq_order = [(r, c, g) for r in (SELF, XN, YN, DIAG) for c in (0, 1) for g in range(GROUPS)]
+    wq_loads, wq_slot = {}, {}
+
+    def refill(slot):
+        if last:
+            return
+        r, c, g = wq_order[len(wq_slot)]
+        wq_slot[r, c, g] = slot
+        rows = pl.ds(column(r, c, g), PIECE)
+        wq_loads[r, c, g] = [
+            loads.start(wq_hbm.at[layer + 1, rows, pl.ds(n * HALF_COLS, HALF_COLS)],
+                        w_buf.at[slot, pl.ds(n * PIECE, PIECE), :])
+            for n in range(MY_COLS // HALF_COLS)
+        ]
 
     meet_all(me)
 
@@ -335,19 +351,20 @@
 
     pending = None
     for g, r in steps:
-        wo_loads[g, r, 1].wait()
-        send_d2d[g, r] = dot(lhs[...], wo_buf[g, r, 1])
-        d2d[g, r] = copies.start(send_d2d.at[g, r], recv_d2d.at[g, r], partner)
-        wo_loads[g, r, 0].wait()
-        acc[g, r] = dot(lhs[...], wo_buf[g, r, 0])
+        for c, target in ((1, send_d2d), (0, acc)):
+            wo_loads[g, r, c].wait()
+            target[g, r] = dot(lhs[...], w_buf[wo_slot[g, r, c]])
+            refill(wo_slot[g, r, c])
+            if c == 1:
+                d2d[g, r] = copies.start(send_d2d.at[g, r], recv_d2d.at[g, r], partner)
         if pending is not None:
             settle(*pending)
             if pending == (0, YN):
                 send_direct(0)
         pending = (g, r)
     settle(*pending)
-    if GROUPS == 1:
-        pass
+    if not last:
+        cache_loads = load_cache(loads, layer + 1, k_hbm, v_hbm, kv_pre)
 
     for g in range(GROUPS):
         first[g, 0].wait_recv()
@@ -361,6 +378,7 @@
 
     res_load.wait()
     gather = {}
+    own_stores = []
 
     def finish_piece(g):
         cols = slice(g * PIECE, (g + 1) * PIECE)
@@ -377,22 +395,23 @@
         gather[YN, 0, g] = [copies.start(mine, h_buf.at[YN, 0, g], yn)]
         gather[SELF, 1, g] = [copies.start(mine, h_buf.at[SELF, 1, g], partner)]
         if not last:
-            own_out[:, cols] = h_buf[SELF, 0, g]
+            own_stores.append(loads.start(mine, own_out.at[:, pl.ds(g * PIECE, PIECE)]))
 
     def arrive(r, c, g):
         for copy in gather[r, c, g]:
             copy.wait_recv()
 
-    stores = []
     if last:
         def use(r, c, g):
-            stores.append(loads.start(h_buf.at[r, c, g], out_hbm.at[:, pl.ds(column(r, c, g), PIECE)]))
+            out_ref[:, pl.ds(column(r, c, g), PIECE)] = h_buf[r, c, g]
     else:
         q_acc[...] = jnp.zeros_like(q_acc)
 
         def use(r, c, g):
-            wq_loads[r, c, g].wait()
-            q_acc[...] += dot(h_buf[r, c, g], wq_buf[r, c, g])
+            for n, load in enumerate(wq_loads[r, c, g]):
+                load.wait()
+                w = w_buf[wq_slot[r, c, g], n * PIECE:(n + 1) * PIECE, :]
+                q_acc[:, n * HALF_COLS:(n + 1) * HALF_COLS] += dot(h_buf[r, c, g], w)
 
     for g in range(GROUPS):
         finish_piece(g)
@@ -423,10 +442,7 @@
         arrive(DIAG, 1, g)
         use(DIAG, 1, g)
 
-    if last:
-        for store in stores:
-            store.wait()
-    else:
+    if not last:
         arrivals = []
         for j in range(TILES):
             q_send[j] = q_acc[:, j * TILE:(j + 1) * TILE].astype(BF16).reshape(DEVICES, MY_ROWS, TILE)
@@ -448,6 +464,8 @@
         vn_out[...] = vn.astype(BF16)
         for copy in arrivals:
             copy.wait_recv()
+        for load in cache_loads + own_stores:
+            load.wait()
     copies.finish()
 
 
@@ -455,12 +473,12 @@
     any_spec = pl.BlockSpec(memory_space=pl.ANY)
     vmem_spec = pl.BlockSpec(memory_space=pltpu.VMEM)
     sends = (DEVICES - 1) + GROUPS * (4 + 6 + 9)
-    loads = 1 + 8 * GROUPS + 1 + 8 * GROUPS
+    loads = 1 + SLOTS + 1
     scratch = [
         pltpu.VMEM((DEVICES, MY_ROWS, MY_HEADS, HEAD_DIM), BF16),
         pltpu.VMEM((ROWS, MY_COLS), BF16),
         pltpu.VMEM((ROWS, MY_COLS), BF16),
-        pltpu.VMEM((GROUPS, 4, 2, MY_COLS, PIECE), BF16),
+        pltpu.VMEM((SLOTS, MY_COLS, PIECE), BF16),
         pltpu.VMEM((GROUPS, 4, ROWS, PIECE), F32),
         pltpu.VMEM((GROUPS, 4, ROWS, PIECE), F32),
         pltpu.VMEM((GROUPS, 4, ROWS, PIECE), F32),
@@ -468,20 +486,14 @@
         pltpu.VMEM((4, 2, GROUPS, ROWS, PIECE), BF16),
     ]
     if last:
-        out_shape = jax.ShapeDtypeStruct((ROWS, D_MODEL), BF16)
-        out_specs = any_spec
+        out_shape = pltpu.VMEM((ROWS, D_MODEL), BF16)
+        out_specs = vmem_spec
     else:
-        out_shape = (
-            jax.ShapeDtypeStruct((ROWS, MY_COLS), BF16),
-            jax.ShapeDtypeStruct((TILES, DEVICES, MY_ROWS, TILE), BF16),
-            jax.ShapeDtypeStruct((MY_ROWS, HEAD_DIM), BF16),
-            jax.ShapeDtypeStruct((MY_ROWS, HEAD_DIM), BF16),
-        )
-        out_specs = (vmem_spec,) * 4
+        out_shape = (jax.ShapeDtypeStruct((ROWS, MY_COLS), BF16),) + QUERY_SHAPES
+        out_specs = (any_spec,) + (vmem_spec,) * len(QUERY_SHAPES)
         sends += TILES * (DEVICES - 1)
-        loads += 2
+        loads += 4 + 2 * SLOTS + GROUPS
         scratch += [
-            pltpu.VMEM((4, 2, GROUPS, PIECE, MY_COLS), BF16),
             pltpu.VMEM((D_MODEL, HEAD_DIM), BF16),
             pltpu.VMEM((D_MODEL, HEAD_DIM), BF16),
             pltpu.VMEM((ROWS, MY_COLS), F32),
@@ -500,19 +512,20 @@
         out_specs=out_specs,
         scratch_shapes=scratch,
         compiler_params=pltpu.CompilerParams(
-            collective_id=2 if last else 1, has_side_effects=True, vmem_limit_bytes=VMEM_LIMIT
+            collective_id=2 if last else 1, has_side_effects=True, vmem_limit_bytes=40 * MIB
         ),
-    )(ctx, residual, w_out, *more)
+    )(*in_vmem(ctx), *in_hbm(residual, w_out, *more))
 
 
 def solution(mesh):
     cache_spec = P(None, ("replica", "model"), None, None)
 
     def device_step(x, cache_len, w_query, w_key, w_value, w_out, k_cache, v_cache):
-        q, kn, vn = query_call(x, w_query, w_key, w_value)
-        ctx, k_all, v_all = attend_call(0, cache_len, q, kn, vn, k_cache, v_cache, ())
-        own, q, kn, vn = combine_call(0, False, ctx, x, w_out, (w_query, w_key, w_value))
-        ctx, k_all, v_all = attend_call(1, cache_len, q, kn, vn, k_cache, v_cache, (k_all, v_all))
+        q, kn, vn, kv_pre = query_call(x, w_query, w_key, w_value, k_cache, v_cache)
+        ctx, k_all, v_all = attend_call(0, cache_len, q, kn, vn, kv_pre, ())
+        own, q, kn, vn, kv_pre = combine_call(
+            0, False, ctx, x, w_out, (w_query, w_key, w_value, k_cache, v_cache))
+        ctx, k_all, v_all = attend_call(1, cache_len, q, kn, vn, kv_pre, (k_all, v_all))
         out = combine_call(1, True, ctx, own, w_out, ())
         return out, k_all, v_all
 

time: 134 us -> 119 us (0.89)
  Pallas kernels: 129 us -> 117 us
  local copies, waits for them, and re-layouts: 3.1 us -> 1.33 us
    pallas_call x2, Pallas kernels: 28.4 us -> 18.9 us  [attend_call(): pl.pallas_call(functools.partial(attend_kernel, layer, bool(prev)), name=...]
    pallas_call x2, Pallas kernels: 85.8 us -> 83.9 us  [combine_call(): pl.pallas_call(functools.partial(combine_kernel, layer, last), name='comb...]
    unnamed x1 -> x3, local copies, waits for them, and re-layouts: 3.1 us -> 1.33 us
where the time goes in v2:
time: 119 us
  Pallas kernels  117 us (98%)
  local copies, waits for them, and re-layouts  1.33 us (1%)
    pallas_call x2, Pallas kernels, combine_call(): pl.pallas_call(functools.partial(combine_kernel, layer, last), name='comb...  83.9 us
    pallas_call x2, Pallas kernels, attend_call(): pl.pallas_call(functools.partial(attend_kernel, layer, bool(prev)), name=...  18.9 us
    pallas_call x1, Pallas kernels, query_call(): pl.pallas_call(query_kernel, name='query', out_shape=QUERY_SHAPES, in_spe...  14.4 us

profile of v2, /device:TPU:0, one launch (start us, length us, event | category | flops | bytes accessed | tf_op | source)
XLA Modules:
  0.0 119.2 jit_solution(5527427896350347080)
XLA Ops:
  0.6 0.0 copy-start
  0.6 14.4 %query.1 = (bf16[4,8,16,256]{3,2,1,0:T(8,128)(2,1)S(1)}, bf16[16,128]{1,0:T(8,128)(2,1)S(1)}, bf16[16,128]{1,0:T(8,128)(2,1)S(1)}, bf16[2,16,2048,128]{3,2,1,0:T(8,128)(2,1)S(1)}) custom-call(bf16[128,8192]{1,0:T(8,128)(2,1)} %refs_1_.1, bf16[2,8192,1024]{2,1,0:T(8,128)(2,1)} %refs_3_.1, bf16[2,8192,128]{2,1,0:T(8,128)(2,1)} %refs_4_.1, ...), custom_call_target="tpu_custom_call" | custom-call | tf_op jit(solution)/shard_map/query/pallas_call | solution.py:159
  15.0 0.0 copy-done
  15.0 9.5 %attend.2 = (bf16[2,16,2048,128]{3,2,1,0:T(8,128)(2,1)}, bf16[2,16,2048,128]{3,2,1,0:T(8,128)(2,1)}, bf16[8,16,8,128]{3,2,1,0:T(8,128)(2,1)S(1)}, bf16[2,16,2048,128]{3,2,1,0:T(8,128)(2,1)S(1)}) custom-call(s32[128]{0:T(128)S(1)} %copy-done, bf16[4,8,16,256]{3,2,1,0:T(8,128)(2,1)S(1)} %get-tuple-element.18.q_ref, ...), custom_call_target="tpu_custom_call", output_to_operand_aliasing={{3}: (4, {})} | custom-call | tf_op jit(solution)/shard_map/attend/pallas_call | solution.py:251
  24.6 45.5 %combine.1 = (bf16[128,1024]{1,0:T(8,128)(2,1)}, bf16[4,8,16,256]{3,2,1,0:T(8,128)(2,1)S(1)}, bf16[16,128]{1,0:T(8,128)(2,1)S(1)}, bf16[16,128]{1,0:T(8,128)(2,1)S(1)}, bf16[2,16,2048,128]{3,2,1,0:T(8,128)(2,1)S(1)}) custom-call(bf16[8,16,8,128]{3,2,1,0:T(8,128)(2,1)S(1)} %get-tuple-element.22.refs_0_, bf16[128,8192]{1,0:T(8,128)(2,1)} %refs_1_.1, ...), custom_call_target="tpu_custom_call" | custom-call | tf_op jit(solution)/shard_map/combine/pallas_call | solution.py:507
  70.1 9.4 %attend.3 = (bf16[2,16,2048,128]{3,2,1,0:T(8,128)(2,1)}, bf16[2,16,2048,128]{3,2,1,0:T(8,128)(2,1)}, bf16[8,16,8,128]{3,2,1,0:T(8,128)(2,1)S(1)}, bf16[2,16,2048,128]{3,2,1,0:T(8,128)(2,1)S(1)}) custom-call(s32[128]{0:T(128)S(1)} %copy-done, ...), custom_call_target="tpu_custom_call", output_to_operand_aliasing={{3}: (4, {}), {0}: (5, {}), {1}: (6, {})} | custom-call | tf_op jit(solution)/shard_map/attend/pallas_call | solution.py:251
  79.5 38.3 %combine_last.1 = bf16[128,8192]{1,0:T(8,128)(2,1)S(1)} custom-call(bf16[8,16,8,128]{3,2,1,0:T(8,128)(2,1)S(1)} %get-tuple-element.29.refs_0_, bf16[128,1024]{1,0:T(8,128)(2,1)} %get-tuple-element.30.refs_1_, bf16[2,1024,8192]{2,1,0:T(8,128)(2,1)} %refs_2_.3), custom_call_target="tpu_custom_call" | custom-call | tf_op jit(solution)/shard_map/combine_last/pallas_call | solution.py:507
  117.8 1.3 %copy.20 = bf16[128,8192]{1,0:T(8,128)(2,1)} copy(bf16[128,8192]{1,0:T(8,128)(2,1)S(1)} %combine_last.1) | data formatting | bytes 4194304
Async XLA Ops:
  0.6 14.4 %copy-start = (s32[128]{0:T(128)S(1)}, s32[128]{0:T(128)}, u32[]{:S(2)}) copy-start(s32[128]{0:T(128)} %len_ref.3) | copy-start | bytes 1540

commit v3 on v2

v3 whole, which is shorter than its diff:
```python
import functools

import jax
import jax.numpy as jnp
from jax import lax
from jax.experimental import pallas as pl
from jax.experimental.pallas import tpu as pltpu
from jax.sharding import PartitionSpec as P

MESH = pl.DeviceIdType.MESH
BF16 = jnp.bfloat16
F32 = jnp.float32
MIB = 1024 * 1024

DEVICES = 8
ROWS = 128
MY_ROWS = 16
D_MODEL = 8192
HEAD_DIM = 128
MY_HEADS = 8
NUM_HEADS = 64
MY_COLS = 1024
SEQ = 2048
TILE = 256
TILES = MY_COLS // TILE

HALF_COLS = 512
GROUPS = 2
PIECE = MY_COLS // GROUPS
HALF = ROWS // 2
SLOTS = 8 * GROUPS
TOGETHER = 8
SPANS = (256, 512, 1024, 2048)


def dot(a, b):
    return jnp.dot(a, b, preferred_element_type=F32)


def places():
    me = lax.axis_index("model")
    core = lax.rem(me, 2)
    x = lax.rem(lax.div(me, 2), 2)
    y = lax.div(me, 4)
    flip = 1 - 2 * core
    xn = me + 2 - 4 * x
    yn = me + 4 - 8 * y
    diag = xn + 4 - 8 * y
    return me, flip, xn, yn, diag


def await_all(ref, sem):
    pltpu.make_async_copy(ref, ref, sem).wait()


class Copies:
    def __init__(self, send_sems, recv_sems):
        self.send_sems, self.recv_sems, self.receives = send_sems, recv_sems, 0

    def new_receive(self):
        self.receives += 1
        return self.recv_sems.at[self.receives - 1]

    def start(self, src, dst, device, kind, recv_sem=None):
        copy = pltpu.make_async_remote_copy(
            src_ref=src,
            dst_ref=dst,
            send_sem=self.send_sems.at[kind],
            recv_sem=self.new_receive() if recv_sem is None else recv_sem,
            device_id={"model": device},
            device_id_type=MESH,
        )
        copy.start()
        return copy


def meet_all(me):
    barrier = pltpu.get_barrier_semaphore()
    for k in range(1, DEVICES):
        pl.semaphore_signal(barrier, inc=1, device_id={"model": lax.rem(me + k, DEVICES)}, device_id_type=MESH)
    pl.semaphore_wait(barrier, DEVICES - 1)


def send_query_tile(copies, me, j, q_send, q_out, kind, recv_sem):
    for k in range(1, DEVICES):
        to = lax.rem(me + k, DEVICES)
        copies.start(q_send.at[j, to], q_out.at[j, me], to, kind, recv_sem)
    q_out[j, me] = q_send[j, me]


def load_cache(layer, k_hbm, v_hbm, kv_pre, sem):
    for i, hbm in enumerate((k_hbm, v_hbm)):
        pltpu.make_async_copy(hbm.at[layer], kv_pre.at[i], sem).start()


def load_kv_weights(layer, wk_hbm, wv_hbm, wkv_buf, sem):
    for i, hbm in enumerate((wk_hbm, wv_hbm)):
        pltpu.make_async_copy(hbm.at[layer], wkv_buf.at[i], sem).start()


def in_vmem(*arrays):
    return [pltpu.with_memory_space_constraint(a, pltpu.VMEM) for a in arrays]


def in_hbm(*arrays):
    return [pltpu.with_memory_space_constraint(a, pltpu.HBM) for a in arrays]


QUERY_SHAPES = (
    pltpu.VMEM((TILES, DEVICES, MY_ROWS, TILE), BF16),
    pltpu.VMEM((MY_ROWS, HEAD_DIM), BF16),
    pltpu.VMEM((MY_ROWS, HEAD_DIM), BF16),
    pltpu.VMEM((2, MY_ROWS, SEQ, HEAD_DIM), BF16),
)


def query_kernel(x_hbm, wq_hbm, wk_hbm, wv_hbm, k_hbm, v_hbm, q_out, kn_out, vn_out, kv_pre,
                 x_buf, wq_buf, wkv_buf, q_send, load_sems, send_sems, recv_sems):
    me, _, _, _, _ = places()
    wkv_sem, cache_sem = load_sems.at[TILES + 1], load_sems.at[TILES + 2]
    x_load = pltpu.make_async_copy(x_hbm, x_buf, load_sems.at[TILES])
    x_load.start()
    wq_loads = [pltpu.make_async_copy(wq_hbm.at[0, :, pl.ds(j * TILE, TILE)], wq_buf.at[j], load_sems.at[j])
                for j in range(TILES)]
    for load in wq_loads:
        load.start()
    load_kv_weights(0, wk_hbm, wv_hbm, wkv_buf, wkv_sem)
    load_cache(0, k_hbm, v_hbm, kv_pre, cache_sem)
    meet_all(me)
    copies = Copies(send_sems, recv_sems)
    q_sem = copies.new_receive()
    x_load.wait()
    for j in range(TILES):
        wq_loads[j].wait()
        q_send[j] = dot(x_buf[...], wq_buf[j]).astype(BF16).reshape(DEVICES, MY_ROWS, TILE)
        send_query_tile(copies, me, j, q_send, q_out, 0, q_sem)
    x_rows = x_buf[pl.ds(pl.multiple_of(me * MY_ROWS, MY_ROWS), MY_ROWS), :]
    await_all(wkv_buf, wkv_sem)
    kn_out[...] = dot(x_rows, wkv_buf[0]).astype(BF16)
    vn_out[...] = dot(x_rows, wkv_buf[1]).astype(BF16)
    others = pl.ds(0, DEVICES - 1)
    await_all(q_out.at[:, others], q_sem)
    await_all(q_send.at[:, others], send_sems.at[0])
    await_all(kv_pre, cache_sem)


def query_call(x, w_query, w_key, w_value, k_cache, v_cache):
    any_spec = pl.BlockSpec(memory_space=pl.ANY)
    vmem_spec = pl.BlockSpec(memory_space=pltpu.VMEM)
    return pl.pallas_call(
        query_kernel,
        name="query",
        out_shape=QUERY_SHAPES,
        in_specs=[any_spec] * 6,
        out_specs=(vmem_spec,) * len(QUERY_SHAPES),
        scratch_shapes=[
            pltpu.VMEM((ROWS, D_MODEL), BF16),
            pltpu.VMEM((TILES, D_MODEL, TILE), BF16),
            pltpu.VMEM((2, D_MODEL, HEAD_DIM), BF16),
            pltpu.VMEM((TILES, DEVICES, MY_ROWS, TILE), BF16),
            pltpu.SemaphoreType.DMA((TILES + 3,)),
            pltpu.SemaphoreType.DMA((1,)),
            pltpu.SemaphoreType.DMA((1,)),
        ],
        compiler_params=pltpu.CompilerParams(
            collective_id=0, has_side_effects=True, vmem_limit_bytes=26 * MIB
        ),
    )(*in_hbm(x, w_query, w_key, w_value, k_cache, v_cache))


def attend_kernel(layer, has_prev, len_ref, q_ref, kn_ref, vn_ref, *refs):
    k_out, v_out, ctx_ref, kv_buf, q_buf, kn_buf, vn_buf, out_sems = refs[-8:]
    k_buf, v_buf = kv_buf.at[0], kv_buf.at[1]
    me = lax.axis_index("model")

    def save(which, b):
        hbm, buf = ((k_out, k_buf), (v_out, v_buf))[which]
        return pltpu.make_async_copy(buf.at[b], hbm.at[layer, b], out_sems.at[which])

    kn_buf[...] = kn_ref[...].astype(F32)
    vn_buf[...] = vn_ref[...].astype(F32)

    @pl.loop(0, MY_ROWS)
    def _(b):
        pos = len_ref[me * MY_ROWS + b]
        base = pl.multiple_of((pos // 16) * 16, 16)
        here = lax.broadcasted_iota(jnp.int32, (16, HEAD_DIM), 0) == pos - base
        for buf, new in ((k_buf, kn_buf), (v_buf, vn_buf)):
            tile = buf[b, pl.ds(base, 16), :].astype(F32)
            row = jnp.broadcast_to(new[pl.ds(b, 1), :], (16, HEAD_DIM))
            buf[b, pl.ds(base, 16), :] = jnp.where(here, row, tile).astype(BF16)

        @pl.when(b >= 1)
        def _():
            save(0, b - 1).start()
            save(1, b - 1).start()

    save(0, MY_ROWS - 1).start()
    save(1, MY_ROWS - 1).start()

    for j in range(TILES):
        for src in range(DEVICES):
            block = q_ref[j, src].astype(F32)
            for h in range(TILE // HEAD_DIM):
                head = src * MY_HEADS + j * (TILE // HEAD_DIM) + h
                q_buf[:, head, :] = block[:, h * HEAD_DIM:(h + 1) * HEAD_DIM]

    scale = HEAD_DIM ** -0.5

    def attend(rows, n):
        t = lax.broadcasted_iota(jnp.int32, (NUM_HEADS, n), 1)
        s = [lax.dot_general(q_buf[b].astype(BF16), k_buf[b, 0:n, :], (((1,), (1,)), ((), ())),
                             preferred_element_type=F32) for b in rows]
        s = [jnp.where(t <= len_ref[me * MY_ROWS + b], v * scale, -jnp.inf) for v, b in zip(s, rows)]
        peak = [jnp.max(v, axis=1, keepdims=True) for v in s]
        e = [jnp.exp(v - u) for v, u in zip(s, peak)]
        share = [1.0 / jnp.sum(v, axis=1, keepdims=True) for v in e]
        p = [(v * u).astype(BF16) for v, u in zip(e, share)]
        c = [dot(v, v_buf[b, 0:n, :]) for v, b in zip(p, rows)]
        for v, b in zip(c, rows):
            ctx_ref[:, b] = v.reshape(DEVICES, MY_HEADS, HEAD_DIM).astype(BF16)

    @pl.loop(0, MY_ROWS // TOGETHER)
    def _(i):
        attend([i * TOGETHER + k for k in range(TOGETHER)], SPANS[0])

    @pl.loop(0, MY_ROWS)
    def _(b):
        pos = len_ref[me * MY_ROWS + b]
        for low, n in zip(SPANS, SPANS[1:]):
            @pl.when(jnp.logical_and(pos >= low, pos < n))
            def _(n=n):
                attend([b], n)

    for which, hbm in enumerate((k_out, v_out)):
        await_all(hbm.at[layer], out_sems.at[which])


def attend_call(layer, cache_len, q, kn, vn, kv_pre, prev):
    any_spec = pl.BlockSpec(memory_space=pl.ANY)
    vmem_spec = pl.BlockSpec(memory_space=pltpu.VMEM)
    whole = jax.ShapeDtypeStruct((2,) + kv_pre.shape[1:], BF16)
    k_all, v_all, ctx, _ = pl.pallas_call(
        functools.partial(attend_kernel, layer, bool(prev)),
        name="attend",
        out_shape=(
            whole,
            whole,
            pltpu.VMEM((DEVICES, MY_ROWS, MY_HEADS, HEAD_DIM), BF16),
            pltpu.VMEM(kv_pre.shape, BF16),
        ),
        in_specs=[pl.BlockSpec(memory_space=pltpu.SMEM)] + [vmem_spec] * 4 + [any_spec] * len(prev),
        out_specs=(any_spec, any_spec, vmem_spec, vmem_spec),
        scratch_shapes=[
            pltpu.VMEM((MY_ROWS, NUM_HEADS, HEAD_DIM), F32),
            pltpu.VMEM((MY_ROWS, HEAD_DIM), F32),
            pltpu.VMEM((MY_ROWS, HEAD_DIM), F32),
            pltpu.SemaphoreType.DMA((2,)),
        ],
        input_output_aliases={4: 3} | ({5: 0, 6: 1} if prev else {}),
        compiler_params=pltpu.CompilerParams(vmem_limit_bytes=16 * MIB),
    )(cache_len, *in_vmem(q, kn, vn, kv_pre), *prev)
    return ctx, k_all, v_all


SELF, XN, YN, DIAG = range(4)
CONTEXT, CORE, SUMS, WHOLE, HALVES, QUERY = range(6)


def combine_kernel(layer, last, *refs):
    if last:
        (ctx_in, res_buf, wo_hbm, out_ref,
         ctx_buf, lhs, w_buf, send_d2d, recv_d2d, acc, rx_diag, ry_diag, rx_dir, ry_dir, rx_fwd, ry_fwd, h_buf,
         load_sems, send_sems, recv_sems) = refs
    else:
        (ctx_in, res_hbm, wo_hbm, wq_hbm, wk_hbm, wv_hbm, k_hbm, v_hbm, own_out, q_out, kn_out, vn_out, kv_pre,
         ctx_buf, lhs, res_buf, w_buf, send_d2d, recv_d2d, acc, rx_diag, ry_diag, rx_dir, ry_dir, rx_fwd, ry_fwd, h_buf,
         wkv_buf, q_acc, q_send,
         load_sems, send_sems, recv_sems) = refs
    me, flip, xn, yn, diag = places()
    partner = me + flip
    chip_mate = {SELF: me, XN: xn, YN: yn, DIAG: diag}
    owner = lambda r, c: chip_mate[r] + c * flip
    column = lambda r, c, g: pl.multiple_of(owner(r, c) * MY_COLS + g * PIECE, PIECE)
    copies = Copies(send_sems, recv_sems)
    order = (DIAG, XN, YN, SELF)
    steps = [(g, r) for g in range(GROUPS) for r in order]
    top, bottom = pl.ds(0, HALF), pl.ds(HALF, HALF)

    wo_slot, wo_loads = {}, []
    for g, r in steps:
        for c in (1, 0):
            slot = wo_slot[g, r, c] = len(wo_slot)
            wo_loads.append(pltpu.make_async_copy(
                wo_hbm.at[layer, :, pl.ds(column(r, c, g), PIECE)], w_buf.at[slot], load_sems.at[slot]))
            wo_loads[-1].start()
    if not last:
        res_sem, wkv_sem, cache_sem = [load_sems.at[SLOTS + i] for i in range(3)]
        res_load = pltpu.make_async_copy(
            res_hbm.at[:, pl.ds(pl.multiple_of(me * MY_COLS, MY_COLS), MY_COLS)], res_buf, res_sem)
        res_load.start()
        load_kv_weights(layer + 1, wk_hbm, wv_hbm, wkv_buf, wkv_sem)
    wq_order = [(r, c, g) for r in (SELF, XN, YN, DIAG) for c in (0, 1) for g in range(GROUPS)]
    wq_slot = {}

    def refill(slot):
        if last:
            return
        r, c, g = wq_order[len(wq_slot)]
        wq_slot[r, c, g] = slot
        rows = pl.ds(column(r, c, g), PIECE)
        for n in range(MY_COLS // HALF_COLS):
            pltpu.make_async_copy(
                wq_hbm.at[layer + 1, rows, pl.ds(n * HALF_COLS, HALF_COLS)],
                w_buf.at[slot, pl.ds(n * PIECE, PIECE), :], load_sems.at[slot]).start()

    meet_all(me)

    ctx_sem = copies.new_receive()
    for k in range(1, DEVICES):
        to = lax.rem(me + k, DEVICES)
        copies.start(ctx_in.at[to], ctx_buf.at[me], to, CONTEXT, ctx_sem)
    ctx_buf[me] = ctx_in[me]
    await_all(ctx_buf.at[pl.ds(0, DEVICES - 1)], ctx_sem)
    for src in range(DEVICES):
        rows = ctx_buf[src].astype(F32).reshape(MY_ROWS, MY_COLS).astype(BF16)
        lhs[src * MY_ROWS:(src + 1) * MY_ROWS, :] = rows

    d2d = {}
    first, direct, forward = {}, {}, {}

    def settle(g, r):
        d2d[g, r].wait_recv()
        acc[g, r] += recv_d2d[g, r]
        if r == DIAG:
            first[g, 0] = copies.start(acc.at[g, r, top], rx_diag.at[g], xn, SUMS)
            first[g, 1] = copies.start(acc.at[g, r, bottom], ry_diag.at[g], yn, SUMS)

    def send_direct(g):
        direct[g, 0] = copies.start(acc.at[g, XN, top], rx_dir.at[g], xn, SUMS)
        direct[g, 1] = copies.start(acc.at[g, YN, bottom], ry_dir.at[g], yn, SUMS)

    pending = None
    for g, r in steps:
        for c, target in ((1, send_d2d), (0, acc)):
            wo_loads[wo_slot[g, r, c]].wait()
            target[g, r] = dot(lhs[...], w_buf[wo_slot[g, r, c]])
            refill(wo_slot[g, r, c])
            if c == 1:
                d2d[g, r] = copies.start(send_d2d.at[g, r], recv_d2d.at[g, r], partner, CORE)
        if pending is not None:
            settle(*pending)
            if pending == (0, YN):
                send_direct(0)
        pending = (g, r)
    settle(*pending)
    if not last:
        load_cache(layer + 1, k_hbm, v_hbm, kv_pre, cache_sem)

    for g in range(GROUPS):
        first[g, 0].wait_recv()
        acc[g, YN, top] += rx_diag[g]
        forward[g, 1] = copies.start(acc.at[g, YN, top], ry_fwd.at[g], yn, SUMS)
        first[g, 1].wait_recv()
        acc[g, XN, bottom] += ry_diag[g]
        forward[g, 0] = copies.start(acc.at[g, XN, bottom], rx_fwd.at[g], xn, SUMS)
        if g + 1 < GROUPS:
            send_direct(g + 1)

    if not last:
        res_load.wait()
    gather = {}

    def finish_piece(g):
        cols = slice(g * PIECE, (g + 1) * PIECE)
        direct[g, 0].wait_recv()
        forward[g, 1].wait_recv()
        total = acc[g, SELF, top] + rx_dir[g] + ry_fwd[g]
        h_buf[SELF, 0, g, top] = (res_buf[top, cols].astype(F32) + total).astype(BF16)
        direct[g, 1].wait_recv()
        forward[g, 0].wait_recv()
        total = acc[g, SELF, bottom] + ry_dir[g] + rx_fwd[g]
        h_buf[SELF, 0, g, bottom] = (res_buf[bottom, cols].astype(F32) + total).astype(BF16)
        mine = h_buf.at[SELF, 0, g]
        gather[XN, 0, g] = copies.start(mine, h_buf.at[XN, 0, g], xn, WHOLE)
        gather[YN, 0, g] = copies.start(mine, h_buf.at[YN, 0, g], yn, WHOLE)
        gather[SELF, 1, g] = copies.start(mine, h_buf.at[SELF, 1, g], partner, WHOLE)
        if not last:
            own_out[:, cols] = h_buf[SELF, 0, g]

    def arrive(r, c, g):
        gather[r, c, g].wait_recv()

    if last:
        def use(r, c, g):
            out_ref[:, pl.ds(column(r, c, g), PIECE)] = h_buf[r, c, g]
    else:
        q_acc[...] = jnp.zeros_like(q_acc)

        def use(r, c, g):
            slot = wq_slot[r, c, g]
            await_all(w_buf.at[slot], load_sems.at[slot])
            for n in range(MY_COLS // HALF_COLS):
                w = w_buf[slot, n * PIECE:(n + 1) * PIECE, :]
                q_acc[:, n * HALF_COLS:(n + 1) * HALF_COLS] += dot(h_buf[r, c, g], w)

    for g in range(GROUPS):
        finish_piece(g)
    for g in range(GROUPS):
        use(SELF, 0, g)
    for g in range(GROUPS):
        arrive(SELF, 1, g)
        use(SELF, 1, g)
    diag_sems = {}
    for g in range(GROUPS):
        diag_sem = diag_sems[g] = copies.new_receive()
        arrive(XN, 0, g)
        copies.start(h_buf.at[XN, 0, g, top], h_buf.at[DIAG, 0, g, top], yn, HALVES, diag_sem)
        gather[XN, 1, g] = copies.start(h_buf.at[XN, 0, g], h_buf.at[XN, 1, g], partner, WHOLE)
        arrive(YN, 0, g)
        copies.start(h_buf.at[YN, 0, g, bottom], h_buf.at[DIAG, 0, g, bottom], xn, HALVES, diag_sem)
        gather[YN, 1, g] = copies.start(h_buf.at[YN, 0, g], h_buf.at[YN, 1, g], partner, WHOLE)
        use(XN, 0, g)
        use(YN, 0, g)
        arrive(XN, 1, g)
        use(XN, 1, g)
        arrive(YN, 1, g)
        use(YN, 1, g)
    for g in range(GROUPS):
        await_all(h_buf.at[DIAG, 0, g], diag_sems[g])
        gather[DIAG, 1, g] = copies.start(h_buf.at[DIAG, 0, g], h_buf.at[DIAG, 1, g], partner, WHOLE)
        use(DIAG, 0, g)
    for g in range(GROUPS):
        arrive(DIAG, 1, g)
        use(DIAG, 1, g)

    if not last:
        q_sem = copies.new_receive()
        for j in range(TILES):
            q_send[j] = q_acc[:, j * TILE:(j + 1) * TILE].astype(BF16).reshape(DEVICES, MY_ROWS, TILE)
            send_query_tile(copies, me, j, q_send, q_out, QUERY, q_sem)
        await_all(wkv_buf, wkv_sem)
        mine = pl.ds(pl.multiple_of(me * MY_ROWS, MY_ROWS), MY_ROWS)
        kn = jnp.zeros((MY_ROWS, HEAD_DIM), F32)
        vn = jnp.zeros((MY_ROWS, HEAD_DIM), F32)
        for r in (SELF, XN, YN, DIAG):
            for c in (0, 1):
                for g in range(GROUPS):
                    rows = h_buf[r, c, g, mine, :]
                    depth = pl.ds(column(r, c, g), PIECE)
                    kn += dot(rows, wkv_buf[0, depth, :])
                    vn += dot(rows, wkv_buf[1, depth, :])
        kn_out[...] = kn.astype(BF16)
        vn_out[...] = vn.astype(BF16)
        others = pl.ds(0, DEVICES - 1)
        await_all(q_out.at[:, others], q_sem)
        await_all(q_send.at[:, others], send_sems.at[QUERY])
        await_all(kv_pre, cache_sem)
    await_all(ctx_in.at[pl.ds(0, DEVICES - 1)], send_sems.at[CONTEXT])
    await_all(send_d2d, send_sems.at[CORE])
    await_all(acc.at[:, pl.ds(0, 3)], send_sems.at[SUMS])
    await_all(h_buf.at[pl.ds(0, 3)], send_sems.at[WHOLE])
    await_all(h_buf.at[0, 0], send_sems.at[HALVES])


def combine_call(layer, last, ctx, residual, w_out, more):
    any_spec = pl.BlockSpec(memory_space=pl.ANY)
    vmem_spec = pl.BlockSpec(memory_space=pltpu.VMEM)
    receives = (1 if last else 2) + GROUPS * (4 + 6 + 7)
    scratch = [
        pltpu.VMEM((DEVICES, MY_ROWS, MY_HEADS, HEAD_DIM), BF16),
        pltpu.VMEM((ROWS, MY_COLS), BF16),
        pltpu.VMEM((SLOTS, MY_COLS, PIECE), BF16),
        pltpu.VMEM((GROUPS, 4, ROWS, PIECE), F32),
        pltpu.VMEM((GROUPS, 4, ROWS, PIECE), F32),
        pltpu.VMEM((GROUPS, 4, ROWS, PIECE), F32),
    ] + [pltpu.VMEM((GROUPS, HALF, PIECE), F32)] * 6 + [
        pltpu.VMEM((4, 2, GROUPS, ROWS, PIECE), BF16),
    ]
    if last:
        out_shape = pltpu.VMEM((ROWS, D_MODEL), BF16)
        out_specs = vmem_spec
    else:
        out_shape = (pltpu.VMEM((ROWS, MY_COLS), BF16),) + QUERY_SHAPES
        out_specs = (vmem_spec,) * len(out_shape)
        scratch.insert(2, pltpu.VMEM((ROWS, MY_COLS), BF16))
        scratch += [
            pltpu.VMEM((2, D_MODEL, HEAD_DIM), BF16),
            pltpu.VMEM((ROWS, MY_COLS), F32),
            pltpu.VMEM((TILES, DEVICES, MY_ROWS, TILE), BF16),
        ]
    scratch += [
        pltpu.SemaphoreType.DMA((SLOTS + (0 if last else 3),)),
        pltpu.SemaphoreType.DMA((5 if last else 6,)),
        pltpu.SemaphoreType.DMA((receives,)),
    ]
    return pl.pallas_call(
        functools.partial(combine_kernel, layer, last),
        name="combine_last" if last else "combine",
        out_shape=out_shape,
        in_specs=[vmem_spec, vmem_spec if last else any_spec] + [any_spec] * (1 + len(more)),
        out_specs=out_specs,
        scratch_shapes=scratch,
        compiler_params=pltpu.CompilerParams(
            collective_id=2 if last else 1, has_side_effects=True, vmem_limit_bytes=40 * MIB
        ),
    )(*in_vmem(ctx), *(in_vmem if last else in_hbm)(residual), *in_hbm(w_out, *more))


def solution(mesh):
    cache_spec = P(None, ("replica", "model"), None, None)

    def device_step(x, cache_len, w_query, w_key, w_value, w_out, k_cache, v_cache):
        q, kn, vn, kv_pre = query_call(x, w_query, w_key, w_value, k_cache, v_cache)
        ctx, k_all, v_all = attend_call(0, cache_len, q, kn, vn, kv_pre, ())
        own, q, kn, vn, kv_pre = combine_call(
            0, False, ctx, x, w_out, (w_query, w_key, w_value, k_cache, v_cache))
        ctx, k_all, v_all = attend_call(1, cache_len, q, kn, vn, kv_pre, (k_all, v_all))
        out = combine_call(1, True, ctx, own, w_out, ())
        return out, k_all, v_all

    return jax.shard_map(
        device_step,
        mesh=mesh,
        in_specs=(P("replica", None), P("replica"), P(None, None, "model"), P(), P(), P(None, "model", None), cache_spec, cache_spec),
        out_specs=(P("replica", None), cache_spec, cache_spec),
        check_vma=False,
    )
```

time: 119 us -> 112 us (0.941)
  Pallas kernels: 117 us -> 110 us
    pallas_call x2, Pallas kernels: 18.9 us -> 13 us  [attend_call(): pl.pallas_call(functools.partial(attend_kernel, layer, bool(prev)), name=...]
where the time goes in v3:
time: 112 us
  Pallas kernels  110 us (98%)
  local copies, waits for them, and re-layouts  1.33 us (1%)
    pallas_call x2, Pallas kernels, combine_call(): pl.pallas_call(functools.partial(combine_kernel, layer, last), name='comb...  82.9 us
    pallas_call x1, Pallas kernels, query_call(): pl.pallas_call(query_kernel, name='query', out_shape=QUERY_SHAPES, in_spe...  13.8 us
    pallas_call x2, Pallas kernels, attend_call(): pl.pallas_call(functools.partial(attend_kernel, layer, bool(prev)), name=...  13 us

profile of v3, /device:TPU:0, one launch (start us, length us, event | category | flops | bytes accessed | tf_op | source)
XLA Modules:
  0.0 111.7 jit_solution(4786473049189361973)
XLA Ops:
  0.6 0.0 copy-start
  0.6 13.8 %query.1 = (bf16[4,8,16,256]{3,2,1,0:T(8,128)(2,1)S(1)}, bf16[16,128]{1,0:T(8,128)(2,1)S(1)}, bf16[16,128]{1,0:T(8,128)(2,1)S(1)}, bf16[2,16,2048,128]{3,2,1,0:T(8,128)(2,1)S(1)}) custom-call(bf16[128,8192]{1,0:T(8,128)(2,1)} %refs_1_.1, bf16[2,8192,1024]{2,1,0:T(8,128)(2,1)} %refs_3_.1, bf16[2,8192,128]{2,1,0:T(8,128)(2,1)} %refs_4_.1, ...), custom_call_target="tpu_custom_call" | custom-call | tf_op jit(solution)/shard_map/query/pallas_call | solution.py:150
  14.5 0.0 copy-done
  14.5 6.6 %attend.2 = (bf16[2,16,2048,128]{3,2,1,0:T(8,128)(2,1)}, bf16[2,16,2048,128]{3,2,1,0:T(8,128)(2,1)}, bf16[8,16,8,128]{3,2,1,0:T(8,128)(2,1)S(1)}, bf16[2,16,2048,128]{3,2,1,0:T(8,128)(2,1)S(1)}) custom-call(s32[128]{0:T(128)S(1)} %copy-done, bf16[4,8,16,256]{3,2,1,0:T(8,128)(2,1)S(1)} %get-tuple-element.18.q_ref, ...), custom_call_target="tpu_custom_call", output_to_operand_aliasing={{3}: (4, {})} | custom-call | tf_op jit(solution)/shard_map/attend/pallas_call | solution.py:243
  21.1 44.8 %combine.1 = (bf16[128,1024]{1,0:T(8,128)(2,1)S(1)}, bf16[4,8,16,256]{3,2,1,0:T(8,128)(2,1)S(1)}, bf16[16,128]{1,0:T(8,128)(2,1)S(1)}, bf16[16,128]{1,0:T(8,128)(2,1)S(1)}, bf16[2,16,2048,128]{3,2,1,0:T(8,128)(2,1)S(1)}) custom-call(bf16[8,16,8,128]{3,2,1,0:T(8,128)(2,1)S(1)} %get-tuple-element.22.refs_0_, bf16[128,8192]{1,0:T(8,128)(2,1)} %refs_1_.1, ...), custom_call_target="tpu_custom_call" | custom-call | tf_op jit(solution)/shard_map/combine/pallas_call | solution.py:497
  65.8 6.4 %attend.3 = (bf16[2,16,2048,128]{3,2,1,0:T(8,128)(2,1)}, bf16[2,16,2048,128]{3,2,1,0:T(8,128)(2,1)}, bf16[8,16,8,128]{3,2,1,0:T(8,128)(2,1)S(1)}, bf16[2,16,2048,128]{3,2,1,0:T(8,128)(2,1)S(1)}) custom-call(s32[128]{0:T(128)S(1)} %copy-done, ...), custom_call_target="tpu_custom_call", output_to_operand_aliasing={{3}: (4, {}), {0}: (5, {}), {1}: (6, {})} | custom-call | tf_op jit(solution)/shard_map/attend/pallas_call | solution.py:243
  72.2 38.1 %combine_last.1 = bf16[128,8192]{1,0:T(8,128)(2,1)S(1)} custom-call(bf16[8,16,8,128]{3,2,1,0:T(8,128)(2,1)S(1)} %get-tuple-element.29.refs_0_, bf16[128,1024]{1,0:T(8,128)(2,1)S(1)} %get-tuple-element.30.refs_1_, bf16[2,1024,8192]{2,1,0:T(8,128)(2,1)} %refs_2_.3), custom_call_target="tpu_custom_call" | custom-call | tf_op jit(solution)/shard_map/combine_last/pallas_call | solution.py:497
  110.4 1.3 %copy.20 = bf16[128,8192]{1,0:T(8,128)(2,1)} copy(bf16[128,8192]{1,0:T(8,128)(2,1)S(1)} %combine_last.1) | data formatting | bytes 4194304
Async XLA Ops:
  0.6 13.8 %copy-start = (s32[128]{0:T(128)S(1)}, s32[128]{0:T(128)}, u32[]{:S(2)}) copy-start(s32[128]{0:T(128)} %len_ref.3) | copy-start | bytes 1540

commit v4 on v3

--- a/solution.py
+++ b/solution.py
@@ -29,6 +29,7 @@
 PIECE = MY_COLS // GROUPS
 HALF = ROWS // 2
 SLOTS = 8 * GROUPS
+LATE_ROWS = 4
 TOGETHER = 8
 SPANS = (256, 512, 1024, 2048)
 
@@ -81,21 +82,34 @@
     pl.semaphore_wait(barrier, DEVICES - 1)
 
 
+def others():
+    me, flip, xn, yn, diag = places()
+    return [diag, diag + flip, xn, yn, xn + flip, yn + flip, me + flip]
+
+
 def send_query_tile(copies, me, j, q_send, q_out, kind, recv_sem):
-    for k in range(1, DEVICES):
-        to = lax.rem(me + k, DEVICES)
+    for to in others():
         copies.start(q_send.at[j, to], q_out.at[j, me], to, kind, recv_sem)
     q_out[j, me] = q_send[j, me]
 
 
-def load_cache(layer, k_hbm, v_hbm, kv_pre, sem):
+def load_cache(layer, rows, k_hbm, v_hbm, kv, sem):
     for i, hbm in enumerate((k_hbm, v_hbm)):
-        pltpu.make_async_copy(hbm.at[layer], kv_pre.at[i], sem).start()
-
-
-def load_kv_weights(layer, wk_hbm, wv_hbm, wkv_buf, sem):
+        pltpu.make_async_copy(hbm.at[layer, rows], kv.at[i, rows], sem).start()
+
+
+def load_kv_weights(layer, core, wk_hbm, wv_hbm, wkv_buf, sem):
     for i, hbm in enumerate((wk_hbm, wv_hbm)):
-        pltpu.make_async_copy(hbm.at[layer], wkv_buf.at[i], sem).start()
+        @pl.when(core == i)
+        def _():
+            pltpu.make_async_copy(hbm.at[layer], wkv_buf, sem).start()
+
+
+def share_new_rows(copies, core, partner, made, kv_send, kv_out, kind):
+    kv_send[...] = made.reshape(2, MY_ROWS, HEAD_DIM).astype(BF16)
+    copy = copies.start(kv_send.at[1 - core], kv_out.at[core], partner, kind)
+    kv_out[core] = kv_send[core]
+    return copy
 
 
 def in_vmem(*arrays):
@@ -108,15 +122,15 @@
 
 QUERY_SHAPES = (
     pltpu.VMEM((TILES, DEVICES, MY_ROWS, TILE), BF16),
-    pltpu.VMEM((MY_ROWS, HEAD_DIM), BF16),
-    pltpu.VMEM((MY_ROWS, HEAD_DIM), BF16),
+    pltpu.VMEM((2, MY_ROWS, HEAD_DIM), BF16),
     pltpu.VMEM((2, MY_ROWS, SEQ, HEAD_DIM), BF16),
 )
 
 
-def query_kernel(x_hbm, wq_hbm, wk_hbm, wv_hbm, k_hbm, v_hbm, q_out, kn_out, vn_out, kv_pre,
-                 x_buf, wq_buf, wkv_buf, q_send, load_sems, send_sems, recv_sems):
-    me, _, _, _, _ = places()
+def query_kernel(x_hbm, wq_hbm, wk_hbm, wv_hbm, k_hbm, v_hbm, q_out, kv_out, kv_pre,
+                 x_buf, wq_buf, wkv_buf, q_send, kv_send, load_sems, send_sems, recv_sems):
+    me, flip, _, _, _ = places()
+    core = lax.rem(me, 2)
     wkv_sem, cache_sem = load_sems.at[TILES + 1], load_sems.at[TILES + 2]
     x_load = pltpu.make_async_copy(x_hbm, x_buf, load_sems.at[TILES])
     x_load.start()
@@ -124,8 +138,9 @@
                 for j in range(TILES)]
     for load in wq_loads:
         load.start()
-    load_kv_weights(0, wk_hbm, wv_hbm, wkv_buf, wkv_sem)
-    load_cache(0, k_hbm, v_hbm, kv_pre, cache_sem)
+    load_kv_weights(0, core, wk_hbm, wv_hbm, wkv_buf, wkv_sem)
+    early = pl.ds(0, MY_ROWS - LATE_ROWS)
+    load_cache(0, early, k_hbm, v_hbm, kv_pre, cache_sem)
     meet_all(me)
     copies = Copies(send_sems, recv_sems)
     q_sem = copies.new_receive()
@@ -134,14 +149,14 @@
         wq_loads[j].wait()
         q_send[j] = dot(x_buf[...], wq_buf[j]).astype(BF16).reshape(DEVICES, MY_ROWS, TILE)
         send_query_tile(copies, me, j, q_send, q_out, 0, q_sem)
-    x_rows = x_buf[pl.ds(pl.multiple_of(me * MY_ROWS, MY_ROWS), MY_ROWS), :]
+    chip_rows = pl.ds(pl.multiple_of((me - core) * MY_ROWS, 2 * MY_ROWS), 2 * MY_ROWS)
     await_all(wkv_buf, wkv_sem)
-    kn_out[...] = dot(x_rows, wkv_buf[0]).astype(BF16)
-    vn_out[...] = dot(x_rows, wkv_buf[1]).astype(BF16)
-    others = pl.ds(0, DEVICES - 1)
-    await_all(q_out.at[:, others], q_sem)
-    await_all(q_send.at[:, others], send_sems.at[0])
-    await_all(kv_pre, cache_sem)
+    shared = share_new_rows(copies, core, me + flip, dot(x_buf[chip_rows, :], wkv_buf[...]), kv_send, kv_out, 1)
+    seven = pl.ds(0, DEVICES - 1)
+    await_all(q_out.at[:, seven], q_sem)
+    shared.wait()
+    await_all(q_send.at[:, seven], send_sems.at[0])
+    await_all(kv_pre.at[:, early], cache_sem)
 
 
 def query_call(x, w_query, w_key, w_value, k_cache, v_cache):
@@ -156,11 +171,12 @@
         scratch_shapes=[
             pltpu.VMEM((ROWS, D_MODEL), BF16),
             pltpu.VMEM((TILES, D_MODEL, TILE), BF16),
-            pltpu.VMEM((2, D_MODEL, HEAD_DIM), BF16),
+            pltpu.VMEM((D_MODEL, HEAD_DIM), BF16),
             pltpu.VMEM((TILES, DEVICES, MY_ROWS, TILE), BF16),
+            pltpu.VMEM((2, MY_ROWS, HEAD_DIM), BF16),
             pltpu.SemaphoreType.DMA((TILES + 3,)),
-            pltpu.SemaphoreType.DMA((1,)),
-            pltpu.SemaphoreType.DMA((1,)),
+            pltpu.SemaphoreType.DMA((2,)),
+            pltpu.SemaphoreType.DMA((2,)),
         ],
         compiler_params=pltpu.CompilerParams(
             collective_id=0, has_side_effects=True, vmem_limit_bytes=26 * MIB
@@ -168,42 +184,54 @@
     )(*in_hbm(x, w_query, w_key, w_value, k_cache, v_cache))
 
 
-def attend_kernel(layer, has_prev, len_ref, q_ref, kn_ref, vn_ref, *refs):
-    k_out, v_out, ctx_ref, kv_buf, q_buf, kn_buf, vn_buf, out_sems = refs[-8:]
+def attend_kernel(layer, late_rows, len_hbm, q_ref, new_ref, *refs):
+    k_hbm, v_hbm = refs[1:3]
+    k_out, v_out, ctx_ref, kv_buf, len_ref, q_buf, new_buf, sems = refs[-8:]
     k_buf, v_buf = kv_buf.at[0], kv_buf.at[1]
     me = lax.axis_index("model")
+    out_sems, len_sem, late_sem = (sems.at[0], sems.at[1]), sems.at[2], sems.at[3]
+    len_load = pltpu.make_async_copy(len_hbm, len_ref, len_sem)
+    len_load.start()
+    late = pl.ds(MY_ROWS - late_rows, late_rows)
+    if late_rows:
+        load_cache(layer, late, k_hbm, v_hbm, kv_buf, late_sem)
 
     def save(which, b):
         hbm, buf = ((k_out, k_buf), (v_out, v_buf))[which]
-        return pltpu.make_async_copy(buf.at[b], hbm.at[layer, b], out_sems.at[which])
-
-    kn_buf[...] = kn_ref[...].astype(F32)
-    vn_buf[...] = vn_ref[...].astype(F32)
-
-    @pl.loop(0, MY_ROWS)
-    def _(b):
-        pos = len_ref[me * MY_ROWS + b]
-        base = pl.multiple_of((pos // 16) * 16, 16)
-        here = lax.broadcasted_iota(jnp.int32, (16, HEAD_DIM), 0) == pos - base
-        for buf, new in ((k_buf, kn_buf), (v_buf, vn_buf)):
-            tile = buf[b, pl.ds(base, 16), :].astype(F32)
-            row = jnp.broadcast_to(new[pl.ds(b, 1), :], (16, HEAD_DIM))
-            buf[b, pl.ds(base, 16), :] = jnp.where(here, row, tile).astype(BF16)
-
-        @pl.when(b >= 1)
-        def _():
-            save(0, b - 1).start()
-            save(1, b - 1).start()
-
-    save(0, MY_ROWS - 1).start()
-    save(1, MY_ROWS - 1).start()
-
+        return pltpu.make_async_copy(buf.at[b], hbm.at[layer, b], out_sems[which])
+
+    new_buf[...] = new_ref[...].astype(F32)
     for j in range(TILES):
         for src in range(DEVICES):
             block = q_ref[j, src].astype(F32)
             for h in range(TILE // HEAD_DIM):
                 head = src * MY_HEADS + j * (TILE // HEAD_DIM) + h
                 q_buf[:, head, :] = block[:, h * HEAD_DIM:(h + 1) * HEAD_DIM]
+
+    def write_tokens(first, last):
+        @pl.loop(first, last)
+        def _(b):
+            pos = len_ref[me * MY_ROWS + b]
+            base = pl.multiple_of((pos // 16) * 16, 16)
+            here = lax.broadcasted_iota(jnp.int32, (16, HEAD_DIM), 0) == pos - base
+            for i, buf in enumerate((k_buf, v_buf)):
+                tile = buf[b, pl.ds(base, 16), :].astype(F32)
+                row = jnp.broadcast_to(new_buf[i, pl.ds(b, 1), :], (16, HEAD_DIM))
+                buf[b, pl.ds(base, 16), :] = jnp.where(here, row, tile).astype(BF16)
+
+            @pl.when(b > first)
+            def _():
+                save(0, b - 1).start()
+                save(1, b - 1).start()
+
+        save(0, last - 1).start()
+        save(1, last - 1).start()
+
+    len_load.wait()
+    write_tokens(0, MY_ROWS - late_rows)
+    if late_rows:
+        await_all(kv_buf.at[:, late], late_sem)
+        write_tokens(MY_ROWS - late_rows, MY_ROWS)
 
     scale = HEAD_DIM ** -0.5
 
@@ -233,38 +261,37 @@
                 attend([b], n)
 
     for which, hbm in enumerate((k_out, v_out)):
-        await_all(hbm.at[layer], out_sems.at[which])
-
-
-def attend_call(layer, cache_len, q, kn, vn, kv_pre, prev):
+        await_all(hbm.at[layer], out_sems[which])
+
+
+def attend_call(layer, late_rows, cache_len, q, kv_new, kv_pre, k_cache, v_cache, prev):
     any_spec = pl.BlockSpec(memory_space=pl.ANY)
     vmem_spec = pl.BlockSpec(memory_space=pltpu.VMEM)
-    whole = jax.ShapeDtypeStruct((2,) + kv_pre.shape[1:], BF16)
     k_all, v_all, ctx, _ = pl.pallas_call(
-        functools.partial(attend_kernel, layer, bool(prev)),
+        functools.partial(attend_kernel, layer, late_rows),
         name="attend",
         out_shape=(
-            whole,
-            whole,
+            jax.ShapeDtypeStruct(k_cache.shape, BF16),
+            jax.ShapeDtypeStruct(v_cache.shape, BF16),
             pltpu.VMEM((DEVICES, MY_ROWS, MY_HEADS, HEAD_DIM), BF16),
             pltpu.VMEM(kv_pre.shape, BF16),
         ),
-        in_specs=[pl.BlockSpec(memory_space=pltpu.SMEM)] + [vmem_spec] * 4 + [any_spec] * len(prev),
+        in_specs=[any_spec] + [vmem_spec] * 3 + [any_spec] * (2 + len(prev)),
         out_specs=(any_spec, any_spec, vmem_spec, vmem_spec),
         scratch_shapes=[
+            pltpu.SMEM((ROWS,), jnp.int32),
             pltpu.VMEM((MY_ROWS, NUM_HEADS, HEAD_DIM), F32),
-            pltpu.VMEM((MY_ROWS, HEAD_DIM), F32),
-            pltpu.VMEM((MY_ROWS, HEAD_DIM), F32),
-            pltpu.SemaphoreType.DMA((2,)),
+            pltpu.VMEM((2, MY_ROWS, HEAD_DIM), F32),
+            pltpu.SemaphoreType.DMA((4,)),
         ],
-        input_output_aliases={4: 3} | ({5: 0, 6: 1} if prev else {}),
+        input_output_aliases={3: 3} | ({6: 0, 7: 1} if prev else {}),
         compiler_params=pltpu.CompilerParams(vmem_limit_bytes=16 * MIB),
-    )(cache_len, *in_vmem(q, kn, vn, kv_pre), *prev)
+    )(*in_hbm(cache_len), *in_vmem(q, kv_new, kv_pre), *in_hbm(k_cache, v_cache), *prev)
     return ctx, k_all, v_all
 
 
 SELF, XN, YN, DIAG = range(4)
-CONTEXT, CORE, SUMS, WHOLE, HALVES, QUERY = range(6)
+CONTEXT, CORE, SUMS, WHOLE, HALVES, QUERY, NEW_ROWS = range(7)
 
 
 def combine_kernel(layer, last, *refs):
@@ -273,12 +300,12 @@
          ctx_buf, lhs, w_buf, send_d2d, recv_d2d, acc, rx_diag, ry_diag, rx_dir, ry_dir, rx_fwd, ry_fwd, h_buf,
          load_sems, send_sems, recv_sems) = refs
     else:
-        (ctx_in, res_hbm, wo_hbm, wq_hbm, wk_hbm, wv_hbm, k_hbm, v_hbm, own_out, q_out, kn_out, vn_out, kv_pre,
+        (ctx_in, res_hbm, wo_hbm, wq_hbm, wk_hbm, wv_hbm, k_hbm, v_hbm, own_out, q_out, kv_out, kv_pre,
          ctx_buf, lhs, res_buf, w_buf, send_d2d, recv_d2d, acc, rx_diag, ry_diag, rx_dir, ry_dir, rx_fwd, ry_fwd, h_buf,
-         wkv_buf, q_acc, q_send,
+         wkv_buf, q_acc, q_send, kv_send,
          load_sems, send_sems, recv_sems) = refs
     me, flip, xn, yn, diag = places()
-    partner = me + flip
+    partner, core = me + flip, lax.rem(me, 2)
     chip_mate = {SELF: me, XN: xn, YN: yn, DIAG: diag}
     owner = lambda r, c: chip_mate[r] + c * flip
     column = lambda r, c, g: pl.multiple_of(owner(r, c) * MY_COLS + g * PIECE, PIECE)
@@ -299,7 +326,7 @@
         res_load = pltpu.make_async_copy(
             res_hbm.at[:, pl.ds(pl.multiple_of(me * MY_COLS, MY_COLS), MY_COLS)], res_buf, res_sem)
         res_load.start()
-        load_kv_weights(layer + 1, wk_hbm, wv_hbm, wkv_buf, wkv_sem)
+        load_kv_weights(layer + 1, core, wk_hbm, wv_hbm, wkv_buf, wkv_sem)
     wq_order = [(r, c, g) for r in (SELF, XN, YN, DIAG) for c in (0, 1) for g in range(GROUPS)]
     wq_slot = {}
 
@@ -317,8 +344,7 @@
     meet_all(me)
 
     ctx_sem = copies.new_receive()
-    for k in range(1, DEVICES):
-        to = lax.rem(me + k, DEVICES)
+    for to in others():
         copies.start(ctx_in.at[to], ctx_buf.at[me], to, CONTEXT, ctx_sem)
     ctx_buf[me] = ctx_in[me]
     await_all(ctx_buf.at[pl.ds(0, DEVICES - 1)], ctx_sem)
@@ -355,7 +381,7 @@
         pending = (g, r)
     settle(*pending)
     if not last:
-        load_cache(layer + 1, k_hbm, v_hbm, kv_pre, cache_sem)
+        load_cache(layer + 1, pl.ds(0, MY_ROWS), k_hbm, v_hbm, kv_pre, cache_sem)
 
     for g in range(GROUPS):
         first[g, 0].wait_recv()
@@ -438,23 +464,21 @@
         q_sem = copies.new_receive()
         for j in range(TILES):
             q_send[j] = q_acc[:, j * TILE:(j + 1) * TILE].astype(BF16).reshape(DEVICES, MY_ROWS, TILE)
-            send_query_tile(copies, me, j, q_send, q_out, QUERY, q_sem)
+            q_out[j, me] = q_send[j, me]
+        for to in others():
+            copies.start(q_send.at[:, to], q_out.at[:, me], to, QUERY, q_sem)
         await_all(wkv_buf, wkv_sem)
-        mine = pl.ds(pl.multiple_of(me * MY_ROWS, MY_ROWS), MY_ROWS)
-        kn = jnp.zeros((MY_ROWS, HEAD_DIM), F32)
-        vn = jnp.zeros((MY_ROWS, HEAD_DIM), F32)
+        chip_rows = pl.ds(pl.multiple_of((me - core) * MY_ROWS, 2 * MY_ROWS), 2 * MY_ROWS)
+        made = jnp.zeros((2 * MY_ROWS, HEAD_DIM), F32)
         for r in (SELF, XN, YN, DIAG):
             for c in (0, 1):
                 for g in range(GROUPS):
-                    rows = h_buf[r, c, g, mine, :]
-                    depth = pl.ds(column(r, c, g), PIECE)
-                    kn += dot(rows, wkv_buf[0, depth, :])
-                    vn += dot(rows, wkv_buf[1, depth, :])
-        kn_out[...] = kn.astype(BF16)
-        vn_out[...] = vn.astype(BF16)
-        others = pl.ds(0, DEVICES - 1)
-        await_all(q_out.at[:, others], q_sem)
-        await_all(q_send.at[:, others], send_sems.at[QUERY])
+                    made += dot(h_buf[r, c, g, chip_rows, :], wkv_buf[pl.ds(column(r, c, g), PIECE), :])
+        shared = share_new_rows(copies, core, partner, made, kv_send, kv_out, NEW_ROWS)
+        seven = pl.ds(0, DEVICES - 1)
+        await_all(q_out.at[:, seven], q_sem)
+        shared.wait()
+        await_all(q_send.at[:, seven], send_sems.at[QUERY])
         await_all(kv_pre, cache_sem)
     await_all(ctx_in.at[pl.ds(0, DEVICES - 1)], send_sems.at[CONTEXT])
     await_all(send_d2d, send_sems.at[CORE])
@@ -466,7 +490,7 @@
 def combine_call(layer, last, ctx, residual, w_out, more):
     any_spec = pl.BlockSpec(memory_space=pl.ANY)
     vmem_spec = pl.BlockSpec(memory_space=pltpu.VMEM)
-    receives = (1 if last else 2) + GROUPS * (4 + 6 + 7)
+    receives = (1 if last else 3) + GROUPS * (4 + 6 + 7)
     scratch = [
         pltpu.VMEM((DEVICES, MY_ROWS, MY_HEADS, HEAD_DIM), BF16),
         pltpu.VMEM((ROWS, MY_COLS), BF16),
@@ -485,13 +509,14 @@
         out_specs = (vmem_spec,) * len(out_shape)
         scratch.insert(2, pltpu.VMEM((ROWS, MY_COLS), BF16))
         scratch += [
-            pltpu.VMEM((2, D_MODEL, HEAD_DIM), BF16),
+            pltpu.VMEM((D_MODEL, HEAD_DIM), BF16),
             pltpu.VMEM((ROWS, MY_COLS), F32),
             pltpu.VMEM((TILES, DEVICES, MY_ROWS, TILE), BF16),
+            pltpu.VMEM((2, MY_ROWS, HEAD_DIM), BF16),
         ]
     scratch += [
         pltpu.SemaphoreType.DMA((SLOTS + (0 if last else 3),)),
-        pltpu.SemaphoreType.DMA((5 if last else 6,)),
+        pltpu.SemaphoreType.DMA((5 if last else 7,)),
         pltpu.SemaphoreType.DMA((receives,)),
     ]
     return pl.pallas_call(
@@ -511,11 +536,11 @@
     cache_spec = P(None, ("replica", "model"), None, None)
 
     def device_step(x, cache_len, w_query, w_key, w_value, w_out, k_cache, v_cache):
-        q, kn, vn, kv_pre = query_call(x, w_query, w_key, w_value, k_cache, v_cache)
-        ctx, k_all, v_all = attend_call(0, cache_len, q, kn, vn, kv_pre, ())
-        own, q, kn, vn, kv_pre = combine_call(
-            0, False, ctx, x, w_out, (w_query, w_key, w_value, k_cache, v_cache))
-        ctx, k_all, v_all = attend_call(1, cache_len, q, kn, vn, kv_pre, (k_all, v_all))
+        caches = (k_cache, v_cache)
+        q, kv_new, kv_pre = query_call(x, w_query, w_key, w_value, *caches)
+        ctx, k_all, v_all = attend_call(0, LATE_ROWS, cache_len, q, kv_new, kv_pre, *caches, ())
+        own, q, kv_new, kv_pre = combine_call(0, False, ctx, x, w_out, (w_query, w_key, w_value, *caches))
+        ctx, k_all, v_all = attend_call(1, 0, cache_len, q, kv_new, kv_pre, *caches, (k_all, v_all))
         out = combine_call(1, True, ctx, own, w_out, ())
         return out, k_all, v_all
 

time: 112 us -> 110 us (0.982)
  Pallas kernels: 110 us -> 108 us
    pallas_call x2, Pallas kernels: 82.9 us -> 79.8 us  [combine_call(): pl.pallas_call(functools.partial(combine_kernel, layer, last), name='comb...]
    pallas_call x2, Pallas kernels: 13 us -> 14.2 us  [attend_call(): pl.pallas_call(functools.partial(attend_kernel, layer, late_rows), name='...]
where the time goes in v4:
time: 110 us
  Pallas kernels  108 us (98%)
  local copies, waits for them, and re-layouts  1.32 us (1%)
    pallas_call x2, Pallas kernels, combine_call(): pl.pallas_call(functools.partial(combine_kernel, layer, last), name='comb...  79.8 us
    pallas_call x2, Pallas kernels, attend_call(): pl.pallas_call(functools.partial(attend_kernel, layer, late_rows), name='...  14.2 us
    pallas_call x1, Pallas kernels, query_call(): pl.pallas_call(query_kernel, name='query', out_shape=QUERY_SHAPES, in_spe...  13.9 us

profile of v4, /device:TPU:0, one launch (start us, length us, event | category | flops | bytes accessed | tf_op | source)
XLA Modules:
  0.0 109.8 jit_solution(5927380332668074809)
XLA Ops:
  0.6 13.9 %query.1 = (bf16[4,8,16,256]{3,2,1,0:T(8,128)(2,1)S(1)}, bf16[2,16,128]{2,1,0:T(8,128)(2,1)S(1)}, bf16[2,16,2048,128]{3,2,1,0:T(8,128)(2,1)S(1)}) custom-call(bf16[128,8192]{1,0:T(8,128)(2,1)} %refs_1_.4, bf16[2,8192,1024]{2,1,0:T(8,128)(2,1)} %refs_3_.1, bf16[2,8192,128]{2,1,0:T(8,128)(2,1)} %refs_4_.1, bf16[2,8192,128]{2,1,0:T(8,128)(2,1)} %refs_5_.1, ...), custom_call_target="tpu_custom_call" | custom-call | tf_op jit(solution)/shard_map/query/pallas_call | solution.py:165
  14.5 7.6 %attend.2 = (bf16[2,16,2048,128]{3,2,1,0:T(8,128)(2,1)}, bf16[2,16,2048,128]{3,2,1,0:T(8,128)(2,1)}, bf16[8,16,8,128]{3,2,1,0:T(8,128)(2,1)S(1)}, bf16[2,16,2048,128]{3,2,1,0:T(8,128)(2,1)S(1)}) custom-call(s32[128]{0:T(128)} %len_hbm.3, bf16[4,8,16,256]{3,2,1,0:T(8,128)(2,1)S(1)} %get-tuple-element.16.q_ref, ...), custom_call_target="tpu_custom_call", output_to_operand_aliasing={{3}: (3, {})} | custom-call | tf_op jit(solution)/shard_map/attend/pallas_call | solution.py:270
  22.1 42.6 %combine.1 = (bf16[128,1024]{1,0:T(8,128)(2,1)S(1)}, bf16[4,8,16,256]{3,2,1,0:T(8,128)(2,1)S(1)}, bf16[2,16,128]{2,1,0:T(8,128)(2,1)S(1)}, bf16[2,16,2048,128]{3,2,1,0:T(8,128)(2,1)S(1)}) custom-call(bf16[8,16,8,128]{3,2,1,0:T(8,128)(2,1)S(1)} %get-tuple-element.19.refs_0_, bf16[128,8192]{1,0:T(8,128)(2,1)} %refs_1_.4, bf16[2,1024,8192]{2,1,0:T(8,128)(2,1)} %refs_2_.7, ...), custom_call_target="tpu_custom_call" | custom-call | tf_op jit(solution)/shard_map/combine/pallas_call | solution.py:522
  64.7 6.5 %attend.3 = (bf16[2,16,2048,128]{3,2,1,0:T(8,128)(2,1)}, bf16[2,16,2048,128]{3,2,1,0:T(8,128)(2,1)}, bf16[8,16,8,128]{3,2,1,0:T(8,128)(2,1)S(1)}, bf16[2,16,2048,128]{3,2,1,0:T(8,128)(2,1)S(1)}) custom-call(s32[128]{0:T(128)} %len_hbm.3, ...), custom_call_target="tpu_custom_call", output_to_operand_aliasing={{3}: (3, {}), {0}: (6, {}), {1}: (7, {})} | custom-call | tf_op jit(solution)/shard_map/attend/pallas_call | solution.py:270
  71.2 37.2 %combine_last.1 = bf16[128,8192]{1,0:T(8,128)(2,1)S(1)} custom-call(bf16[8,16,8,128]{3,2,1,0:T(8,128)(2,1)S(1)} %get-tuple-element.25.refs_0_, bf16[128,1024]{1,0:T(8,128)(2,1)S(1)} %get-tuple-element.26.refs_1_, bf16[2,1024,8192]{2,1,0:T(8,128)(2,1)} %refs_2_.7), custom_call_target="tpu_custom_call" | custom-call | tf_op jit(solution)/shard_map/combine_last/pallas_call | solution.py:522
  108.4 1.3 %copy.20 = bf16[128,8192]{1,0:T(8,128)(2,1)} copy(bf16[128,8192]{1,0:T(8,128)(2,1)S(1)} %combine_last.1) | data formatting | bytes 4194304

commit v5 on v4

v5 whole, which is shorter than its diff:
```python
import functools

import jax
import jax.numpy as jnp
from jax import lax
from jax.experimental import pallas as pl
from jax.experimental.pallas import tpu as pltpu
from jax.sharding import PartitionSpec as P

MESH = pl.DeviceIdType.MESH
BF16 = jnp.bfloat16
F32 = jnp.float32
MIB = 1024 * 1024

DEVICES = 8
ROWS = 128
MY_ROWS = 16
D_MODEL = 8192
HEAD_DIM = 128
MY_HEADS = 8
NUM_HEADS = 64
MY_COLS = 1024
SEQ = 2048
QUERY_TILE = 512
QUERY_DEPTH = 2048

GROUPS = 2
GROUP_SEQS = MY_ROWS // GROUPS
GROUP_ROWS = ROWS // GROUPS
HALF = GROUP_ROWS // 2
LATE_ROWS = 4
TOGETHER = 8
SPANS = (256, 512, 1024, 2048)


def dot(a, b):
    return jnp.dot(a, b, preferred_element_type=F32)


def places():
    me = lax.axis_index("model")
    core = lax.rem(me, 2)
    x = lax.rem(lax.div(me, 2), 2)
    y = lax.div(me, 4)
    flip = 1 - 2 * core
    xn = me + 2 - 4 * x
    yn = me + 4 - 8 * y
    diag = xn + 4 - 8 * y
    return me, flip, xn, yn, diag


def await_all(ref, sem):
    pltpu.make_async_copy(ref, ref, sem).wait()


class Copies:
    def __init__(self, send_sems, recv_sems):
        self.send_sems, self.recv_sems, self.receives = send_sems, recv_sems, 0

    def new_receive(self):
        self.receives += 1
        return self.recv_sems.at[self.receives - 1]

    def start(self, src, dst, device, kind, recv_sem=None):
        copy = pltpu.make_async_remote_copy(
            src_ref=src,
            dst_ref=dst,
            send_sem=self.send_sems.at[kind],
            recv_sem=self.new_receive() if recv_sem is None else recv_sem,
            device_id={"model": device},
            device_id_type=MESH,
        )
        copy.start()
        return copy


def meet_all(me):
    barrier = pltpu.get_barrier_semaphore()
    for k in range(1, DEVICES):
        pl.semaphore_signal(barrier, inc=1, device_id={"model": lax.rem(me + k, DEVICES)}, device_id_type=MESH)
    pl.semaphore_wait(barrier, DEVICES - 1)


def others():
    me, flip, xn, yn, diag = places()
    return [diag, diag + flip, xn, yn, xn + flip, yn + flip, me + flip]


def load_cache(layer, rows, k_hbm, v_hbm, kv, sem):
    for i, hbm in enumerate((k_hbm, v_hbm)):
        pltpu.make_async_copy(hbm.at[layer, rows], kv.at[i, rows], sem).start()


def load_kv_weights(layer, core, wk_hbm, wv_hbm, wkv_buf, sem):
    for i, hbm in enumerate((wk_hbm, wv_hbm)):
        @pl.when(core == i)
        def _():
            pltpu.make_async_copy(hbm.at[layer], wkv_buf, sem).start()


def share_new_rows(copies, core, partner, made, kv_send, kv_out, kind):
    kv_send[...] = made.reshape(2, MY_ROWS, HEAD_DIM).astype(BF16)
    copy = copies.start(kv_send.at[1 - core], kv_out.at[core], partner, kind)
    kv_out[core] = kv_send[core]
    return copy


def in_vmem(*arrays):
    return [pltpu.with_memory_space_constraint(a, pltpu.VMEM) for a in arrays]


def in_hbm(*arrays):
    return [pltpu.with_memory_space_constraint(a, pltpu.HBM) for a in arrays]


QUERY_SHAPES = (
    pltpu.VMEM((DEVICES, MY_ROWS, MY_COLS), BF16),
    pltpu.VMEM((2, MY_ROWS, HEAD_DIM), BF16),
    pltpu.VMEM((2, MY_ROWS, SEQ, HEAD_DIM), BF16),
)


def query_kernel(x_hbm, wq_hbm, wk_hbm, wv_hbm, k_hbm, v_hbm, q_out, kv_out, kv_pre,
                 x_buf, wq_buf, wkv_buf, q_send, kv_send, load_sems, send_sems, recv_sems):
    me, flip, _, _, _ = places()
    core = lax.rem(me, 2)
    columns = [pl.ds(j * QUERY_TILE, QUERY_TILE) for j in range(MY_COLS // QUERY_TILE)]
    depths = [pl.ds(k * QUERY_DEPTH, QUERY_DEPTH) for k in range(D_MODEL // QUERY_DEPTH)]
    x_sem, wkv_sem, cache_sem = [load_sems.at[i] for i in range(3)]
    x_load = pltpu.make_async_copy(x_hbm, x_buf, x_sem)
    x_load.start()
    wq_loads = []
    for cols in columns:
        for depth in depths:
            sem = load_sems.at[3 + len(wq_loads)]
            wq_loads.append(pltpu.make_async_copy(wq_hbm.at[0, depth, cols], wq_buf.at[depth, cols], sem))
            wq_loads[-1].start()
    load_kv_weights(0, core, wk_hbm, wv_hbm, wkv_buf, wkv_sem)
    early = pl.ds(0, MY_ROWS - LATE_ROWS)
    load_cache(0, early, k_hbm, v_hbm, kv_pre, cache_sem)
    meet_all(me)
    copies = Copies(send_sems, recv_sems)
    q_sem = copies.new_receive()
    x_load.wait()
    for j, cols in enumerate(columns):
        q = None
        for k, depth in enumerate(depths):
            wq_loads[j * len(depths) + k].wait()
            part = dot(x_buf[:, depth], wq_buf[depth, cols])
            q = part if q is None else q + part
        q_send[:, :, cols] = q.astype(BF16).reshape(DEVICES, MY_ROWS, QUERY_TILE)
        for to in others():
            copies.start(q_send.at[to, :, cols], q_out.at[me, :, cols], to, 0, q_sem)
    q_out[me] = q_send[me]
    chip_rows = pl.ds(pl.multiple_of((me - core) * MY_ROWS, 2 * MY_ROWS), 2 * MY_ROWS)
    await_all(wkv_buf, wkv_sem)
    shared = share_new_rows(copies, core, me + flip, dot(x_buf[chip_rows, :], wkv_buf[...]), kv_send, kv_out, 1)
    seven = pl.ds(0, DEVICES - 1)
    await_all(q_out.at[seven], q_sem)
    shared.wait()
    await_all(q_send.at[seven], send_sems.at[0])
    await_all(kv_pre.at[:, early], cache_sem)


def query_call(x, w_query, w_key, w_value, k_cache, v_cache):
    any_spec = pl.BlockSpec(memory_space=pl.ANY)
    vmem_spec = pl.BlockSpec(memory_space=pltpu.VMEM)
    return pl.pallas_call(
        query_kernel,
        name="query",
        out_shape=QUERY_SHAPES,
        in_specs=[any_spec] * 6,
        out_specs=(vmem_spec,) * len(QUERY_SHAPES),
        scratch_shapes=[
            pltpu.VMEM((ROWS, D_MODEL), BF16),
            pltpu.VMEM((D_MODEL, MY_COLS), BF16),
            pltpu.VMEM((D_MODEL, HEAD_DIM), BF16),
            pltpu.VMEM((DEVICES, MY_ROWS, MY_COLS), BF16),
            pltpu.VMEM((2, MY_ROWS, HEAD_DIM), BF16),
            pltpu.SemaphoreType.DMA((3 + (MY_COLS // QUERY_TILE) * (D_MODEL // QUERY_DEPTH),)),
            pltpu.SemaphoreType.DMA((2,)),
            pltpu.SemaphoreType.DMA((2,)),
        ],
        compiler_params=pltpu.CompilerParams(
            collective_id=0, has_side_effects=True, vmem_limit_bytes=26 * MIB
        ),
    )(*in_hbm(x, w_query, w_key, w_value, k_cache, v_cache))


def attend_kernel(layer, late_rows, len_hbm, q_ref, new_ref, *refs):
    k_hbm, v_hbm = refs[1:3]
    k_out, v_out, ctx_ref, kv_buf, len_ref, q_buf, new_buf, sems = refs[-8:]
    k_buf, v_buf = kv_buf.at[0], kv_buf.at[1]
    me = lax.axis_index("model")
    out_sems, len_sem, late_sem = (sems.at[0], sems.at[1]), sems.at[2], sems.at[3]
    len_load = pltpu.make_async_copy(len_hbm, len_ref, len_sem)
    len_load.start()
    late = pl.ds(MY_ROWS - late_rows, late_rows)
    if late_rows:
        load_cache(layer, late, k_hbm, v_hbm, kv_buf, late_sem)

    def save(which, b):
        hbm, buf = ((k_out, k_buf), (v_out, v_buf))[which]
        return pltpu.make_async_copy(buf.at[b], hbm.at[layer, b], out_sems[which])

    new_buf[...] = new_ref[...].astype(F32)
    for src in range(DEVICES):
        block = q_ref[src].astype(F32)
        for h in range(MY_HEADS):
            q_buf[:, src * MY_HEADS + h, :] = block[:, h * HEAD_DIM:(h + 1) * HEAD_DIM]

    def write_tokens(first, last):
        @pl.loop(first, last)
        def _(b):
            pos = len_ref[me * MY_ROWS + b]
            base = pl.multiple_of((pos // 16) * 16, 16)
            here = lax.broadcasted_iota(jnp.int32, (16, HEAD_DIM), 0) == pos - base
            for i, buf in enumerate((k_buf, v_buf)):
                tile = buf[b, pl.ds(base, 16), :].astype(F32)
                row = jnp.broadcast_to(new_buf[i, pl.ds(b, 1), :], (16, HEAD_DIM))
                buf[b, pl.ds(base, 16), :] = jnp.where(here, row, tile).astype(BF16)

            @pl.when(b > first)
            def _():
                save(0, b - 1).start()
                save(1, b - 1).start()

        save(0, last - 1).start()
        save(1, last - 1).start()

    len_load.wait()
    write_tokens(0, MY_ROWS - late_rows)

    scale = HEAD_DIM ** -0.5

    def attend(rows, n):
        t = lax.broadcasted_iota(jnp.int32, (NUM_HEADS, n), 1)
        s = [lax.dot_general(q_buf[b].astype(BF16), k_buf[b, 0:n, :], (((1,), (1,)), ((), ())),
                             preferred_element_type=F32) for b in rows]
        s = [jnp.where(t <= len_ref[me * MY_ROWS + b], v * scale, -jnp.inf) for v, b in zip(s, rows)]
        peak = [jnp.max(v, axis=1, keepdims=True) for v in s]
        e = [jnp.exp(v - u) for v, u in zip(s, peak)]
        share = [1.0 / jnp.sum(v, axis=1, keepdims=True) for v in e]
        p = [(v * u).astype(BF16) for v, u in zip(e, share)]
        c = [dot(v, v_buf[b, 0:n, :]) for v, b in zip(p, rows)]
        for v, b in zip(c, rows):
            ctx_ref[:, b] = v.reshape(DEVICES, MY_HEADS, HEAD_DIM).astype(BF16)

    attend(list(range(TOGETHER)), SPANS[0])
    if late_rows:
        await_all(kv_buf.at[:, late], late_sem)
        write_tokens(MY_ROWS - late_rows, MY_ROWS)
    attend(list(range(TOGETHER, MY_ROWS)), SPANS[0])

    @pl.loop(0, MY_ROWS)
    def _(b):
        pos = len_ref[me * MY_ROWS + b]
        for low, n in zip(SPANS, SPANS[1:]):
            @pl.when(jnp.logical_and(pos >= low, pos < n))
            def _(n=n):
                attend([b], n)

    for which, hbm in enumerate((k_out, v_out)):
        await_all(hbm.at[layer], out_sems[which])


def attend_call(layer, late_rows, cache_len, q, kv_new, kv_pre, k_cache, v_cache, prev):
    any_spec = pl.BlockSpec(memory_space=pl.ANY)
    vmem_spec = pl.BlockSpec(memory_space=pltpu.VMEM)
    k_all, v_all, ctx, _ = pl.pallas_call(
        functools.partial(attend_kernel, layer, late_rows),
        name="attend",
        out_shape=(
            jax.ShapeDtypeStruct(k_cache.shape, BF16),
            jax.ShapeDtypeStruct(v_cache.shape, BF16),
            pltpu.VMEM((DEVICES, MY_ROWS, MY_HEADS, HEAD_DIM), BF16),
            pltpu.VMEM(kv_pre.shape, BF16),
        ),
        in_specs=[any_spec] + [vmem_spec] * 3 + [any_spec] * (2 + len(prev)),
        out_specs=(any_spec, any_spec, vmem_spec, vmem_spec),
        scratch_shapes=[
            pltpu.SMEM((ROWS,), jnp.int32),
            pltpu.VMEM((MY_ROWS, NUM_HEADS, HEAD_DIM), F32),
            pltpu.VMEM((2, MY_ROWS, HEAD_DIM), F32),
            pltpu.SemaphoreType.DMA((4,)),
        ],
        input_output_aliases={3: 3} | ({6: 0, 7: 1} if prev else {}),
        compiler_params=pltpu.CompilerParams(vmem_limit_bytes=16 * MIB),
    )(*in_hbm(cache_len), *in_vmem(q, kv_new, kv_pre), *in_hbm(k_cache, v_cache), *prev)
    return ctx, k_all, v_all


SELF, XN, YN, DIAG = range(4)
PASS_ON_AFTER = XN
LEFT, RIGHT = pl.ds(0, MY_COLS // 2), pl.ds(MY_COLS // 2, MY_COLS // 2)
CONTEXT, CORE, SUMS, WHOLE, HALVES, QUERY, NEW_ROWS = range(7)


def combine_kernel(layer, last, *refs):
    if last:
        (ctx_in, res_buf, wo_hbm, out_ref,
         ctx_buf, lhs, w_buf, send_d2d, recv_d2d, acc, rx_diag, ry_diag, top_in, bottom_in, h_buf,
         load_sems, send_sems, recv_sems) = refs
    else:
        (ctx_in, res_hbm, wo_hbm, wq_hbm, wk_hbm, wv_hbm, k_hbm, v_hbm, own_out, q_out, kv_out, kv_pre,
         ctx_buf, lhs, res_buf, w_buf, send_d2d, recv_d2d, acc, rx_diag, ry_diag, top_in, bottom_in, h_buf,
         wkv_buf, q_acc, q_send, kv_send,
         load_sems, send_sems, recv_sems) = refs
    me, flip, xn, yn, diag = places()
    partner, core = me + flip, lax.rem(me, 2)
    chip_mate = {SELF: me, XN: xn, YN: yn, DIAG: diag}
    columns = lambda r, c: pl.ds(pl.multiple_of((chip_mate[r] + c * flip) * MY_COLS, MY_COLS), MY_COLS)
    copies = Copies(send_sems, recv_sems)
    wo_order = [(r, c) for r in (DIAG, XN, YN, SELF) for c in (1, 0)]
    wq_order = [(r, c) for r in (SELF, XN, YN, DIAG) for c in (0, 1)]
    top, bottom = pl.ds(0, HALF), pl.ds(HALF, HALF)
    seven = pl.ds(0, DEVICES - 1)
    seqs = [pl.ds(g * GROUP_SEQS, GROUP_SEQS) for g in range(GROUPS)]

    for slot, (r, c) in enumerate(wo_order):
        pltpu.make_async_copy(wo_hbm.at[layer, :, columns(r, c)], w_buf.at[slot], load_sems.at[slot // 2]).start()
    if not last:
        wq_sem, res_sem, wkv_sem, cache_sem = [load_sems.at[4 + i] for i in range(4)]
        res_load = pltpu.make_async_copy(res_hbm.at[:, :, :, columns(SELF, 0)], res_buf, res_sem)
        res_load.start()
        load_kv_weights(layer + 1, core, wk_hbm, wv_hbm, wkv_buf, wkv_sem)

    meet_all(me)

    ctx_sems = [copies.new_receive() for _ in range(GROUPS)]

    def send_context(g):
        for to in others():
            copies.start(ctx_in.at[to, seqs[g]], ctx_buf.at[g, me], to, CONTEXT, ctx_sems[g])
        ctx_buf[g, me] = ctx_in[me, seqs[g]]

    send_context(0)

    d2d, first, in_sems = {}, {}, {}

    def receive_context(g):
        await_all(ctx_buf.at[g, seven], ctx_sems[g])
        if g + 1 < GROUPS:
            send_context(g + 1)
        rows = ctx_buf[g].astype(F32).reshape(GROUP_ROWS, MY_HEADS, HEAD_DIM)
        lhs[g] = rows.reshape(GROUP_ROWS, MY_COLS).astype(BF16)

    def settle(g, r):
        await_all(recv_d2d.at[g, r], d2d[g, r])
        acc[g, r] += recv_d2d[g, r]
        if r == DIAG:
            first[g, 0] = copies.start(acc.at[g, r, top], rx_diag.at[g], xn, SUMS)
            first[g, 1] = copies.start(acc.at[g, r, bottom], ry_diag.at[g], yn, SUMS)
        if r == YN:
            in_sems[g] = copies.new_receive(), copies.new_receive()
            copies.start(acc.at[g, XN, top], top_in.at[g, 0], xn, SUMS, in_sems[g][0])
            copies.start(acc.at[g, YN, bottom], bottom_in.at[g, 0], yn, SUMS, in_sems[g][1])

    def pass_on(g):
        first[g, 0].wait_recv()
        acc[g, YN, top] += rx_diag[g]
        copies.start(acc.at[g, YN, top], top_in.at[g, 1], yn, SUMS, in_sems[g][0])
        first[g, 1].wait_recv()
        acc[g, XN, bottom] += ry_diag[g]
        copies.start(acc.at[g, XN, bottom], bottom_in.at[g, 1], xn, SUMS, in_sems[g][1])

    pending = None
    for g in range(GROUPS):
        receive_context(g)
        for slot, (r, c) in enumerate(wo_order):
            if g == 0 and c == 1:
                await_all(w_buf.at[pl.ds(slot, 2)], load_sems.at[slot // 2])
            if c == 1:
                d2d[g, r] = copies.new_receive()
                for cols in (LEFT, RIGHT) if r == DIAG else (pl.ds(0, MY_COLS),):
                    send_d2d[g, r, :, cols] = dot(lhs[g], w_buf[slot, :, cols])
                    copies.start(send_d2d.at[g, r, :, cols], recv_d2d.at[g, r, :, cols], partner, CORE, d2d[g, r])
            else:
                acc[g, r] = dot(lhs[g], w_buf[slot])
            if not last and g == GROUPS - 1:
                pltpu.make_async_copy(wq_hbm.at[layer + 1, columns(*wq_order[slot]), :], w_buf.at[slot], wq_sem).start()
            if c == 1 and pending is not None:
                settle(*pending)
                if g > 0 and pending == (g, PASS_ON_AFTER):
                    pass_on(g - 1)
            pending = (g, r)
    settle(*pending)
    if not last:
        load_cache(layer + 1, pl.ds(0, MY_ROWS), k_hbm, v_hbm, kv_pre, cache_sem)
    pass_on(GROUPS - 1)

    gather, diag_sems = {}, {}
    if not last:
        res_load.wait()

    def finish_group(g):
        if last:
            residual = res_buf[g].astype(F32)
        else:
            residual = res_buf[:, g].astype(F32).reshape(GROUP_ROWS, MY_COLS)
        await_all(top_in.at[g], in_sems[g][0])
        total = acc[g, SELF, top] + top_in[g, 0] + top_in[g, 1]
        h_buf[SELF, 0, g, top] = (residual[:HALF] + total).astype(BF16)
        await_all(bottom_in.at[g], in_sems[g][1])
        total = acc[g, SELF, bottom] + bottom_in[g, 0] + bottom_in[g, 1]
        h_buf[SELF, 0, g, bottom] = (residual[HALF:] + total).astype(BF16)
        mine = h_buf.at[SELF, 0, g]
        for r, device, halves in ((XN, xn, (top, bottom)), (YN, yn, (bottom, top))):
            gather[r, 0, g] = [copies.start(h_buf.at[SELF, 0, g, half], h_buf.at[r, 0, g, half], device, HALVES)
                               for half in halves]
        gather[SELF, 1, g] = copies.start(mine, h_buf.at[SELF, 1, g], partner, WHOLE)
        if not last:
            own_out[g] = h_buf[SELF, 0, g]

    def arrive(r, c, g):
        gather[r, c, g].wait_recv()

    if last:
        def use(g, *pieces):
            for r, c in pieces:
                rows = h_buf[r, c, g].astype(F32).reshape(DEVICES, GROUP_SEQS, MY_COLS).astype(BF16)
                out_ref[:, g, :, columns(r, c)] = rows
    else:
        wq_slot = {piece: slot for slot, piece in enumerate(wq_order)}

        def use(g, *pieces):
            q_acc[g] += sum(dot(h_buf[r, c, g], w_buf[wq_slot[r, c]]) for r, c in pieces)

    def relay_first(g):
        diag_sems[g] = copies.new_receive()
        for r, device, half in ((XN, yn, top), (YN, xn, bottom)):
            gather[r, 0, g][0].wait_recv()
            copies.start(h_buf.at[r, 0, g, half], h_buf.at[DIAG, 0, g, half], device, HALVES, diag_sems[g])

    def relay_second(g):
        for r in (XN, YN):
            gather[r, 0, g][1].wait_recv()
            gather[r, 1, g] = copies.start(h_buf.at[r, 0, g], h_buf.at[r, 1, g], partner, WHOLE)

    def relay_diag(g):
        await_all(h_buf.at[DIAG, 0, g], diag_sems[g])
        gather[DIAG, 1, g] = copies.start(h_buf.at[DIAG, 0, g], h_buf.at[DIAG, 1, g], partner, WHOLE)

    def send_query(g):
        q_send[g] = q_acc[g].astype(BF16).reshape(DEVICES, GROUP_SEQS, MY_COLS)
        for to in others():
            copies.start(q_send.at[g, to], q_out.at[me, seqs[g], :], to, QUERY, q_sem)

    if not last:
        q_sem = copies.new_receive()
        await_all(w_buf, wq_sem)
        q_acc[...] = jnp.zeros_like(q_acc)
    finish_group(0)
    finish_group(1)
    relay_first(0)
    for g in range(GROUPS):
        arrive(SELF, 1, g)
        use(g, (SELF, 0), (SELF, 1))
    relay_second(0)
    use(0, (XN, 0), (YN, 0))
    relay_first(1)
    arrive(XN, 1, 0)
    arrive(YN, 1, 0)
    use(0, (XN, 1), (YN, 1))
    relay_second(1)
    use(1, (XN, 0), (YN, 0))
    relay_diag(0)
    use(0, (DIAG, 0))
    arrive(XN, 1, 1)
    arrive(YN, 1, 1)
    use(1, (XN, 1), (YN, 1))
    relay_diag(1)
    arrive(DIAG, 1, 0)
    use(0, (DIAG, 1))
    if not last:
        send_query(0)
    use(1, (DIAG, 0))
    arrive(DIAG, 1, 1)
    use(1, (DIAG, 1))

    if not last:
        send_query(GROUPS - 1)
        for g in range(GROUPS):
            q_out[me, seqs[g], :] = q_send[g, me]
        await_all(wkv_buf, wkv_sem)
        chip_rows = pl.ds(pl.multiple_of((me - core) * GROUP_SEQS, 2 * GROUP_SEQS), 2 * GROUP_SEQS)
        made = jnp.zeros((GROUPS * 2 * GROUP_SEQS, HEAD_DIM), F32)
        for r, c in wq_order:
            rows = jnp.concatenate([h_buf[r, c, g, chip_rows, :] for g in range(GROUPS)], axis=0)
            made += dot(rows, wkv_buf[columns(r, c), :])
        made = made.reshape(GROUPS, 2, GROUP_SEQS, HEAD_DIM)
        made = jnp.concatenate([made[g, k] for k in range(2) for g in range(GROUPS)], axis=0)
        shared = share_new_rows(copies, core, partner, made, kv_send, kv_out, NEW_ROWS)
        await_all(q_out.at[seven], q_sem)
        shared.wait()
        await_all(q_send.at[:, seven], send_sems.at[QUERY])
        await_all(kv_pre, cache_sem)
    await_all(ctx_in.at[seven], send_sems.at[CONTEXT])
    await_all(send_d2d, send_sems.at[CORE])
    await_all(acc.at[:, pl.ds(0, 3)], send_sems.at[SUMS])
    await_all(h_buf.at[pl.ds(0, 2)], send_sems.at[WHOLE])
    await_all(h_buf.at[pl.ds(0, 3), 0], send_sems.at[HALVES])


def combine_call(layer, last, ctx, residual, w_out, more):
    any_spec = pl.BlockSpec(memory_space=pl.ANY)
    vmem_spec = pl.BlockSpec(memory_space=pltpu.VMEM)
    receives = (2 if last else 4) + GROUPS * (4 + 4 + 9)
    scratch = [
        pltpu.VMEM((GROUPS, DEVICES, GROUP_SEQS, MY_HEADS, HEAD_DIM), BF16),
        pltpu.VMEM((GROUPS, GROUP_ROWS, MY_COLS), BF16),
        pltpu.VMEM((DEVICES, MY_COLS, MY_COLS), BF16),
        pltpu.VMEM((GROUPS, 4, GROUP_ROWS, MY_COLS), F32),
        pltpu.VMEM((GROUPS, 4, GROUP_ROWS, MY_COLS), F32),
        pltpu.VMEM((GROUPS, 4, GROUP_ROWS, MY_COLS), F32),
        pltpu.VMEM((GROUPS, HALF, MY_COLS), F32),
        pltpu.VMEM((GROUPS, HALF, MY_COLS), F32),
        pltpu.VMEM((GROUPS, 2, HALF, MY_COLS), F32),
        pltpu.VMEM((GROUPS, 2, HALF, MY_COLS), F32),
        pltpu.VMEM((4, 2, GROUPS, GROUP_ROWS, MY_COLS), BF16),
    ]
    if last:
        out_shape = pltpu.VMEM((DEVICES, GROUPS, GROUP_SEQS, D_MODEL), BF16)
        out_specs = vmem_spec
    else:
        out_shape = (pltpu.VMEM((GROUPS, GROUP_ROWS, MY_COLS), BF16),) + QUERY_SHAPES
        out_specs = (vmem_spec,) * len(out_shape)
        scratch.insert(2, pltpu.VMEM((DEVICES, GROUPS, GROUP_SEQS, MY_COLS), BF16))
        scratch += [
            pltpu.VMEM((D_MODEL, HEAD_DIM), BF16),
            pltpu.VMEM((GROUPS, GROUP_ROWS, MY_COLS), F32),
            pltpu.VMEM((GROUPS, DEVICES, GROUP_SEQS, MY_COLS), BF16),
            pltpu.VMEM((2, MY_ROWS, HEAD_DIM), BF16),
        ]
    scratch += [
        pltpu.SemaphoreType.DMA((4 if last else 8,)),
        pltpu.SemaphoreType.DMA((5 if last else 7,)),
        pltpu.SemaphoreType.DMA((receives,)),
    ]
    return pl.pallas_call(
        functools.partial(combine_kernel, layer, last),
        name="combine_last" if last else "combine",
        out_shape=out_shape,
        in_specs=[vmem_spec, vmem_spec if last else any_spec] + [any_spec] * (1 + len(more)),
        out_specs=out_specs,
        scratch_shapes=scratch,
        compiler_params=pltpu.CompilerParams(
            collective_id=2 if last else 1, has_side_effects=True, vmem_limit_bytes=40 * MIB
        ),
    )(*in_vmem(ctx), *(in_vmem if last else in_hbm)(residual), *in_hbm(w_out, *more))


def solution(mesh):
    cache_spec = P(None, ("replica", "model"), None, None)

    def device_step(x, cache_len, w_query, w_key, w_value, w_out, k_cache, v_cache):
        caches = (k_cache, v_cache)
        q, kv_new, kv_pre = query_call(x, w_query, w_key, w_value, *caches)
        ctx, k_all, v_all = attend_call(0, LATE_ROWS, cache_len, q, kv_new, kv_pre, *caches, ())
        own, q, kv_new, kv_pre = combine_call(0, False, ctx, x.reshape(DEVICES, GROUPS, GROUP_SEQS, D_MODEL), w_out, (w_query, w_key, w_value, *caches))
        ctx, k_all, v_all = attend_call(1, 0, cache_len, q, kv_new, kv_pre, *caches, (k_all, v_all))
        out = combine_call(1, True, ctx, own, w_out, ())
        return out.reshape(x.shape), k_all, v_all

    return jax.shard_map(
        device_step,
        mesh=mesh,
        in_specs=(P("replica", None), P("replica"), P(None, None, "model"), P(), P(), P(None, "model", None), cache_spec, cache_spec),
        out_specs=(P("replica", None), cache_spec, cache_spec),
        check_vma=False,
    )
```

time: 110 us -> 104 us (0.945)
  Pallas kernels: 108 us -> 102 us
    pallas_call x2, Pallas kernels: 79.8 us -> 75.9 us  [combine_call(): pl.pallas_call(functools.partial(combine_kernel, layer, last), name='comb...]
where the time goes in v5:
time: 104 us
  Pallas kernels  102 us (98%)
  local copies, waits for them, and re-layouts  1.32 us (1%)
    pallas_call x2, Pallas kernels, combine_call(): pl.pallas_call(functools.partial(combine_kernel, layer, last), name='comb...  75.9 us
    pallas_call x2, Pallas kernels, attend_call(): pl.pallas_call(functools.partial(attend_kernel, layer, late_rows), name='...  13.2 us
    pallas_call x1, Pallas kernels, query_call(): pl.pallas_call(query_kernel, name='query', out_shape=QUERY_SHAPES, in_spe...  13.1 us

profile of v5, /device:TPU:0, one launch (start us, length us, event | category | flops | bytes accessed | tf_op | source)
XLA Modules:
  0.0 104.2 jit_solution(292878306213909487)
XLA Ops:
  0.6 13.1 %query.1 = (bf16[8,16,1024]{2,1,0:T(8,128)(2,1)S(1)}, bf16[2,16,128]{2,1,0:T(8,128)(2,1)S(1)}, bf16[2,16,2048,128]{3,2,1,0:T(8,128)(2,1)S(1)}) custom-call(bf16[128,8192]{1,0:T(8,128)(2,1)} %x_hbm.1, bf16[2,8192,1024]{2,1,0:T(8,128)(2,1)} %refs_3_.1, bf16[2,8192,128]{2,1,0:T(8,128)(2,1)} %refs_4_.1, bf16[2,8192,128]{2,1,0:T(8,128)(2,1)} %refs_5_.1, ...), custom_call_target="tpu_custom_call" | custom-call | tf_op jit(solution)/shard_map/query/pallas_call | solution.py:168
  13.7 6.7 %attend.2 = (bf16[2,16,2048,128]{3,2,1,0:T(8,128)(2,1)}, bf16[2,16,2048,128]{3,2,1,0:T(8,128)(2,1)}, bf16[8,16,8,128]{3,2,1,0:T(8,128)(2,1)S(1)}, bf16[2,16,2048,128]{3,2,1,0:T(8,128)(2,1)S(1)}) custom-call(s32[128]{0:T(128)} %len_hbm.3, bf16[8,16,1024]{2,1,0:T(8,128)(2,1)S(1)} %get-tuple-element.16.q_ref, ...), custom_call_target="tpu_custom_call", output_to_operand_aliasing={{3}: (3, {})} | custom-call | tf_op jit(solution)/shard_map/attend/pallas_call | solution.py:270
  20.4 40.5 %combine.1 = (bf16[2,64,1024]{2,1,0:T(8,128)(2,1)S(1)}, bf16[8,16,1024]{2,1,0:T(8,128)(2,1)S(1)}, bf16[2,16,128]{2,1,0:T(8,128)(2,1)S(1)}, bf16[2,16,2048,128]{3,2,1,0:T(8,128)(2,1)S(1)}) custom-call(bf16[8,16,8,128]{3,2,1,0:T(8,128)(2,1)S(1)} %get-tuple-element.19.refs_0_, bf16[8,2,8,8192]{3,2,1,0:T(8,128)(2,1)} %bitcast.3, bf16[2,1024,8192]{2,1,0:T(8,128)(2,1)} %refs_2_.7, ...), custom_call_target="tpu_custom_call" | custom-call | tf_op jit(solution)/shard_map/combine/pallas_call | solution.py:540
  60.9 6.5 %attend.3 = (bf16[2,16,2048,128]{3,2,1,0:T(8,128)(2,1)}, bf16[2,16,2048,128]{3,2,1,0:T(8,128)(2,1)}, bf16[8,16,8,128]{3,2,1,0:T(8,128)(2,1)S(1)}, bf16[2,16,2048,128]{3,2,1,0:T(8,128)(2,1)S(1)}) custom-call(s32[128]{0:T(128)} %len_hbm.3, ...), custom_call_target="tpu_custom_call", output_to_operand_aliasing={{3}: (3, {}), {0}: (6, {}), {1}: (7, {})} | custom-call | tf_op jit(solution)/shard_map/attend/pallas_call | solution.py:270
  67.4 35.4 %combine_last.1 = bf16[8,2,8,8192]{3,2,1,0:T(8,128)(2,1)S(1)} custom-call(bf16[8,16,8,128]{3,2,1,0:T(8,128)(2,1)S(1)} %get-tuple-element.25.refs_0_, bf16[2,64,1024]{2,1,0:T(8,128)(2,1)S(1)} %get-tuple-element.26.refs_1_, bf16[2,1024,8192]{2,1,0:T(8,128)(2,1)} %refs_2_.7), custom_call_target="tpu_custom_call" | custom-call | tf_op jit(solution)/shard_map/combine_last/pallas_call | solution.py:540
  102.8 1.3 %copy.20 = bf16[128,8192]{1,0:T(8,128)(2,1)} copy(bf16[128,8192]{1,0:T(8,128)(2,1)S(1)} %bitcast.2) | data formatting | bytes 4194304

commit v6 on v5

--- a/solution.py
+++ b/solution.py
@@ -29,7 +29,7 @@
 GROUP_ROWS = ROWS // GROUPS
 HALF = GROUP_ROWS // 2
 LATE_ROWS = 4
-TOGETHER = 8
+TOGETHER = 6
 SPANS = (256, 512, 1024, 2048)
 
 
@@ -189,7 +189,7 @@
 
 def attend_kernel(layer, late_rows, len_hbm, q_ref, new_ref, *refs):
     k_hbm, v_hbm = refs[1:3]
-    k_out, v_out, ctx_ref, kv_buf, len_ref, q_buf, new_buf, sems = refs[-8:]
+    k_out, v_out, ctx_ref, kv_buf, len_ref, long_ref, q_buf, new_buf, sems = refs[-9:]
     k_buf, v_buf = kv_buf.at[0], kv_buf.at[1]
     me = lax.axis_index("model")
     out_sems, len_sem, late_sem = (sems.at[0], sems.at[1]), sems.at[2], sems.at[3]
@@ -246,19 +246,35 @@
         for v, b in zip(c, rows):
             ctx_ref[:, b] = v.reshape(DEVICES, MY_HEADS, HEAD_DIM).astype(BF16)
 
-    attend(list(range(TOGETHER)), SPANS[0])
+    def attend_all(first, last):
+        for at in range(first, last, TOGETHER):
+            attend(list(range(at, min(at + TOGETHER, last))), SPANS[0])
+
+        def note_long(b, count):
+            is_long = len_ref[me * MY_ROWS + b] >= SPANS[0]
+
+            @pl.when(is_long)
+            def _():
+                long_ref[count] = b
+
+            return count + is_long.astype(jnp.int32)
+
+        count = lax.fori_loop(first, last, note_long, jnp.int32(0))
+
+        @pl.loop(0, (count + 1) // 2)
+        def _(i):
+            pair = [long_ref[2 * i], long_ref[jnp.minimum(2 * i + 1, count - 1)]]
+            longest = jnp.maximum(*[len_ref[me * MY_ROWS + b] for b in pair])
+            for low, n in zip(SPANS, SPANS[1:]):
+                @pl.when(jnp.logical_and(longest >= low, longest < n))
+                def _(n=n):
+                    attend(pair, n)
+
+    attend_all(0, MY_ROWS - late_rows)
     if late_rows:
         await_all(kv_buf.at[:, late], late_sem)
         write_tokens(MY_ROWS - late_rows, MY_ROWS)
-    attend(list(range(TOGETHER, MY_ROWS)), SPANS[0])
-
-    @pl.loop(0, MY_ROWS)
-    def _(b):
-        pos = len_ref[me * MY_ROWS + b]
-        for low, n in zip(SPANS, SPANS[1:]):
-            @pl.when(jnp.logical_and(pos >= low, pos < n))
-            def _(n=n):
-                attend([b], n)
+        attend_all(MY_ROWS - late_rows, MY_ROWS)
 
     for which, hbm in enumerate((k_out, v_out)):
         await_all(hbm.at[layer], out_sems[which])
@@ -276,17 +292,18 @@
             pltpu.VMEM((DEVICES, MY_ROWS, MY_HEADS, HEAD_DIM), BF16),
             pltpu.VMEM(kv_pre.shape, BF16),
         ),
-        in_specs=[any_spec] + [vmem_spec] * 3 + [any_spec] * (2 + len(prev)),
+        in_specs=[vmem_spec] * 4 + [any_spec] * (2 + len(prev)),
         out_specs=(any_spec, any_spec, vmem_spec, vmem_spec),
         scratch_shapes=[
             pltpu.SMEM((ROWS,), jnp.int32),
+            pltpu.SMEM((MY_ROWS,), jnp.int32),
             pltpu.VMEM((MY_ROWS, NUM_HEADS, HEAD_DIM), F32),
             pltpu.VMEM((2, MY_ROWS, HEAD_DIM), F32),
             pltpu.SemaphoreType.DMA((4,)),
         ],
         input_output_aliases={3: 3} | ({6: 0, 7: 1} if prev else {}),
         compiler_params=pltpu.CompilerParams(vmem_limit_bytes=16 * MIB),
-    )(*in_hbm(cache_len), *in_vmem(q, kv_new, kv_pre), *in_hbm(k_cache, v_cache), *prev)
+    )(*in_vmem(cache_len, q, kv_new, kv_pre), *in_hbm(k_cache, v_cache), *prev)
     return ctx, k_all, v_all
 
 

time: 104 us -> 104 us (level)
  no operation moved by 1% of the time
where the time goes in v6:
time: 104 us
  Pallas kernels  102 us (98%)
  local copies, waits for them, and re-layouts  1.33 us (1%)
    pallas_call x2, Pallas kernels, combine_call(): pl.pallas_call(functools.partial(combine_kernel, layer, last), name='comb...  75.9 us
    pallas_call x1, Pallas kernels, query_call(): pl.pallas_call(query_kernel, name='query', out_shape=QUERY_SHAPES, in_spe...  13.1 us
    pallas_call x2, Pallas kernels, attend_call(): pl.pallas_call(functools.partial(attend_kernel, layer, late_rows), name='...  13 us

profile of v6, /device:TPU:0, one launch (start us, length us, event | category | flops | bytes accessed | tf_op | source)
XLA Modules:
  0.0 104.0 jit_solution(11872333724896877723)
XLA Ops:
  0.6 0.0 copy-start
  0.6 13.1 %query.1 = (bf16[8,16,1024]{2,1,0:T(8,128)(2,1)S(1)}, bf16[2,16,128]{2,1,0:T(8,128)(2,1)S(1)}, bf16[2,16,2048,128]{3,2,1,0:T(8,128)(2,1)S(1)}) custom-call(bf16[128,8192]{1,0:T(8,128)(2,1)} %x_hbm.1, bf16[2,8192,1024]{2,1,0:T(8,128)(2,1)} %refs_3_.1, bf16[2,8192,128]{2,1,0:T(8,128)(2,1)} %refs_4_.1, bf16[2,8192,128]{2,1,0:T(8,128)(2,1)} %refs_5_.1, ...), custom_call_target="tpu_custom_call" | custom-call | tf_op jit(solution)/shard_map/query/pallas_call | solution.py:168
  13.7 0.0 copy-done
  13.7 6.6 %attend.2 = (bf16[2,16,2048,128]{3,2,1,0:T(8,128)(2,1)}, bf16[2,16,2048,128]{3,2,1,0:T(8,128)(2,1)}, bf16[8,16,8,128]{3,2,1,0:T(8,128)(2,1)S(1)}, bf16[2,16,2048,128]{3,2,1,0:T(8,128)(2,1)S(1)}) custom-call(s32[128]{0:T(128)S(1)} %copy-done, bf16[8,16,1024]{2,1,0:T(8,128)(2,1)S(1)} %get-tuple-element.16.q_ref, ...), custom_call_target="tpu_custom_call", output_to_operand_aliasing={{3}: (3, {})} | custom-call | tf_op jit(solution)/shard_map/attend/pallas_call | solution.py:286
  20.3 40.5 %combine.1 = (bf16[2,64,1024]{2,1,0:T(8,128)(2,1)S(1)}, bf16[8,16,1024]{2,1,0:T(8,128)(2,1)S(1)}, bf16[2,16,128]{2,1,0:T(8,128)(2,1)S(1)}, bf16[2,16,2048,128]{3,2,1,0:T(8,128)(2,1)S(1)}) custom-call(bf16[8,16,8,128]{3,2,1,0:T(8,128)(2,1)S(1)} %get-tuple-element.19.refs_0_, bf16[8,2,8,8192]{3,2,1,0:T(8,128)(2,1)} %bitcast.3, bf16[2,1024,8192]{2,1,0:T(8,128)(2,1)} %refs_2_.7, ...), custom_call_target="tpu_custom_call" | custom-call | tf_op jit(solution)/shard_map/combine/pallas_call | solution.py:557
  60.8 6.4 %attend.3 = (bf16[2,16,2048,128]{3,2,1,0:T(8,128)(2,1)}, bf16[2,16,2048,128]{3,2,1,0:T(8,128)(2,1)}, bf16[8,16,8,128]{3,2,1,0:T(8,128)(2,1)S(1)}, bf16[2,16,2048,128]{3,2,1,0:T(8,128)(2,1)S(1)}) custom-call(s32[128]{0:T(128)S(1)} %copy-done, ...), custom_call_target="tpu_custom_call", output_to_operand_aliasing={{3}: (3, {}), {0}: (6, {}), {1}: (7, {})} | custom-call | tf_op jit(solution)/shard_map/attend/pallas_call | solution.py:286
  67.2 35.4 %combine_last.1 = bf16[8,2,8,8192]{3,2,1,0:T(8,128)(2,1)S(1)} custom-call(bf16[8,16,8,128]{3,2,1,0:T(8,128)(2,1)S(1)} %get-tuple-element.25.refs_0_, bf16[2,64,1024]{2,1,0:T(8,128)(2,1)S(1)} %get-tuple-element.26.refs_1_, bf16[2,1024,8192]{2,1,0:T(8,128)(2,1)} %refs_2_.7), custom_call_target="tpu_custom_call" | custom-call | tf_op jit(solution)/shard_map/combine_last/pallas_call | solution.py:557
  102.6 1.3 %copy.20 = bf16[128,8192]{1,0:T(8,128)(2,1)} copy(bf16[128,8192]{1,0:T(8,128)(2,1)S(1)} %bitcast.2) | data formatting | bytes 4194304
Async XLA Ops:
  0.6 13.1 %copy-start = (s32[128]{0:T(128)S(1)}, s32[128]{0:T(128)}, u32[]{:S(2)}) copy-start(s32[128]{0:T(128)} %len_hbm.3) | copy-start | bytes 1540

commit v7 on v6

--- a/solution.py
+++ b/solution.py
@@ -29,6 +29,7 @@
 GROUP_ROWS = ROWS // GROUPS
 HALF = GROUP_ROWS // 2
 LATE_ROWS = 4
+READY_ROWS = 2
 TOGETHER = 6
 SPANS = (256, 512, 1024, 2048)
 
@@ -187,7 +188,7 @@
     )(*in_hbm(x, w_query, w_key, w_value, k_cache, v_cache))
 
 
-def attend_kernel(layer, late_rows, len_hbm, q_ref, new_ref, *refs):
+def attend_kernel(layer, late_rows, ready_rows, len_hbm, q_ref, new_ref, *refs):
     k_hbm, v_hbm = refs[1:3]
     k_out, v_out, ctx_ref, kv_buf, len_ref, long_ref, q_buf, new_buf, sems = refs[-9:]
     k_buf, v_buf = kv_buf.at[0], kv_buf.at[1]
@@ -203,6 +204,10 @@
         hbm, buf = ((k_out, k_buf), (v_out, v_buf))[which]
         return pltpu.make_async_copy(buf.at[b], hbm.at[layer, b], out_sems[which])
 
+    for b in range(ready_rows):
+        save(0, b).start()
+        save(1, b).start()
+
     new_buf[...] = new_ref[...].astype(F32)
     for src in range(DEVICES):
         block = q_ref[src].astype(F32)
@@ -229,7 +234,7 @@
         save(1, last - 1).start()
 
     len_load.wait()
-    write_tokens(0, MY_ROWS - late_rows)
+    write_tokens(ready_rows, MY_ROWS - late_rows)
 
     scale = HEAD_DIM ** -0.5
 
@@ -280,11 +285,11 @@
         await_all(hbm.at[layer], out_sems[which])
 
 
-def attend_call(layer, late_rows, cache_len, q, kv_new, kv_pre, k_cache, v_cache, prev):
+def attend_call(layer, late_rows, ready_rows, cache_len, q, kv_new, kv_pre, k_cache, v_cache, prev):
     any_spec = pl.BlockSpec(memory_space=pl.ANY)
     vmem_spec = pl.BlockSpec(memory_space=pltpu.VMEM)
     k_all, v_all, ctx, _ = pl.pallas_call(
-        functools.partial(attend_kernel, layer, late_rows),
+        functools.partial(attend_kernel, layer, late_rows, ready_rows),
         name="attend",
         out_shape=(
             jax.ShapeDtypeStruct(k_cache.shape, BF16),
@@ -309,19 +314,19 @@
 
 SELF, XN, YN, DIAG = range(4)
 PASS_ON_AFTER = XN
-LEFT, RIGHT = pl.ds(0, MY_COLS // 2), pl.ds(MY_COLS // 2, MY_COLS // 2)
+LEFT, RIGHT, WHOLE_WIDTH = pl.ds(0, MY_COLS // 2), pl.ds(MY_COLS // 2, MY_COLS // 2), pl.ds(0, MY_COLS)
 CONTEXT, CORE, SUMS, WHOLE, HALVES, QUERY, NEW_ROWS = range(7)
 
 
 def combine_kernel(layer, last, *refs):
     if last:
         (ctx_in, res_buf, wo_hbm, out_ref,
-         ctx_buf, lhs, w_buf, send_d2d, recv_d2d, acc, rx_diag, ry_diag, top_in, bottom_in, h_buf,
+         ctx_buf, lhs, w_buf, send_d2d, recv_d2d, acc, diag_in, top_in, bottom_in, h_buf,
          load_sems, send_sems, recv_sems) = refs
     else:
-        (ctx_in, res_hbm, wo_hbm, wq_hbm, wk_hbm, wv_hbm, k_hbm, v_hbm, own_out, q_out, kv_out, kv_pre,
-         ctx_buf, lhs, res_buf, w_buf, send_d2d, recv_d2d, acc, rx_diag, ry_diag, top_in, bottom_in, h_buf,
-         wkv_buf, q_acc, q_send, kv_send,
+        (ctx_in, res_hbm, wo_hbm, wq_hbm, wk_hbm, wv_hbm, k_hbm, v_hbm, len_hbm, own_out, q_out, kv_out, kv_pre,
+         ctx_buf, lhs, res_buf, w_buf, send_d2d, recv_d2d, acc, diag_in, top_in, bottom_in, h_buf,
+         wkv_buf, q_acc, q_send, kv_send, len_ref,
          load_sems, send_sems, recv_sems) = refs
     me, flip, xn, yn, diag = places()
     partner, core = me + flip, lax.rem(me, 2)
@@ -337,10 +342,12 @@
     for slot, (r, c) in enumerate(wo_order):
         pltpu.make_async_copy(wo_hbm.at[layer, :, columns(r, c)], w_buf.at[slot], load_sems.at[slot // 2]).start()
     if not last:
-        wq_sem, res_sem, wkv_sem, cache_sem = [load_sems.at[4 + i] for i in range(4)]
+        wq_sem, res_sem, wkv_sem, cache_sem, len_sem = [load_sems.at[4 + i] for i in range(5)]
         res_load = pltpu.make_async_copy(res_hbm.at[:, :, :, columns(SELF, 0)], res_buf, res_sem)
         res_load.start()
         load_kv_weights(layer + 1, core, wk_hbm, wv_hbm, wkv_buf, wkv_sem)
+        len_load = pltpu.make_async_copy(len_hbm, len_ref, len_sem)
+        len_load.start()
 
     meet_all(me)
 
@@ -362,23 +369,35 @@
         rows = ctx_buf[g].astype(F32).reshape(GROUP_ROWS, MY_HEADS, HEAD_DIM)
         lhs[g] = rows.reshape(GROUP_ROWS, MY_COLS).astype(BF16)
 
+    def add_partner(g, r, cols):
+        await_all(recv_d2d.at[g, r, :, cols], d2d[g, r, cols.start])
+        acc[g, r, :, cols] += recv_d2d[g, r, :, cols]
+
+    def start_diagonal(g, cols):
+        if g not in first:
+            first[g] = copies.new_receive()
+        add_partner(g, DIAG, cols)
+        copies.start(acc.at[g, DIAG, top, cols], diag_in.at[g, 0, :, cols], xn, SUMS, first[g])
+        copies.start(acc.at[g, DIAG, bottom, cols], diag_in.at[g, 1, :, cols], yn, SUMS, first[g])
+
     def settle(g, r):
-        await_all(recv_d2d.at[g, r], d2d[g, r])
-        acc[g, r] += recv_d2d[g, r]
         if r == DIAG:
-            first[g, 0] = copies.start(acc.at[g, r, top], rx_diag.at[g], xn, SUMS)
-            first[g, 1] = copies.start(acc.at[g, r, bottom], ry_diag.at[g], yn, SUMS)
+            start_diagonal(g, pieces_of(g, r)[-1])
+            return
+        add_partner(g, r, WHOLE_WIDTH)
         if r == YN:
             in_sems[g] = copies.new_receive(), copies.new_receive()
             copies.start(acc.at[g, XN, top], top_in.at[g, 0], xn, SUMS, in_sems[g][0])
             copies.start(acc.at[g, YN, bottom], bottom_in.at[g, 0], yn, SUMS, in_sems[g][1])
 
+    def pieces_of(g, r):
+        return (LEFT, RIGHT) if (g, r) == (0, DIAG) else (WHOLE_WIDTH,)
+
     def pass_on(g):
-        first[g, 0].wait_recv()
-        acc[g, YN, top] += rx_diag[g]
+        await_all(diag_in.at[g], first[g])
+        acc[g, YN, top] += diag_in[g, 0]
         copies.start(acc.at[g, YN, top], top_in.at[g, 1], yn, SUMS, in_sems[g][0])
-        first[g, 1].wait_recv()
-        acc[g, XN, bottom] += ry_diag[g]
+        acc[g, XN, bottom] += diag_in[g, 1]
         copies.start(acc.at[g, XN, bottom], bottom_in.at[g, 1], xn, SUMS, in_sems[g][1])
 
     pending = None
@@ -388,12 +407,14 @@
             if g == 0 and c == 1:
                 await_all(w_buf.at[pl.ds(slot, 2)], load_sems.at[slot // 2])
             if c == 1:
-                d2d[g, r] = copies.new_receive()
-                for cols in (LEFT, RIGHT) if r == DIAG else (pl.ds(0, MY_COLS),):
+                for cols in pieces_of(g, r):
+                    d2d[g, r, cols.start] = copies.new_receive()
                     send_d2d[g, r, :, cols] = dot(lhs[g], w_buf[slot, :, cols])
-                    copies.start(send_d2d.at[g, r, :, cols], recv_d2d.at[g, r, :, cols], partner, CORE, d2d[g, r])
+                    copies.start(send_d2d.at[g, r, :, cols], recv_d2d.at[g, r, :, cols], partner, CORE, d2d[g, r, cols.start])
             else:
                 acc[g, r] = dot(lhs[g], w_buf[slot])
+                if len(pieces_of(g, r)) > 1:
+                    start_diagonal(g, LEFT)
             if not last and g == GROUPS - 1:
                 pltpu.make_async_copy(wq_hbm.at[layer + 1, columns(*wq_order[slot]), :], w_buf.at[slot], wq_sem).start()
             if c == 1 and pending is not None:
@@ -406,7 +427,7 @@
         load_cache(layer + 1, pl.ds(0, MY_ROWS), k_hbm, v_hbm, kv_pre, cache_sem)
     pass_on(GROUPS - 1)
 
-    gather, diag_sems = {}, {}
+    gather, diag_sems, relay_sems = {}, {}, {}
     if not last:
         res_load.wait()
 
@@ -450,9 +471,10 @@
             copies.start(h_buf.at[r, 0, g, half], h_buf.at[DIAG, 0, g, half], device, HALVES, diag_sems[g])
 
     def relay_second(g):
+        relay_sems[g] = copies.new_receive()
         for r in (XN, YN):
             gather[r, 0, g][1].wait_recv()
-            gather[r, 1, g] = copies.start(h_buf.at[r, 0, g], h_buf.at[r, 1, g], partner, WHOLE)
+            copies.start(h_buf.at[r, 0, g], h_buf.at[r, 1, g], partner, WHOLE, relay_sems[g])
 
     def relay_diag(g):
         await_all(h_buf.at[DIAG, 0, g], diag_sems[g])
@@ -476,15 +498,13 @@
     relay_second(0)
     use(0, (XN, 0), (YN, 0))
     relay_first(1)
-    arrive(XN, 1, 0)
-    arrive(YN, 1, 0)
+    await_all(h_buf.at[pl.ds(XN, 2), 1, 0], relay_sems[0])
     use(0, (XN, 1), (YN, 1))
     relay_second(1)
     use(1, (XN, 0), (YN, 0))
     relay_diag(0)
     use(0, (DIAG, 0))
-    arrive(XN, 1, 1)
-    arrive(YN, 1, 1)
+    await_all(h_buf.at[pl.ds(XN, 2), 1, 1], relay_sems[1])
     use(1, (XN, 1), (YN, 1))
     relay_diag(1)
     arrive(DIAG, 1, 0)
@@ -508,10 +528,16 @@
         made = made.reshape(GROUPS, 2, GROUP_SEQS, HEAD_DIM)
         made = jnp.concatenate([made[g, k] for k in range(2) for g in range(GROUPS)], axis=0)
         shared = share_new_rows(copies, core, partner, made, kv_send, kv_out, NEW_ROWS)
+        len_load.wait()
+        await_all(kv_pre, cache_sem)
+        shared.wait()
+        for b in range(READY_ROWS):
+            here = lax.broadcasted_iota(jnp.int32, (SEQ, HEAD_DIM), 0) == len_ref[me * MY_ROWS + b]
+            for i in range(2):
+                row = jnp.broadcast_to(kv_out[i, b:b + 1, :].astype(F32), (SEQ, HEAD_DIM))
+                kv_pre[i, b] = jnp.where(here, row, kv_pre[i, b].astype(F32)).astype(BF16)
         await_all(q_out.at[seven], q_sem)
-        shared.wait()
         await_all(q_send.at[:, seven], send_sems.at[QUERY])
-        await_all(kv_pre, cache_sem)
     await_all(ctx_in.at[seven], send_sems.at[CONTEXT])
     await_all(send_d2d, send_sems.at[CORE])
     await_all(acc.at[:, pl.ds(0, 3)], send_sems.at[SUMS])
@@ -522,7 +548,7 @@
 def combine_call(layer, last, ctx, residual, w_out, more):
     any_spec = pl.BlockSpec(memory_space=pl.ANY)
     vmem_spec = pl.BlockSpec(memory_space=pltpu.VMEM)
-    receives = (2 if last else 4) + GROUPS * (4 + 4 + 9)
+    receives = (2 if last else 4) + 1 + GROUPS * (4 + 3 + 8)
     scratch = [
         pltpu.VMEM((GROUPS, DEVICES, GROUP_SEQS, MY_HEADS, HEAD_DIM), BF16),
         pltpu.VMEM((GROUPS, GROUP_ROWS, MY_COLS), BF16),
@@ -530,8 +556,7 @@
         pltpu.VMEM((GROUPS, 4, GROUP_ROWS, MY_COLS), F32),
         pltpu.VMEM((GROUPS, 4, GROUP_ROWS, MY_COLS), F32),
         pltpu.VMEM((GROUPS, 4, GROUP_ROWS, MY_COLS), F32),
-        pltpu.VMEM((GROUPS, HALF, MY_COLS), F32),
-        pltpu.VMEM((GROUPS, HALF, MY_COLS), F32),
+        pltpu.VMEM((GROUPS, 2, HALF, MY_COLS), F32),
         pltpu.VMEM((GROUPS, 2, HALF, MY_COLS), F32),
         pltpu.VMEM((GROUPS, 2, HALF, MY_COLS), F32),
         pltpu.VMEM((4, 2, GROUPS, GROUP_ROWS, MY_COLS), BF16),
@@ -548,9 +573,10 @@
             pltpu.VMEM((GROUPS, GROUP_ROWS, MY_COLS), F32),
             pltpu.VMEM((GROUPS, DEVICES, GROUP_SEQS, MY_COLS), BF16),
             pltpu.VMEM((2, MY_ROWS, HEAD_DIM), BF16),
+            pltpu.SMEM((ROWS,), jnp.int32),
         ]
     scratch += [
-        pltpu.SemaphoreType.DMA((4 if last else 8,)),
+        pltpu.SemaphoreType.DMA((4 if last else 9,)),
         pltpu.SemaphoreType.DMA((5 if last else 7,)),
         pltpu.SemaphoreType.DMA((receives,)),
     ]
@@ -573,9 +599,9 @@
     def device_step(x, cache_len, w_query, w_key, w_value, w_out, k_cache, v_cache):
         caches = (k_cache, v_cache)
         q, kv_new, kv_pre = query_call(x, w_query, w_key, w_value, *caches)
-        ctx, k_all, v_all = attend_call(0, LATE_ROWS, cache_len, q, kv_new, kv_pre, *caches, ())
-        own, q, kv_new, kv_pre = combine_call(0, False, ctx, x.reshape(DEVICES, GROUPS, GROUP_SEQS, D_MODEL), w_out, (w_query, w_key, w_value, *caches))
-        ctx, k_all, v_all = attend_call(1, 0, cache_len, q, kv_new, kv_pre, *caches, (k_all, v_all))
+        ctx, k_all, v_all = attend_call(0, LATE_ROWS, 0, cache_len, q, kv_new, kv_pre, *caches, ())
+        own, q, kv_new, kv_pre = combine_call(0, False, ctx, x.reshape(DEVICES, GROUPS, GROUP_SEQS, D_MODEL), w_out, (w_query, w_key, w_value, *caches, cache_len))
+        ctx, k_all, v_all = attend_call(1, 0, READY_ROWS, cache_len, q, kv_new, kv_pre, *caches, (k_all, v_all))
         out = combine_call(1, True, ctx, own, w_out, ())
         return out.reshape(x.shape), k_all, v_all
 

time: 104 us -> 103 us (level)
  no operation moved by 1% of the time
where the time goes in v7:
time: 103 us
  Pallas kernels  101 us (98%)
  local copies, waits for them, and re-layouts  1.33 us (1%)
    pallas_call x2, Pallas kernels, combine_call(): pl.pallas_call(functools.partial(combine_kernel, layer, last), name='comb...  75.3 us
    pallas_call x1, Pallas kernels, query_call(): pl.pallas_call(query_kernel, name='query', out_shape=QUERY_SHAPES, in_spe...  13.1 us
    pallas_call x2, Pallas kernels, attend_call(): pl.pallas_call(functools.partial(attend_kernel, layer, late_rows, ready_r...  12.4 us

profile of v7, /device:TPU:0, one launch (start us, length us, event | category | flops | bytes accessed | tf_op | source)
XLA Modules:
  0.0 102.9 jit_solution(17623360641166121802)
XLA Ops:
  0.6 0.0 copy-start
  0.6 13.1 %query.1 = (bf16[8,16,1024]{2,1,0:T(8,128)(2,1)S(1)}, bf16[2,16,128]{2,1,0:T(8,128)(2,1)S(1)}, bf16[2,16,2048,128]{3,2,1,0:T(8,128)(2,1)S(1)}) custom-call(bf16[128,8192]{1,0:T(8,128)(2,1)} %x_hbm.1, bf16[2,8192,1024]{2,1,0:T(8,128)(2,1)} %refs_3_.1, bf16[2,8192,128]{2,1,0:T(8,128)(2,1)} %refs_4_.1, bf16[2,8192,128]{2,1,0:T(8,128)(2,1)} %refs_5_.1, ...), custom_call_target="tpu_custom_call" | custom-call | tf_op jit(solution)/shard_map/query/pallas_call | solution.py:169
  13.7 0.0 copy-done
  13.7 6.6 %attend.2 = (bf16[2,16,2048,128]{3,2,1,0:T(8,128)(2,1)}, bf16[2,16,2048,128]{3,2,1,0:T(8,128)(2,1)}, bf16[8,16,8,128]{3,2,1,0:T(8,128)(2,1)S(1)}, bf16[2,16,2048,128]{3,2,1,0:T(8,128)(2,1)S(1)}) custom-call(s32[128]{0:T(128)S(1)} %copy-done, bf16[8,16,1024]{2,1,0:T(8,128)(2,1)S(1)} %get-tuple-element.16.q_ref, ...), custom_call_target="tpu_custom_call", output_to_operand_aliasing={{3}: (3, {})} | custom-call | tf_op jit(solution)/shard_map/attend/pallas_call | solution.py:291
  20.3 0.0 copy-start.1
  20.4 40.2 %combine.1 = (bf16[2,64,1024]{2,1,0:T(8,128)(2,1)S(1)}, bf16[8,16,1024]{2,1,0:T(8,128)(2,1)S(1)}, bf16[2,16,128]{2,1,0:T(8,128)(2,1)S(1)}, bf16[2,16,2048,128]{3,2,1,0:T(8,128)(2,1)S(1)}) custom-call(bf16[8,16,8,128]{3,2,1,0:T(8,128)(2,1)S(1)} %get-tuple-element.19.refs_0_, bf16[8,2,8,8192]{3,2,1,0:T(8,128)(2,1)} %bitcast.3, bf16[2,1024,8192]{2,1,0:T(8,128)(2,1)} %refs_2_.7, ...), custom_call_target="tpu_custom_call" | custom-call | tf_op jit(solution)/shard_map/combine/pallas_call | solution.py:583
  60.6 0.0 copy-done.1
  60.6 5.8 %attend.3 = (bf16[2,16,2048,128]{3,2,1,0:T(8,128)(2,1)}, bf16[2,16,2048,128]{3,2,1,0:T(8,128)(2,1)}, bf16[8,16,8,128]{3,2,1,0:T(8,128)(2,1)S(1)}, bf16[2,16,2048,128]{3,2,1,0:T(8,128)(2,1)S(1)}) custom-call(s32[128]{0:T(128)S(1)} %copy-done.1, ...), custom_call_target="tpu_custom_call", output_to_operand_aliasing={{3}: (3, {}), {0}: (6, {}), {1}: (7, {})} | custom-call | tf_op jit(solution)/shard_map/attend/pallas_call | solution.py:291
  66.4 35.1 %combine_last.1 = bf16[8,2,8,8192]{3,2,1,0:T(8,128)(2,1)S(1)} custom-call(bf16[8,16,8,128]{3,2,1,0:T(8,128)(2,1)S(1)} %get-tuple-element.25.refs_0_, bf16[2,64,1024]{2,1,0:T(8,128)(2,1)S(1)} %get-tuple-element.26.refs_1_, bf16[2,1024,8192]{2,1,0:T(8,128)(2,1)} %refs_2_.7), custom_call_target="tpu_custom_call" | custom-call | tf_op jit(solution)/shard_map/combine_last/pallas_call | solution.py:583
  101.5 1.3 %copy.20 = bf16[128,8192]{1,0:T(8,128)(2,1)} copy(bf16[128,8192]{1,0:T(8,128)(2,1)S(1)} %bitcast.2) | data formatting | bytes 4194304
Async XLA Ops:
  0.6 13.1 %copy-start = (s32[128]{0:T(128)S(1)}, s32[128]{0:T(128)}, u32[]{:S(2)}) copy-start(s32[128]{0:T(128)} %len_hbm.3) | copy-start | bytes 1540
  20.3 40.2 %copy-start.1 = (s32[128]{0:T(128)S(1)}, s32[128]{0:T(128)}, u32[]{:S(2)}) copy-start(s32[128]{0:T(128)} %len_hbm.3) | copy-start | bytes 1540

commit v8 on v7

--- a/solution.py
+++ b/solution.py
@@ -75,11 +75,13 @@
         return copy
 
 
-def meet_all(me):
-    barrier = pltpu.get_barrier_semaphore()
+def greet_all(me):
     for k in range(1, DEVICES):
-        pl.semaphore_signal(barrier, inc=1, device_id={"model": lax.rem(me + k, DEVICES)}, device_id_type=MESH)
-    pl.semaphore_wait(barrier, DEVICES - 1)
+        pl.semaphore_signal(pltpu.get_barrier_semaphore(), inc=1, device_id={"model": lax.rem(me + k, DEVICES)}, device_id_type=MESH)
+
+
+def await_greetings():
+    pl.semaphore_wait(pltpu.get_barrier_semaphore(), DEVICES - 1)
 
 
 def others():
@@ -139,7 +141,8 @@
     load_kv_weights(0, core, wk_hbm, wv_hbm, wkv_buf, wkv_sem)
     early = pl.ds(0, MY_ROWS - LATE_ROWS)
     load_cache(0, early, k_hbm, v_hbm, kv_pre, cache_sem)
-    meet_all(me)
+    greet_all(me)
+    await_greetings()
     copies = Copies(send_sems, recv_sems)
     q_sem = copies.new_receive()
     x_load.wait()
@@ -330,6 +333,7 @@
          load_sems, send_sems, recv_sems) = refs
     me, flip, xn, yn, diag = places()
     partner, core = me + flip, lax.rem(me, 2)
+    greet_all(me)
     chip_mate = {SELF: me, XN: xn, YN: yn, DIAG: diag}
     columns = lambda r, c: pl.ds(pl.multiple_of((chip_mate[r] + c * flip) * MY_COLS, MY_COLS), MY_COLS)
     copies = Copies(send_sems, recv_sems)
@@ -349,7 +353,7 @@
         len_load = pltpu.make_async_copy(len_hbm, len_ref, len_sem)
         len_load.start()
 
-    meet_all(me)
+    await_greetings()
 
     ctx_sems = [copies.new_receive() for _ in range(GROUPS)]
 

time: 103 us -> 103 us (level)
  no operation moved by 1% of the time
where the time goes in v8:
time: 103 us
  Pallas kernels  101 us (98%)
  local copies, waits for them, and re-layouts  1.33 us (1%)
    pallas_call x2, Pallas kernels, combine_call(): pl.pallas_call(functools.partial(combine_kernel, layer, last), name='comb...  75.3 us
    pallas_call x1, Pallas kernels, query_call(): pl.pallas_call(query_kernel, name='query', out_shape=QUERY_SHAPES, in_spe...  13.1 us
    pallas_call x2, Pallas kernels, attend_call(): pl.pallas_call(functools.partial(attend_kernel, layer, late_rows, ready_r...  12.5 us

profile of v8, /device:TPU:0, one launch (start us, length us, event | category | flops | bytes accessed | tf_op | source)
XLA Modules:
  0.0 102.8 jit_solution(13334487996811316069)
XLA Ops:
  0.6 0.0 copy-start
  0.6 13.1 %query.1 = (bf16[8,16,1024]{2,1,0:T(8,128)(2,1)S(1)}, bf16[2,16,128]{2,1,0:T(8,128)(2,1)S(1)}, bf16[2,16,2048,128]{3,2,1,0:T(8,128)(2,1)S(1)}) custom-call(bf16[128,8192]{1,0:T(8,128)(2,1)} %x_hbm.1, bf16[2,8192,1024]{2,1,0:T(8,128)(2,1)} %refs_3_.1, bf16[2,8192,128]{2,1,0:T(8,128)(2,1)} %refs_4_.1, bf16[2,8192,128]{2,1,0:T(8,128)(2,1)} %refs_5_.1, ...), custom_call_target="tpu_custom_call" | custom-call | tf_op jit(solution)/shard_map/query/pallas_call | solution.py:172
  13.7 0.0 copy-done
  13.7 6.6 %attend.2 = (bf16[2,16,2048,128]{3,2,1,0:T(8,128)(2,1)}, bf16[2,16,2048,128]{3,2,1,0:T(8,128)(2,1)}, bf16[8,16,8,128]{3,2,1,0:T(8,128)(2,1)S(1)}, bf16[2,16,2048,128]{3,2,1,0:T(8,128)(2,1)S(1)}) custom-call(s32[128]{0:T(128)S(1)} %copy-done, bf16[8,16,1024]{2,1,0:T(8,128)(2,1)S(1)} %get-tuple-element.16.q_ref, ...), custom_call_target="tpu_custom_call", output_to_operand_aliasing={{3}: (3, {})} | custom-call | tf_op jit(solution)/shard_map/attend/pallas_call | solution.py:294
  20.3 0.0 copy-start.1
  20.4 40.2 %combine.1 = (bf16[2,64,1024]{2,1,0:T(8,128)(2,1)S(1)}, bf16[8,16,1024]{2,1,0:T(8,128)(2,1)S(1)}, bf16[2,16,128]{2,1,0:T(8,128)(2,1)S(1)}, bf16[2,16,2048,128]{3,2,1,0:T(8,128)(2,1)S(1)}) custom-call(bf16[8,16,8,128]{3,2,1,0:T(8,128)(2,1)S(1)} %get-tuple-element.19.refs_0_, bf16[8,2,8,8192]{3,2,1,0:T(8,128)(2,1)} %bitcast.3, bf16[2,1024,8192]{2,1,0:T(8,128)(2,1)} %refs_2_.7, ...), custom_call_target="tpu_custom_call" | custom-call | tf_op jit(solution)/shard_map/combine/pallas_call | solution.py:587
  60.6 0.0 copy-done.1
  60.6 5.8 %attend.3 = (bf16[2,16,2048,128]{3,2,1,0:T(8,128)(2,1)}, bf16[2,16,2048,128]{3,2,1,0:T(8,128)(2,1)}, bf16[8,16,8,128]{3,2,1,0:T(8,128)(2,1)S(1)}, bf16[2,16,2048,128]{3,2,1,0:T(8,128)(2,1)S(1)}) custom-call(s32[128]{0:T(128)S(1)} %copy-done.1, ...), custom_call_target="tpu_custom_call", output_to_operand_aliasing={{3}: (3, {}), {0}: (6, {}), {1}: (7, {})} | custom-call | tf_op jit(solution)/shard_map/attend/pallas_call | solution.py:294
  66.4 35.1 %combine_last.1 = bf16[8,2,8,8192]{3,2,1,0:T(8,128)(2,1)S(1)} custom-call(bf16[8,16,8,128]{3,2,1,0:T(8,128)(2,1)S(1)} %get-tuple-element.25.refs_0_, bf16[2,64,1024]{2,1,0:T(8,128)(2,1)S(1)} %get-tuple-element.26.refs_1_, bf16[2,1024,8192]{2,1,0:T(8,128)(2,1)} %refs_2_.7), custom_call_target="tpu_custom_call" | custom-call | tf_op jit(solution)/shard_map/combine_last/pallas_call | solution.py:587
  101.5 1.3 %copy.20 = bf16[128,8192]{1,0:T(8,128)(2,1)} copy(bf16[128,8192]{1,0:T(8,128)(2,1)S(1)} %bitcast.2) | data formatting | bytes 4194304
Async XLA Ops:
  0.6 13.1 %copy-start = (s32[128]{0:T(128)S(1)}, s32[128]{0:T(128)}, u32[]{:S(2)}) copy-start(s32[128]{0:T(128)} %len_hbm.3) | copy-start | bytes 1540
  20.3 40.2 %copy-start.1 = (s32[128]{0:T(128)S(1)}, s32[128]{0:T(128)}, u32[]{:S(2)}) copy-start(s32[128]{0:T(128)} %len_hbm.3) | copy-start | bytes 1540
